TPU v7x, 256 devices: a whole 4x4x8 slice. The times are simulated.
256 devices in a mesh: dp: 256 (over y, x, z, core).
Axes of the slice: x: 4, y: 4, z: 8, core: 2. Of those that a mesh axis runs over, the one named last changes fastest.
Arguments:
- grads: bfloat16 [256, 4096, 128], P('dp'), may hold values from -3200 to 3200
- master: float32 [4096, 128], P('dp'), may hold values from -6 to 6
- first_q: bfloat16 [4096, 128], P('dp'), may hold values from -1 to 1
- first_scale: float32 [4096], P('dp'), may hold values from 0.005 to 0.05
- second_q: bfloat16 [4096, 128], P('dp'), may hold values from 0.099609375 to 1
- second_scale: float32 [4096], P('dp'), may hold values from 2e-05 to 0.0002
Outputs:
- weights: bfloat16 [4096, 128], replicated
- master_new: float32 [4096, 128], P('dp')
- first_q_new: bfloat16 [4096, 128], P('dp')
- first_scale_new: float32 [4096], P('dp')
- second_q_new: bfloat16 [4096, 128], P('dp')
- second_scale_new: float32 [4096], P('dp')
All inputs are finite; a program needn't handle non-finite values. Where the computation divides by a largest or mean magnitude, that divisor is 1e-20 or more.
Results may differ from a plain program's by a relative error of at most 0.001.
Values may be sent and summed in bfloat16 or wider, within the bound.
No kernel may reach another device: no remote copies, remote signals or barrier semaphores. Data moves between devices by JAX's collectives and lax.ppermute only.
A program may use at most 64 MiB of HBM per device.

v0:
```python
import jax
import jax.numpy as jnp
from jax import lax
from jax.sharding import Mesh
from jax.sharding import PartitionSpec as P

DP = ("dp_0", "dp_1", "dp_2", "dp_3")


beta_one = 0.9
beta_two = 0.95
learn_rate = 0.05
decay_rate = 0.1
adam_epsilon = 1e-08
clip_rms = 0.01
first_fix = 1.0 - 0.9**10
second_fix = 1.0 - 0.95**10


def from_partner(block, axis, stride):
    count = lax.axis_size(axis)
    route = []
    for low in range(count):
        high = low | 1 << stride
        if high != low and high < count:
            route += [(low, high), (high, low)]
    return lax.ppermute(block, axis, route)


def sent_to_all(x, axis):
    copies = jnp.broadcast_to(x, (lax.axis_size(axis), *x.shape))
    return lax.all_to_all(copies, axis, split_axis=0, concat_axis=0, tiled=True)


def taken_together(x, axis):
    return sent_to_all(x, axis).sum(axis=0)


def one_axis_at_a_time(x, axes):
    far, near = axes
    return taken_together(taken_together(x, near), far)


def joined_along(pieces, dim):
    lengths = list(pieces.shape[1:])
    lengths[dim] *= pieces.shape[0]
    return jnp.moveaxis(pieces, 0, dim).reshape(lengths)


def gather_axes(x, axes, dim):
    far, near = axes
    pieces = sent_to_all(sent_to_all(x, far), near)
    return joined_along(pieces.swapaxes(0, 1).reshape(-1, *x.shape), dim)


def advance(clipped, master, first_q, first_scale, second_q, second_scale):
    first = first_q.astype(jnp.float32) * first_scale[:, None]
    second = second_q.astype(jnp.float32) * second_scale[:, None]
    first_new = beta_one * first + (1.0 - beta_one) * clipped
    second_new = beta_two * second + (1.0 - beta_two) * clipped * clipped
    change = first_new / first_fix / (jnp.sqrt(second_new / second_fix) + adam_epsilon)
    master_new = master * (1.0 - learn_rate * decay_rate) - learn_rate * change
    first_scale_new = jnp.max(jnp.abs(first_new), axis=1) + 1e-08
    second_scale_new = jnp.max(jnp.abs(second_new), axis=1) + 1e-08
    first_q_new = (first_new / first_scale_new[:, None]).astype(jnp.bfloat16)
    second_q_new = (second_new / second_scale_new[:, None]).astype(jnp.bfloat16)
    return (master_new, first_q_new, first_scale_new, second_q_new, second_scale_new)


def split_half(current, index, bit):
    half = current.shape[0] // 2
    upper = index >> bit & 1
    keeping = lax.dynamic_slice_in_dim(current, upper * half, half, 0)
    sending = lax.dynamic_slice_in_dim(current, (1 - upper) * half, half, 0)
    return (keeping, sending)


def shards(grads, master, first_q, first_scale, second_q, second_scale):
    local = grads[0]
    index = lax.axis_index(DP)
    levels = lax.axis_size(DP).bit_length() - 1
    keeping, sending = split_half(local, index, levels - 1)
    arrived = from_partner(sending, DP, levels - 1)
    total = keeping.astype(jnp.float32) + arrived.astype(jnp.float32)
    for level in range(levels - 2, -1, -1):
        keeping, sending = split_half(total, index, level)
        arrived = from_partner(sending, DP, level)
        total = keeping + arrived
    squares = one_axis_at_a_time(jnp.sum(total * total), ("dp_0", ("dp_1", "dp_2", "dp_3")))
    limit = clip_rms * jnp.sqrt(jnp.float32(local.shape[0] * local.shape[1]))
    factor = jnp.minimum(1.0, limit / (jnp.sqrt(squares) + 1e-06))
    clipped = factor * total
    master_new, first_q_new, first_scale_new, second_q_new, second_scale_new = advance(
        clipped, master, first_q, first_scale, second_q, second_scale
    )
    weights = gather_axes(master_new.astype(jnp.bfloat16), ("dp_0", ("dp_1", "dp_2", "dp_3")), 0)
    return (weights, master_new, first_q_new, first_scale_new, second_q_new, second_scale_new)


def solution(mesh):
    torus = Mesh(mesh.devices.reshape(4, 4, 8, 2), ("dp_0", "dp_1", "dp_2", "dp_3"))
    in_specs = (P(DP, None, None), P(DP, None), P(DP, None), P(DP), P(DP, None), P(DP))
    out_specs = (P(), P(DP, None), P(DP, None), P(DP), P(DP, None), P(DP))
    return jax.shard_map(
        shards, mesh=torus, in_specs=in_specs, out_specs=out_specs, check_vma=False
    )
```

profile of v0, /device:TPU:1, one launch (start us, length us, event | category | flops | bytes accessed | tf_op | source)
XLA Modules:
  0.0 143.0 jit_solution(7684715481834606550)
XLA Ops:
  0.6 0.0 copy-start
  0.7 1.2 dynamic-slice_bitcast_fusion
  1.8 3.8 %collective-permute-start = (bf16[2048,128]{1,0:T(8,128)(2,1)S(1)}, bf16[2048,128]{1,0:T(8,128)(2,1)S(1)}, u32[]{:S(2)}, u32[]{:S(2)}) collective-permute-start(bf16[2048,128]{1,0:T(8,128)(2,1)S(1)} %dynamic-slice_bitcast_fusion), channel_id=1, source_target_pairs={{0,128},{128,0},{1,129},{129,1},{2,130},{130,2},{3,131},{131,3},{4... | collective-permute-start | bytes 1572872 | tf_op jit(solution)/shard_map/ppermute | solution.py:27
  5.6 10.6 %collective-permute-done = bf16[2048,128]{1,0:T(8,128)(2,1)S(1)} collective-permute-done((bf16[2048,128]{1,0:T(8,128)(2,1)S(1)}, bf16[2048,128]{1,0:T(8,128)(2,1)S(1)}, u32[]{:S(2)}, u32[]{:S(2)}) %collective-permute-start) | collective-permute-done | bytes 524320 | tf_op jit(solution)/shard_map/ppermute | solution.py:27
  16.2 0.0 copy-done
  16.3 0.1 convert_add_fusion
  16.4 2.2 %collective-permute-start.1 = (f32[1024,128]{1,0:T(8,128)S(1)}, f32[1024,128]{1,0:T(8,128)S(1)}, u32[]{:S(2)}, u32[]{:S(2)}) collective-permute-start(f32[1024,128]{1,0:T(8,128)S(1)} %constant_dynamic-slice_fusion.6), channel_id=1, source_target_pairs={{0,64},{64,0},{1,65},{65,1},{2,66},{66,2},{3,67},{67,3},{4,68},{68... | collective-permute-start | bytes 1572872 | tf_op jit(solution)/shard_map/ppermute | solution.py:27
  18.6 10.4 %collective-permute-done.1 = f32[1024,128]{1,0:T(8,128)S(1)} collective-permute-done((f32[1024,128]{1,0:T(8,128)S(1)}, f32[1024,128]{1,0:T(8,128)S(1)}, u32[]{:S(2)}, u32[]{:S(2)}) %collective-permute-start.1) | collective-permute-done | bytes 524320 | tf_op jit(solution)/shard_map/ppermute | solution.py:27
  29.0 0.1 dynamic-slice_add_fusion
  29.1 3.1 %collective-permute-start.2 = (f32[512,128]{1,0:T(8,128)S(1)}, f32[512,128]{1,0:T(8,128)S(1)}, u32[]{:S(2)}, u32[]{:S(2)}) collective-permute-start(f32[512,128]{1,0:T(8,128)S(1)} %constant_dynamic-slice_fusion.5), channel_id=1, source_target_pairs={{0,32},{32,0},{1,33},{33,1},{2,34},{34,2},{3,35},{35,3},{4,36},{36... | collective-permute-start | bytes 786440 | tf_op jit(solution)/shard_map/ppermute | solution.py:27
  32.2 3.8 %collective-permute-done.2 = f32[512,128]{1,0:T(8,128)S(1)} collective-permute-done((f32[512,128]{1,0:T(8,128)S(1)}, f32[512,128]{1,0:T(8,128)S(1)}, u32[]{:S(2)}, u32[]{:S(2)}) %collective-permute-start.2) | collective-permute-done | bytes 262176 | tf_op jit(solution)/shard_map/ppermute | solution.py:27
  36.0 1.5 %collective-permute-start.3 = (f32[256,128]{1,0:T(8,128)S(1)}, f32[256,128]{1,0:T(8,128)S(1)}, u32[]{:S(2)}, u32[]{:S(2)}) collective-permute-start(f32[256,128]{1,0:T(8,128)S(1)} %constant_dynamic-slice_fusion.4), channel_id=1, source_target_pairs={{0,16},{16,0},{1,17},{17,1},{2,18},{18,2},{3,19},{19,3},{4,20},{20... | collective-permute-start | bytes 393224 | tf_op jit(solution)/shard_map/ppermute | solution.py:27
  37.5 3.0 %collective-permute-done.3 = f32[256,128]{1,0:T(8,128)S(1)} collective-permute-done((f32[256,128]{1,0:T(8,128)S(1)}, f32[256,128]{1,0:T(8,128)S(1)}, u32[]{:S(2)}, u32[]{:S(2)}) %collective-permute-start.3) | collective-permute-done | bytes 131104 | tf_op jit(solution)/shard_map/ppermute | solution.py:27
  40.5 7.0 %collective-permute-start.4 = (f32[128,128]{1,0:T(8,128)S(1)}, f32[128,128]{1,0:T(8,128)S(1)}, u32[]{:S(2)}, u32[]{:S(2)}) collective-permute-start(f32[128,128]{1,0:T(8,128)S(1)} %constant_dynamic-slice_fusion.3), channel_id=1, source_target_pairs={{0,8},{8,0},{1,9},{9,1},{2,10},{10,2},{3,11},{11,3},{4,12},{12,4},... | collective-permute-start | bytes 196616 | tf_op jit(solution)/shard_map/ppermute | solution.py:27
  47.5 1.7 %collective-permute-done.4 = f32[128,128]{1,0:T(8,128)S(1)} collective-permute-done((f32[128,128]{1,0:T(8,128)S(1)}, f32[128,128]{1,0:T(8,128)S(1)}, u32[]{:S(2)}, u32[]{:S(2)}) %collective-permute-start.4) | collective-permute-done | bytes 65568 | tf_op jit(solution)/shard_map/ppermute | solution.py:27
  49.3 1.5 %collective-permute-start.5 = (f32[64,128]{1,0:T(8,128)S(1)}, f32[64,128]{1,0:T(8,128)S(1)}, u32[]{:S(2)}, u32[]{:S(2)}) collective-permute-start(f32[64,128]{1,0:T(8,128)S(1)} %constant_dynamic-slice_fusion.2), channel_id=1, source_target_pairs={{0,4},{4,0},{1,5},{5,1},{2,6},{6,2},{3,7},{7,3},{8,12},{12,8},{9,1... | collective-permute-start | bytes 98312 | tf_op jit(solution)/shard_map/ppermute | solution.py:27
  50.8 2.6 %collective-permute-done.5 = f32[64,128]{1,0:T(8,128)S(1)} collective-permute-done((f32[64,128]{1,0:T(8,128)S(1)}, f32[64,128]{1,0:T(8,128)S(1)}, u32[]{:S(2)}, u32[]{:S(2)}) %collective-permute-start.5) | collective-permute-done | bytes 32800 | tf_op jit(solution)/shard_map/ppermute | solution.py:27
  53.3 0.8 collective-permute-start.6
  54.1 1.9 %collective-permute-done.6 = f32[32,128]{1,0:T(8,128)S(1)} collective-permute-done((f32[32,128]{1,0:T(8,128)S(1)}, f32[32,128]{1,0:T(8,128)S(1)}, u32[]{:S(2)}, u32[]{:S(2)}) %collective-permute-start.6) | collective-permute-done | bytes 16416 | tf_op jit(solution)/shard_map/ppermute | solution.py:27
  56.0 7.9 %collective-permute-start.7 = (f32[16,128]{1,0:T(8,128)S(1)}, f32[16,128]{1,0:T(8,128)S(1)}, u32[]{:S(2)}, u32[]{:S(2)}) collective-permute-start(f32[16,128]{1,0:T(8,128)S(1)} %constant_dynamic-slice_fusion), channel_id=1, source_target_pairs={{0,1},{1,0},{2,3},{3,2},{4,5},{5,4},{6,7},{7,6},{8,9},{9,8},{10,11... | collective-permute-start | bytes 24584 | tf_op jit(solution)/shard_map/ppermute | solution.py:27
  63.9 0.8 collective-permute-done.7
  64.7 0.6 multiply_reduce_fusion
  65.3 0.7 broadcast_in_dim.16
  66.0 0.0 copy-start.4
  66.0 0.0 copy-start.5
  66.0 19.8 %all_to_all.22 = f32[64,1,1]{2,1,0:T(1,128)S(1)} all-to-all(f32[64,1,1]{2,1,0:T(1,128)S(1)} %broadcast_in_dim.16), channel_id=1, replica_groups=mesh['dp_0'=4,'dp_1'=4,'dp_2'=8,'dp_3'=2] {'dp_1','dp_2','dp_3'}, dimensions={0} | all-to-all | bytes 512 | tf_op jit(solution)/shard_map/all_to_all | solution.py:32
  85.9 0.7 reduce_sum.28
  86.5 0.6 broadcast_in_dim.17
  87.2 0.0 copy-start.3
  87.2 8.1 %all_to_all.23 = f32[4,1,1]{2,1,0:T(1,128)S(1)} all-to-all(f32[4,1,1]{2,1,0:T(1,128)S(1)} %broadcast_in_dim.17), channel_id=1, replica_groups=mesh['dp_0'=4,'dp_1'=4,'dp_2'=8,'dp_3'=2] {'dp_0'}, dimensions={0} | all-to-all | bytes 32 | tf_op jit(solution)/shard_map/all_to_all | solution.py:32
  95.3 0.6 reduce_sum.29
  96.6 0.0 copy-start.1
  96.7 0.0 copy-done.4
  96.7 0.0 copy-done.5
  96.7 0.0 copy-done.3
  96.7 0.0 copy-done.2
  96.7 0.6 copy-done.1
  97.3 0.8 abs_reduce_fusion
  98.1 6.6 %all_to_all.24 = bf16[4,16,128]{2,1,0:T(8,128)(2,1)S(1)} all-to-all(bf16[4,16,128]{2,1,0:T(8,128)(2,1)S(1)} %broadcast_in_dim.18), channel_id=1, replica_groups=mesh['dp_0'=4,'dp_1'=4,'dp_2'=8,'dp_3'=2] {'dp_0'}, dimensions={0} | all-to-all | bytes 32768 | tf_op jit(solution)/shard_map/all_to_all | solution.py:32
  104.7 1.2 broadcast_in_dim.19
  105.9 7.3 %all-to-all-start.3 = ((bf16[64,4,16,128]{3,2,1,0:T(8,128)(2,1)}), bf16[64,4,16,128]{3,2,1,0:T(8,128)(2,1)S(1)}, u32[]{:S(2)}, u32[]{:S(2)}) async-start(bf16[64,4,16,128]{3,2,1,0:T(8,128)(2,1)} %broadcast_in_dim.19), calls=%async_computation.3 | async-start | bytes 2097152 | tf_op jit(solution)/shard_map/all_to_all | solution.py:32
  113.3 0.0 copy-start.6
  113.3 0.0 copy-start.7
  113.3 0.5 copy-done.6
  113.8 0.0 copy-done.7
  113.8 0.7 divide_convert_fusion
  114.5 27.3 %all-to-all-done.3 = bf16[64,4,16,128]{3,2,1,0:T(8,128)(2,1)S(1)} async-done(((bf16[64,4,16,128]{3,2,1,0:T(8,128)(2,1)}), bf16[64,4,16,128]{3,2,1,0:T(8,128)(2,1)S(1)}, u32[]{:S(2)}, u32[]{:S(2)}) %all-to-all-start.3) | async-done | bytes 1048608 | tf_op jit(solution)/shard_map/all_to_all | solution.py:32
  141.8 1.1 copy.16
  (15 shorter events, 0.2 us)
Async XLA Ops:
  0.6 15.6 %copy-start = (bf16[1,4096,128]{2,1,0:T(8,128)(2,1)S(1)}, bf16[1,4096,128]{2,1,0:T(8,128)(2,1)}, u32[]{:S(2)}) copy-start(bf16[1,4096,128]{2,1,0:T(8,128)(2,1)} %param.6) | copy-start | bytes 3145732
  1.8 14.4 %collective-permute-start = (bf16[2048,128]{1,0:T(8,128)(2,1)S(1)}, bf16[2048,128]{1,0:T(8,128)(2,1)S(1)}, u32[]{:S(2)}, u32[]{:S(2)}) collective-permute-start(bf16[2048,128]{1,0:T(8,128)(2,1)S(1)} %dynamic-slice_bitcast_fusion), channel_id=1, source_target_pairs={{0,128},{128,0},{1,129},{129,1},{2,130},{130,2},{3,131},{131,3},{4... | collective-permute-start | bytes 1572872 | tf_op jit(solution)/shard_map/ppermute | solution.py:27
  16.4 12.6 %collective-permute-start.1 = (f32[1024,128]{1,0:T(8,128)S(1)}, f32[1024,128]{1,0:T(8,128)S(1)}, u32[]{:S(2)}, u32[]{:S(2)}) collective-permute-start(f32[1024,128]{1,0:T(8,128)S(1)} %constant_dynamic-slice_fusion.6), channel_id=1, source_target_pairs={{0,64},{64,0},{1,65},{65,1},{2,66},{66,2},{3,67},{67,3},{4,68},{68... | collective-permute-start | bytes 1572872 | tf_op jit(solution)/shard_map/ppermute | solution.py:27
  29.1 6.9 %collective-permute-start.2 = (f32[512,128]{1,0:T(8,128)S(1)}, f32[512,128]{1,0:T(8,128)S(1)}, u32[]{:S(2)}, u32[]{:S(2)}) collective-permute-start(f32[512,128]{1,0:T(8,128)S(1)} %constant_dynamic-slice_fusion.5), channel_id=1, source_target_pairs={{0,32},{32,0},{1,33},{33,1},{2,34},{34,2},{3,35},{35,3},{4,36},{36... | collective-permute-start | bytes 786440 | tf_op jit(solution)/shard_map/ppermute | solution.py:27
  36.0 4.5 %collective-permute-start.3 = (f32[256,128]{1,0:T(8,128)S(1)}, f32[256,128]{1,0:T(8,128)S(1)}, u32[]{:S(2)}, u32[]{:S(2)}) collective-permute-start(f32[256,128]{1,0:T(8,128)S(1)} %constant_dynamic-slice_fusion.4), channel_id=1, source_target_pairs={{0,16},{16,0},{1,17},{17,1},{2,18},{18,2},{3,19},{19,3},{4,20},{20... | collective-permute-start | bytes 393224 | tf_op jit(solution)/shard_map/ppermute | solution.py:27
  40.5 8.7 %collective-permute-start.4 = (f32[128,128]{1,0:T(8,128)S(1)}, f32[128,128]{1,0:T(8,128)S(1)}, u32[]{:S(2)}, u32[]{:S(2)}) collective-permute-start(f32[128,128]{1,0:T(8,128)S(1)} %constant_dynamic-slice_fusion.3), channel_id=1, source_target_pairs={{0,8},{8,0},{1,9},{9,1},{2,10},{10,2},{3,11},{11,3},{4,12},{12,4},... | collective-permute-start | bytes 196616 | tf_op jit(solution)/shard_map/ppermute | solution.py:27
  49.3 4.0 %collective-permute-start.5 = (f32[64,128]{1,0:T(8,128)S(1)}, f32[64,128]{1,0:T(8,128)S(1)}, u32[]{:S(2)}, u32[]{:S(2)}) collective-permute-start(f32[64,128]{1,0:T(8,128)S(1)} %constant_dynamic-slice_fusion.2), channel_id=1, source_target_pairs={{0,4},{4,0},{1,5},{5,1},{2,6},{6,2},{3,7},{7,3},{8,12},{12,8},{9,1... | collective-permute-start | bytes 98312 | tf_op jit(solution)/shard_map/ppermute | solution.py:27
  53.3 2.7 %collective-permute-start.6 = (f32[32,128]{1,0:T(8,128)S(1)}, f32[32,128]{1,0:T(8,128)S(1)}, u32[]{:S(2)}, u32[]{:S(2)}) collective-permute-start(f32[32,128]{1,0:T(8,128)S(1)} %constant_dynamic-slice_fusion.1), channel_id=1, source_target_pairs={{0,2},{2,0},{1,3},{3,1},{4,6},{6,4},{5,7},{7,5},{8,10},{10,8},{9,1... | collective-permute-start | bytes 49160 | tf_op jit(solution)/shard_map/ppermute | solution.py:27
  56.0 8.7 %collective-permute-start.7 = (f32[16,128]{1,0:T(8,128)S(1)}, f32[16,128]{1,0:T(8,128)S(1)}, u32[]{:S(2)}, u32[]{:S(2)}) collective-permute-start(f32[16,128]{1,0:T(8,128)S(1)} %constant_dynamic-slice_fusion), channel_id=1, source_target_pairs={{0,1},{1,0},{2,3},{3,2},{4,5},{5,4},{6,7},{7,6},{8,9},{9,8},{10,11... | collective-permute-start | bytes 24584 | tf_op jit(solution)/shard_map/ppermute | solution.py:27
  66.0 30.7 %copy-start.4 = (f32[16]{0:T(128)S(1)}, f32[16]{0:T(128)}, u32[]{:S(2)}) copy-start(f32[16]{0:T(128)} %param.11) | copy-start | bytes 196
  66.0 30.7 %copy-start.5 = (f32[16]{0:T(128)S(1)}, f32[16]{0:T(128)}, u32[]{:S(2)}) copy-start(f32[16]{0:T(128)} %param.9) | copy-start | bytes 196
  87.2 9.5 %copy-start.3 = (f32[16,128]{1,0:T(8,128)S(1)}, f32[16,128]{1,0:T(8,128)}, u32[]{:S(2)}) copy-start(f32[16,128]{1,0:T(8,128)} %param.7) | copy-start | bytes 24580
  95.9 0.8 copy-start.2
  96.6 0.7 copy-start.1
  105.9 35.9 %all-to-all-start.3 = ((bf16[64,4,16,128]{3,2,1,0:T(8,128)(2,1)}), bf16[64,4,16,128]{3,2,1,0:T(8,128)(2,1)S(1)}, u32[]{:S(2)}, u32[]{:S(2)}) async-start(bf16[64,4,16,128]{3,2,1,0:T(8,128)(2,1)} %broadcast_in_dim.19), calls=%async_computation.3 | async-start | bytes 2097152 | tf_op jit(solution)/shard_map/all_to_all | solution.py:32
  113.3 0.5 copy-start.6
  113.3 0.5 copy-start.7
where the time goes:
time: 143 us
  waiting for transfers between devices  62.1 us (43%)
  starting transfers between devices  35.1 us (25%)
  blocking collectives  34.5 us (24%)
  local copies, waits for them, and re-layouts  6.11 us (4%)
  other arithmetic  3.58 us (3%)
  between operations  1.59 us (1%)
    ppermute x8, waiting for transfers between devices, from_partner(): return lax.ppermute(block, axis, route)  34.8 us
    all_to_all x3, blocking collectives, sent_to_all(): return lax.all_to_all(copies, axis, split_axis=0, concat_axis=0, tiled=True)  34.5 us
    ppermute x8, starting transfers between devices, from_partner(): return lax.ppermute(block, axis, route)  27.7 us
    all_to_all x1, waiting for transfers between devices, sent_to_all(): return lax.all_to_all(copies, axis, split_axis=0, concat_axis=0, tiled=True)  27.3 us
    all_to_all x1, starting transfers between devices, sent_to_all(): return lax.all_to_all(copies, axis, split_axis=0, concat_axis=0, tiled=True)  7.33 us
  transfers between devices with their start and end apart: 9, of which 9 were waited for; matrix products, arithmetic and copies ran while one was open for 0% of the time, Pallas kernels for 0%

commit v1 on v0

v1 whole, which is shorter than its diff:
```python
import jax
import jax.numpy as jnp
from jax import lax
from jax.sharding import Mesh
from jax.sharding import PartitionSpec as P

DP = ("y", "x", "z", "c")


beta_one = 0.9
beta_two = 0.95
learn_rate = 0.05
decay_rate = 0.1
adam_epsilon = 1e-08
clip_rms = 0.01
first_fix = 1.0 - 0.9**10
second_fix = 1.0 - 0.95**10


def exchange(x, axes):
    return lax.all_to_all(x, axes, split_axis=0, concat_axis=0, tiled=True)


def sent_to_all(x, axes):
    return exchange(jnp.broadcast_to(x, (lax.axis_size(axes), *x.shape)), axes)


def advance(clipped, master, first, second):
    first_new = beta_one * first + (1.0 - beta_one) * clipped
    second_new = beta_two * second + (1.0 - beta_two) * clipped * clipped
    change = first_new / first_fix / (jnp.sqrt(second_new / second_fix) + adam_epsilon)
    master_new = master * (1.0 - learn_rate * decay_rate) - learn_rate * change
    return master_new, first_new, second_new


def shards(grads, master, first_q, first_scale, second_q, second_scale):
    blocks, width = grads.shape[1:]
    rows = master.shape[0]
    planes, line, cores = lax.axis_size(("y", "x")), lax.axis_size("z"), lax.axis_size("c")
    held = line * rows
    first = first_q.astype(jnp.float32) * first_scale[:, None]
    second = second_q.astype(jnp.float32) * second_scale[:, None]

    local = grads[0].reshape(planes, line, cores, rows, width).swapaxes(1, 2)
    arrived = exchange(local.reshape(planes * cores, held, width), ("y", "x", "c"))
    part = arrived.astype(jnp.float32).sum(axis=0)

    packed = jnp.concatenate([part, master, first, second], axis=0)
    shared = sent_to_all(packed, "z")
    total = shared[:, :held].sum(axis=0)
    states = shared[:, held:].reshape(line, 3, rows, width)
    line_master, line_first, line_second = (
        states[:, i].reshape(held, width) for i in range(3)
    )

    squares = sent_to_all(jnp.sum(total * total, axis=0, keepdims=True), ("y", "x", "c")).sum()
    limit = clip_rms * jnp.sqrt(jnp.float32(blocks * width))
    factor = jnp.minimum(1.0, limit / (jnp.sqrt(squares) + 1e-06))

    line_new, _, _ = advance(factor * total, line_master, line_first, line_second)
    weights = sent_to_all(line_new.astype(jnp.bfloat16), ("y", "x"))
    weights = weights.reshape(planes, line, 1, rows, width)
    partner = lax.ppermute(weights, "c", [(0, 1), (1, 0)])
    mine = jnp.arange(cores) == lax.axis_index("c")
    weights = jnp.where(mine[:, None, None], weights, partner).reshape(blocks, width)

    own = lax.dynamic_slice_in_dim(total, lax.axis_index("z") * rows, rows, 0)
    master_new, first_new, second_new = advance(factor * own, master, first, second)
    first_scale_new = jnp.max(jnp.abs(first_new), axis=1) + 1e-08
    second_scale_new = jnp.max(jnp.abs(second_new), axis=1) + 1e-08
    first_q_new = (first_new / first_scale_new[:, None]).astype(jnp.bfloat16)
    second_q_new = (second_new / second_scale_new[:, None]).astype(jnp.bfloat16)
    return (weights, master_new, first_q_new, first_scale_new, second_q_new, second_scale_new)


def solution(mesh):
    torus = Mesh(mesh.devices.reshape(4, 4, 8, 2), DP)
    in_specs = (P(DP, None, None), P(DP, None), P(DP, None), P(DP), P(DP, None), P(DP))
    out_specs = (P(), P(DP, None), P(DP, None), P(DP), P(DP, None), P(DP))
    return jax.shard_map(
        shards, mesh=torus, in_specs=in_specs, out_specs=out_specs, check_vma=False
    )
```

time: 143 us -> 92.8 us (0.65)
  waiting for transfers between devices: 62.1 us -> 34.2 us
  starting transfers between devices: 35.1 us -> 19.6 us
  blocking collectives: 34.5 us -> 28.8 us
  local copies, waits for them, and re-layouts: 6.11 us -> 4.3 us
    ppermute x8 -> x1, waiting for transfers between devices: 34.8 us -> 0.84 us  [shards(): partner = lax.ppermute(weights, 'c', [(0, 1), (1, 0)])]
    ppermute x8 -> x1, starting transfers between devices: 27.7 us -> 1.76 us  [shards(): partner = lax.ppermute(weights, 'c', [(0, 1), (1, 0)])]
    all_to_all x1 -> x3, starting transfers between devices: 7.33 us -> 17.8 us  [exchange(): return lax.all_to_all(x, axes, split_axis=0, concat_axis=0, tiled=True)]
    all_to_all x1 -> x3, waiting for transfers between devices: 27.3 us -> 33.4 us  [exchange(): return lax.all_to_all(x, axes, split_axis=0, concat_axis=0, tiled=True)]
    all_to_all x3 -> x1, blocking collectives: 34.5 us -> 28.8 us  [exchange(): return lax.all_to_all(x, axes, split_axis=0, concat_axis=0, tiled=True)]
    transpose x0 -> x1, local copies, waits for them, and re-layouts: none -> 2.45 us  [shards(): local = grads[0].reshape(planes, line, cores, rows, width).swapaxes(1, 2)]
    select_n x0 -> x1, other arithmetic: none -> 1.48 us  [shards(): jnp.where(mine[:, None, None], weights, partner).reshape(blocks, width)]
  transfers between devices with their start and end apart: 9 -> 4, of which waited for: 9 -> 4; matrix products, arithmetic and copies ran while one was open for 0% -> 2% of each run, Pallas kernels for 0% -> 0%
where the time goes in v1:
time: 92.8 us; the launch traced here: 92.4 us
  waiting for transfers between devices  34.2 us (37%)
  blocking collectives  28.8 us (31%)
  starting transfers between devices  19.6 us (21%)
  local copies, waits for them, and re-layouts  4.3 us (5%)
  other arithmetic  3.96 us (4%)
  between operations  1.51 us (2%)
    all_to_all x3, waiting for transfers between devices, exchange(): return lax.all_to_all(x, axes, split_axis=0, concat_axis=0, tiled=True)  33.4 us
    all_to_all x1, blocking collectives, exchange(): return lax.all_to_all(x, axes, split_axis=0, concat_axis=0, tiled=True)  28.8 us
    all_to_all x3, starting transfers between devices, exchange(): return lax.all_to_all(x, axes, split_axis=0, concat_axis=0, tiled=True)  17.8 us
    transpose x1, local copies, waits for them, and re-layouts, shards(): local = grads[0].reshape(planes, line, cores, rows, width).swapaxes(1, 2)  2.45 us
  transfers between devices with their start and end apart: 4, of which 4 were waited for; matrix products, arithmetic and copies ran while one was open for 2% of the time, Pallas kernels for 0%

profile of v1, /device:TPU:1, one launch (start us, length us, event | category | flops | bytes accessed | tf_op | source)
XLA Modules:
  0.0 92.4 jit_solution(9270323979498627176)
XLA Ops:
  0.6 2.5 %copy.14 = bf16[16,2,8,16,128]{4,3,2,1,0:T(8,128)(2,1)} copy(bf16[16,2,8,16,128]{4,3,1,2,0:T(8,128)(2,1)} %bitcast.31) | data formatting | bytes 2097152 | tf_op jit(solution)/shard_map/transpose | solution.py:44
  3.1 0.0 copy-start
  3.1 0.0 copy-start.1
  3.1 0.0 copy-start.3
  3.1 0.0 copy-start.4
  3.1 8.7 %all-to-all-start = ((bf16[32,128,128]{2,1,0:T(8,128)(2,1)}), bf16[32,128,128]{2,1,0:T(8,128)(2,1)S(1)}, u32[]{:S(2)}, u32[]{:S(2)}) async-start(bf16[32,128,128]{2,1,0:T(8,128)(2,1)} %bitcast.2), calls=%async_computation | async-start | bytes 2097152 | tf_op jit(solution)/shard_map/all_to_all | solution.py:21
  11.8 0.0 copy-done
  11.8 0.0 copy-done.1
  11.8 0.0 copy-done.3
  11.9 0.0 copy-done.4
  11.9 0.0 copy-start.2
  11.9 0.1 convert_multiply_fusion
  12.0 16.9 %all-to-all-done = bf16[32,128,128]{2,1,0:T(8,128)(2,1)S(1)} async-done(((bf16[32,128,128]{2,1,0:T(8,128)(2,1)}), bf16[32,128,128]{2,1,0:T(8,128)(2,1)S(1)}, u32[]{:S(2)}, u32[]{:S(2)}) %all-to-all-start) | async-done | bytes 1048608 | tf_op jit(solution)/shard_map/all_to_all | solution.py:21
  28.9 0.2 convert_reduce_fusion
  29.0 0.0 copy-done.2
  29.1 28.8 %all_to_all.20 = f32[8,176,128]{2,1,0:T(8,128)S(1)} all-to-all(f32[8,176,128]{2,1,0:T(8,128)S(1)} %broadcast_in_dim.54), channel_id=1, replica_groups=mesh['y'=4,'x'=4,'z'=8,'c'=2] {'z'}, dimensions={0} | all-to-all | bytes 1441792 | tf_op jit(solution)/shard_map/all_to_all | solution.py:21
  58.0 0.6 broadcast_in_dim.55
  58.6 5.5 %all-to-all-start.2 = ((f32[32,1,128]{2,1,0:T(1,128)}), f32[32,1,128]{2,1,0:T(1,128)S(1)}, u32[]{:S(2)}, u32[]{:S(2)}) async-start(f32[32,1,128]{2,1,0:T(1,128)} %broadcast_in_dim.55), calls=%async_computation.2 | async-start | bytes 32768 | tf_op jit(solution)/shard_map/all_to_all | solution.py:21
  64.2 6.8 %all-to-all-done.2 = f32[32,1,128]{2,1,0:T(1,128)S(1)} async-done(((f32[32,1,128]{2,1,0:T(1,128)}), f32[32,1,128]{2,1,0:T(1,128)S(1)}, u32[]{:S(2)}, u32[]{:S(2)}) %all-to-all-start.2) | async-done | bytes 16416 | tf_op jit(solution)/shard_map/all_to_all | solution.py:21
  71.0 0.6 reduce_sum.39
  72.4 0.1 fusion.8
  72.4 0.9 broadcast_in_dim.56
  73.3 3.6 %all-to-all-start.3 = ((bf16[16,128,128]{2,1,0:T(8,128)(2,1)}), bf16[16,128,128]{2,1,0:T(8,128)(2,1)S(1)}, u32[]{:S(2)}, u32[]{:S(2)}) async-start(bf16[16,128,128]{2,1,0:T(8,128)(2,1)} %broadcast_in_dim.56), calls=%async_computation.3 | async-start | bytes 1048576 | tf_op jit(solution)/shard_map/all_to_all | solution.py:21
  76.9 0.1 broadcast_in_dim.51
  77.0 0.1 broadcast_in_dim.52
  77.2 0.8 abs_reduce_fusion
  78.0 9.6 %all-to-all-done.3 = bf16[16,128,128]{2,1,0:T(8,128)(2,1)S(1)} async-done(((bf16[16,128,128]{2,1,0:T(8,128)(2,1)}), bf16[16,128,128]{2,1,0:T(8,128)(2,1)S(1)}, u32[]{:S(2)}, u32[]{:S(2)}) %all-to-all-start.3) | async-done | bytes 524320 | tf_op jit(solution)/shard_map/all_to_all | solution.py:21
  87.6 1.8 %collective-permute-start = (bf16[16,8,1,16,128]{4,3,1,0,2:T(8,128)(2,1)S(1)}, bf16[16,8,1,16,128]{4,3,1,0,2:T(8,128)(2,1)S(1)}, u32[]{:S(2)}, u32[]{:S(2)}) collective-permute-start(bf16[16,8,1,16,128]{4,3,1,0,2:T(8,128)(2,1)S(1)} %bitcast.29), channel_id=1, source_target_pairs={{0,1},{1,0},{2,3},{3,2},{4,5},{5,4},{6,7},{7,6},{8,9},{9,8},{10,11... | collective-permute-start | bytes 1572872 | tf_op jit(solution)/shard_map/ppermute | solution.py:63
  89.4 0.0 copy-start.5
  89.4 0.0 copy-start.6
  89.4 0.7 divide_convert_fusion
  90.1 0.8 collective-permute-done
  90.9 1.5 %bitcast_select_fusion = bf16[4096,128]{1,0:T(8,128)(2,1)} fusion(pred[4096]{0:T(1024)(128)(4,1)S(1)} %broadcast_in_dim.52, bf16[16,8,16,128]{3,2,1,0:T(8,128)(2,1)S(1)} %bitcast.33, bf16[16,8,16,128]{3,2,1,0:T(8,128)(2,1)S(1)} %bitcast.30), kind=kLoop, calls=%fused_computation.1 | loop fusion | flops 524288 | bytes 2101248 | tf_op jit(solution)/shard_map/jit(_where)/select_n | solution.py:65
  92.4 0.0 copy-done.5
  92.4 0.0 copy-done.6
  (9 shorter events, 0.2 us)
Async XLA Ops:
  3.1 8.7 %copy-start = (bf16[16,128]{1,0:T(8,128)(2,1)S(1)}, bf16[16,128]{1,0:T(8,128)(2,1)}, u32[]{:S(2)}) copy-start(bf16[16,128]{1,0:T(8,128)(2,1)} %param.10) | copy-start | bytes 12292
  3.1 8.7 %copy-start.1 = (bf16[16,128]{1,0:T(8,128)(2,1)S(1)}, bf16[16,128]{1,0:T(8,128)(2,1)}, u32[]{:S(2)}) copy-start(bf16[16,128]{1,0:T(8,128)(2,1)} %param.8) | copy-start | bytes 12292
  3.1 8.8 %copy-start.3 = (f32[16]{0:T(128)S(1)}, f32[16]{0:T(128)}, u32[]{:S(2)}) copy-start(f32[16]{0:T(128)} %param.11) | copy-start | bytes 196
  3.1 8.8 %copy-start.4 = (f32[16]{0:T(128)S(1)}, f32[16]{0:T(128)}, u32[]{:S(2)}) copy-start(f32[16]{0:T(128)} %param.9) | copy-start | bytes 196
  3.1 25.8 %all-to-all-start = ((bf16[32,128,128]{2,1,0:T(8,128)(2,1)}), bf16[32,128,128]{2,1,0:T(8,128)(2,1)S(1)}, u32[]{:S(2)}, u32[]{:S(2)}) async-start(bf16[32,128,128]{2,1,0:T(8,128)(2,1)} %bitcast.2), calls=%async_computation | async-start | bytes 2097152 | tf_op jit(solution)/shard_map/all_to_all | solution.py:21
  11.9 17.2 %copy-start.2 = (f32[16,128]{1,0:T(8,128)S(1)}, f32[16,128]{1,0:T(8,128)}, u32[]{:S(2)}) copy-start(f32[16,128]{1,0:T(8,128)} %param.7) | copy-start | bytes 24580
  58.6 12.4 %all-to-all-start.2 = ((f32[32,1,128]{2,1,0:T(1,128)}), f32[32,1,128]{2,1,0:T(1,128)S(1)}, u32[]{:S(2)}, u32[]{:S(2)}) async-start(f32[32,1,128]{2,1,0:T(1,128)} %broadcast_in_dim.55), calls=%async_computation.2 | async-start | bytes 32768 | tf_op jit(solution)/shard_map/all_to_all | solution.py:21
  73.3 14.3 %all-to-all-start.3 = ((bf16[16,128,128]{2,1,0:T(8,128)(2,1)}), bf16[16,128,128]{2,1,0:T(8,128)(2,1)S(1)}, u32[]{:S(2)}, u32[]{:S(2)}) async-start(bf16[16,128,128]{2,1,0:T(8,128)(2,1)} %broadcast_in_dim.56), calls=%async_computation.3 | async-start | bytes 1048576 | tf_op jit(solution)/shard_map/all_to_all | solution.py:21
  87.6 3.3 %collective-permute-start = (bf16[16,8,1,16,128]{4,3,1,0,2:T(8,128)(2,1)S(1)}, bf16[16,8,1,16,128]{4,3,1,0,2:T(8,128)(2,1)S(1)}, u32[]{:S(2)}, u32[]{:S(2)}) collective-permute-start(bf16[16,8,1,16,128]{4,3,1,0,2:T(8,128)(2,1)S(1)} %bitcast.29), channel_id=1, source_target_pairs={{0,1},{1,0},{2,3},{3,2},{4,5},{5,4},{6,7},{7,6},{8,9},{9,8},{10,11... | collective-permute-start | bytes 1572872 | tf_op jit(solution)/shard_map/ppermute | solution.py:63
  89.4 3.0 %copy-start.5 = (f32[16]{0:T(128)}, f32[16]{0:T(128)S(1)}, u32[]{:S(2)}) copy-start(f32[16]{0:T(128)S(1)} %broadcast_add_fusion) | copy-start | bytes 196
  89.4 3.0 %copy-start.6 = (f32[16]{0:T(128)}, f32[16]{0:T(128)S(1)}, u32[]{:S(2)}) copy-start(f32[16]{0:T(128)S(1)} %broadcast_add_fusion.1) | copy-start | bytes 196

commit v2 on v1

--- a/solution.py
+++ b/solution.py
@@ -25,6 +25,16 @@
     return exchange(jnp.broadcast_to(x, (lax.axis_size(axes), *x.shape)), axes)
 
 
+def doubled(x, axis):
+    count = lax.axis_size(axis)
+    index = lax.axis_index(axis)
+    for level in range(count.bit_length() - 1):
+        other = lax.ppermute(x, axis, [(i, i ^ 1 << level) for i in range(count)])
+        mine = jnp.arange(2) == (index >> level & 1)
+        x = jnp.where(mine[:, None, None, None, None], x, other).reshape(-1, *x.shape[1:])
+    return x
+
+
 def advance(clipped, master, first, second):
     first_new = beta_one * first + (1.0 - beta_one) * clipped
     second_new = beta_two * second + (1.0 - beta_two) * clipped * clipped
@@ -38,17 +48,19 @@
     rows = master.shape[0]
     planes, line, cores = lax.axis_size(("y", "x")), lax.axis_size("z"), lax.axis_size("c")
     held = line * rows
+    swap = [(0, 1), (1, 0)]
     first = first_q.astype(jnp.float32) * first_scale[:, None]
     second = second_q.astype(jnp.float32) * second_scale[:, None]
 
-    local = grads[0].reshape(planes, line, cores, rows, width).swapaxes(1, 2)
-    arrived = exchange(local.reshape(planes * cores, held, width), ("y", "x", "c"))
-    part = arrived.astype(jnp.float32).sum(axis=0)
+    arrived = exchange(grads[0].reshape(planes, line * cores * rows, width), ("y", "x"))
+    states = doubled(jnp.stack([master, first, second])[None], "z")
+    arrived, states = lax.optimization_barrier((arrived, states))
+    both = arrived.astype(jnp.float32).sum(axis=0).reshape(line, cores, rows, width)
+    core = lax.axis_index("c")
+    kept, sent = (lax.dynamic_index_in_dim(both, i, 1, False) for i in (core, 1 - core))
+    part = (kept + lax.ppermute(sent, "c", swap)).reshape(held, width)
 
-    packed = jnp.concatenate([part, master, first, second], axis=0)
-    shared = sent_to_all(packed, "z")
-    total = shared[:, :held].sum(axis=0)
-    states = shared[:, held:].reshape(line, 3, rows, width)
+    total = sent_to_all(part, "z").sum(axis=0)
     line_master, line_first, line_second = (
         states[:, i].reshape(held, width) for i in range(3)
     )
@@ -60,7 +72,7 @@
     line_new, _, _ = advance(factor * total, line_master, line_first, line_second)
     weights = sent_to_all(line_new.astype(jnp.bfloat16), ("y", "x"))
     weights = weights.reshape(planes, line, 1, rows, width)
-    partner = lax.ppermute(weights, "c", [(0, 1), (1, 0)])
+    partner = lax.ppermute(weights, "c", swap)
     mine = jnp.arange(cores) == lax.axis_index("c")
     weights = jnp.where(mine[:, None, None], weights, partner).reshape(blocks, width)
 

time: 92.8 us -> 92.2 us (level)
  starting transfers between devices: 19.6 us -> 36.8 us
  waiting for transfers between devices: 34.2 us -> 23 us
  blocking collectives: 28.8 us -> 24 us
  local copies, waits for them, and re-layouts: 4.3 us -> 2.2 us
    all_to_all x3, waiting for transfers between devices: 33.4 us -> 16.5 us  [exchange(): return lax.all_to_all(x, axes, split_axis=0, concat_axis=0, tiled=True)]
    ppermute x1 -> x5, starting transfers between devices: 1.76 us -> 16.6 us  [the longest x3 10.9 us: doubled(): other = lax.ppermute(x, axis, [(i, i ^ 1 << level) for i in range(count)])]
    ppermute x1 -> x5, waiting for transfers between devices: 0.84 us -> 6.55 us  [the longest x3 4.81 us: doubled(): other = lax.ppermute(x, axis, [(i, i ^ 1 << level) for i in range(count)])]
    all_to_all x1, blocking collectives: 28.8 us -> 24 us  [exchange(): return lax.all_to_all(x, axes, split_axis=0, concat_axis=0, tiled=True)]
    transpose x1 -> x0, local copies, waits for them, and re-layouts: 2.45 us -> none  [shards(): local = grads[0].reshape(planes, line, cores, rows, width).swapaxes(1, 2)]
    all_to_all x3, starting transfers between devices: 17.8 us -> 20.2 us  [exchange(): return lax.all_to_all(x, axes, split_axis=0, concat_axis=0, tiled=True)]
  transfers between devices with their start and end apart: 4 -> 8, of which waited for: 4 -> 7; matrix products, arithmetic and copies ran while one was open for 2% -> 3% of each run, Pallas kernels for 0% -> 0%
where the time goes in v2:
time: 92.2 us; the launch traced here: 91.8 us
  starting transfers between devices  36.8 us (40%)
  blocking collectives  24 us (26%)
  waiting for transfers between devices  23 us (25%)
  other arithmetic  4.22 us (5%)
  local copies, waits for them, and re-layouts  2.2 us (2%)
  between operations  1.57 us (2%)
    all_to_all x1, blocking collectives, exchange(): return lax.all_to_all(x, axes, split_axis=0, concat_axis=0, tiled=True)  24 us
    all_to_all x3, starting transfers between devices, exchange(): return lax.all_to_all(x, axes, split_axis=0, concat_axis=0, tiled=True)  20.2 us
    all_to_all x3, waiting for transfers between devices, exchange(): return lax.all_to_all(x, axes, split_axis=0, concat_axis=0, tiled=True)  16.5 us
    ppermute x3, starting transfers between devices, doubled(): other = lax.ppermute(x, axis, [(i, i ^ 1 << level) for i in range(count)])  10.9 us
    ppermute x3, waiting for transfers between devices, doubled(): other = lax.ppermute(x, axis, [(i, i ^ 1 << level) for i in range(count)])  4.81 us
    ppermute x1, starting transfers between devices, shards(): part = (kept + lax.ppermute(sent, 'c', swap)).reshape(held, width)  3.92 us
  transfers between devices with their start and end apart: 8, of which 7 were waited for; matrix products, arithmetic and copies ran while one was open for 3% of the time, Pallas kernels for 0%

profile of v2, /device:TPU:1, one launch (start us, length us, event | category | flops | bytes accessed | tf_op | source)
XLA Modules:
  0.0 91.8 jit_solution(15651150867768357495)
XLA Ops:
  0.6 0.0 copy-start
  0.6 0.0 copy-start.1
  0.7 0.0 copy-start.3
  0.7 0.0 copy-start.4
  0.7 0.0 copy-start.2
  0.7 7.7 %all-to-all-start = ((bf16[16,256,128]{2,1,0:T(8,128)(2,1)}), bf16[16,256,128]{2,1,0:T(8,128)(2,1)S(1)}, u32[]{:S(2)}, u32[]{:S(2)}) async-start(bf16[16,256,128]{2,1,0:T(8,128)(2,1)} %bitcast.45), calls=%async_computation | async-start | bytes 2097152 | tf_op jit(solution)/shard_map/all_to_all | solution.py:21
  8.4 0.0 copy-done
  8.4 0.0 copy-done.1
  8.4 0.0 copy-done.3
  8.4 0.0 copy-done.4
  8.4 0.1 fusion.10
  8.5 0.0 copy-done.2
  8.5 1.7 %collective-permute-start = (f32[1,3,16,128]{3,2,1,0:T(8,128)S(1)}, f32[1,3,16,128]{3,2,1,0:T(8,128)S(1)}, u32[]{:S(2)}, u32[]{:S(2)}) collective-permute-start(f32[1,3,16,128]{3,2,1,0:T(8,128)S(1)} %get-tuple-element.19), channel_id=1, source_target_pairs={{0,2},{2,0},{4,6},{6,4},{8,10},{10,8},{12,14},{14,12},{1,3},{3,1},... | collective-permute-start | bytes 73736 | tf_op jit(solution)/shard_map/ppermute | solution.py:32
  10.3 1.2 %collective-permute-done = f32[1,3,16,128]{3,2,1,0:T(8,128)S(1)} collective-permute-done((f32[1,3,16,128]{3,2,1,0:T(8,128)S(1)}, f32[1,3,16,128]{3,2,1,0:T(8,128)S(1)}, u32[]{:S(2)}, u32[]{:S(2)}) %collective-permute-start) | collective-permute-done | bytes 24608 | tf_op jit(solution)/shard_map/ppermute | solution.py:32
  11.5 0.1 broadcast_select_fusion.2
  11.5 3.0 %collective-permute-start.1 = (f32[2,3,16,128]{3,2,0,1:T(8,128)S(1)}, f32[2,3,16,128]{3,2,0,1:T(8,128)S(1)}, u32[]{:S(2)}, u32[]{:S(2)}) collective-permute-start(f32[2,3,16,128]{3,2,0,1:T(8,128)S(1)} %broadcast_select_fusion.2), channel_id=1, source_target_pairs={{0,4},{2,6},{4,0},{6,2},{8,12},{10,14},{12,8},{14,10},{1,5},{3,7},... | collective-permute-start | bytes 147464 | tf_op jit(solution)/shard_map/ppermute | solution.py:32
  14.6 0.1 broadcast_in_dim.127
  14.6 0.1 broadcast_in_dim.128
  14.7 1.6 %collective-permute-done.1 = f32[2,3,16,128]{3,2,0,1:T(8,128)S(1)} collective-permute-done((f32[2,3,16,128]{3,2,0,1:T(8,128)S(1)}, f32[2,3,16,128]{3,2,0,1:T(8,128)S(1)}, u32[]{:S(2)}, u32[]{:S(2)}) %collective-permute-start.1) | collective-permute-done | bytes 49184 | tf_op jit(solution)/shard_map/ppermute | solution.py:32
  16.4 0.1 broadcast_select_fusion.1
  16.4 6.2 %collective-permute-start.2 = (f32[4,3,16,128]{3,2,0,1:T(8,128)S(1)}, f32[4,3,16,128]{3,2,0,1:T(8,128)S(1)}, u32[]{:S(2)}, u32[]{:S(2)}) collective-permute-start(f32[4,3,16,128]{3,2,0,1:T(8,128)S(1)} %broadcast_select_fusion.1), channel_id=1, source_target_pairs={{0,8},{2,10},{4,12},{6,14},{8,0},{10,2},{12,4},{14,6},{1,9},{3,11}... | collective-permute-start | bytes 294920 | tf_op jit(solution)/shard_map/ppermute | solution.py:32
  22.6 0.1 broadcast_in_dim.124
  22.7 0.1 broadcast_in_dim.125
  22.8 2.0 %collective-permute-done.2 = f32[4,3,16,128]{3,2,0,1:T(8,128)S(1)} collective-permute-done((f32[4,3,16,128]{3,2,0,1:T(8,128)S(1)}, f32[4,3,16,128]{3,2,0,1:T(8,128)S(1)}, u32[]{:S(2)}, u32[]{:S(2)}) %collective-permute-start.2) | collective-permute-done | bytes 98336 | tf_op jit(solution)/shard_map/ppermute | solution.py:32
  24.8 0.1 broadcast_select_fusion
  24.9 0.0 all-to-all-done
  24.9 0.1 convert_reduce_fusion
  25.1 3.9 %collective-permute-start.3 = (f32[8,16,128]{2,1,0:T(8,128)S(1)}, f32[8,16,128]{2,1,0:T(8,128)S(1)}, u32[]{:S(2)}, u32[]{:S(2)}) collective-permute-start(f32[8,16,128]{2,1,0:T(8,128)S(1)} %dynamic-slice_bitcast_fusion), channel_id=1, source_target_pairs={{0,1},{1,0},{2,3},{3,2},{4,5},{5,4},{6,7},{7,6},{8,9},{9,8},{10,11... | collective-permute-start | bytes 196616 | tf_op jit(solution)/shard_map/ppermute | solution.py:61
  29.0 0.9 collective-permute-done.3
  30.0 24.0 %all_to_all.20 = f32[8,128,128]{2,1,0:T(8,128)S(1)} all-to-all(f32[8,128,128]{2,1,0:T(8,128)S(1)} %broadcast_in_dim.142), channel_id=1, replica_groups=mesh['y'=4,'x'=4,'z'=8,'c'=2] {'z'}, dimensions={0} | all-to-all | bytes 1048576 | tf_op jit(solution)/shard_map/all_to_all | solution.py:21
  54.1 0.6 broadcast_in_dim.143
  54.7 8.9 %all-to-all-start.2 = ((f32[32,1,128]{2,1,0:T(1,128)}), f32[32,1,128]{2,1,0:T(1,128)S(1)}, u32[]{:S(2)}, u32[]{:S(2)}) async-start(f32[32,1,128]{2,1,0:T(1,128)} %broadcast_in_dim.143), calls=%async_computation.2 | async-start | bytes 32768 | tf_op jit(solution)/shard_map/all_to_all | solution.py:21
  63.6 6.9 %all-to-all-done.2 = f32[32,1,128]{2,1,0:T(1,128)S(1)} async-done(((f32[32,1,128]{2,1,0:T(1,128)}), f32[32,1,128]{2,1,0:T(1,128)S(1)}, u32[]{:S(2)}, u32[]{:S(2)}) %all-to-all-start.2) | async-done | bytes 16416 | tf_op jit(solution)/shard_map/all_to_all | solution.py:21
  70.5 0.6 reduce_sum.39
  71.8 0.1 fusion.8
  71.9 0.9 broadcast_in_dim.144
  72.8 3.6 %all-to-all-start.3 = ((bf16[16,128,128]{2,1,0:T(8,128)(2,1)}), bf16[16,128,128]{2,1,0:T(8,128)(2,1)S(1)}, u32[]{:S(2)}, u32[]{:S(2)}) async-start(bf16[16,128,128]{2,1,0:T(8,128)(2,1)} %broadcast_in_dim.144), calls=%async_computation.3 | async-start | bytes 1048576 | tf_op jit(solution)/shard_map/all_to_all | solution.py:21
  76.4 0.1 broadcast_in_dim.121
  76.5 0.1 broadcast_in_dim.122
  76.6 0.8 abs_reduce_fusion
  77.4 9.6 %all-to-all-done.3 = bf16[16,128,128]{2,1,0:T(8,128)(2,1)S(1)} async-done(((bf16[16,128,128]{2,1,0:T(8,128)(2,1)}), bf16[16,128,128]{2,1,0:T(8,128)(2,1)S(1)}, u32[]{:S(2)}, u32[]{:S(2)}) %all-to-all-start.3) | async-done | bytes 524320 | tf_op jit(solution)/shard_map/all_to_all | solution.py:21
  87.1 1.8 %collective-permute-start.4 = (bf16[16,8,1,16,128]{4,3,1,0,2:T(8,128)(2,1)S(1)}, bf16[16,8,1,16,128]{4,3,1,0,2:T(8,128)(2,1)S(1)}, u32[]{:S(2)}, u32[]{:S(2)}) collective-permute-start(bf16[16,8,1,16,128]{4,3,1,0,2:T(8,128)(2,1)S(1)} %bitcast.43), channel_id=1, source_target_pairs={{0,1},{1,0},{2,3},{3,2},{4,5},{5,4},{6,7},{7,6},{8,9},{9,8},{10,11... | collective-permute-start | bytes 1572872 | tf_op jit(solution)/shard_map/ppermute | solution.py:75
  88.8 0.0 copy-start.5
  88.8 0.7 divide_convert_fusion
  89.5 0.8 collective-permute-done.4
  90.4 1.5 %bitcast_select_fusion = bf16[4096,128]{1,0:T(8,128)(2,1)} fusion(pred[4096]{0:T(1024)(128)(4,1)S(1)} %broadcast_in_dim.122, bf16[16,8,16,128]{3,2,1,0:T(8,128)(2,1)S(1)} %bitcast.50, bf16[16,8,16,128]{3,2,1,0:T(8,128)(2,1)S(1)} %bitcast.44), kind=kLoop, calls=%fused_computation.1 | loop fusion | flops 524288 | bytes 2101248 | tf_op jit(solution)/shard_map/jit(_where)/select_n | solution.py:77
  91.8 0.0 copy-done.5
  91.8 0.0 copy-done.6
  (18 shorter events, 0.2 us)
Async XLA Ops:
  0.6 7.8 %copy-start = (bf16[16,128]{1,0:T(8,128)(2,1)S(1)}, bf16[16,128]{1,0:T(8,128)(2,1)}, u32[]{:S(2)}) copy-start(bf16[16,128]{1,0:T(8,128)(2,1)} %param.10) | copy-start | bytes 12292
  0.6 7.8 %copy-start.1 = (bf16[16,128]{1,0:T(8,128)(2,1)S(1)}, bf16[16,128]{1,0:T(8,128)(2,1)}, u32[]{:S(2)}) copy-start(bf16[16,128]{1,0:T(8,128)(2,1)} %param.8) | copy-start | bytes 12292
  0.7 7.8 %copy-start.3 = (f32[16]{0:T(128)S(1)}, f32[16]{0:T(128)}, u32[]{:S(2)}) copy-start(f32[16]{0:T(128)} %param.11) | copy-start | bytes 196
  0.7 7.8 %copy-start.4 = (f32[16]{0:T(128)S(1)}, f32[16]{0:T(128)}, u32[]{:S(2)}) copy-start(f32[16]{0:T(128)} %param.9) | copy-start | bytes 196
  0.7 7.9 %copy-start.2 = (f32[16,128]{1,0:T(8,128)S(1)}, f32[16,128]{1,0:T(8,128)}, u32[]{:S(2)}) copy-start(f32[16,128]{1,0:T(8,128)} %param.7) | copy-start | bytes 24580
  0.7 24.2 %all-to-all-start = ((bf16[16,256,128]{2,1,0:T(8,128)(2,1)}), bf16[16,256,128]{2,1,0:T(8,128)(2,1)S(1)}, u32[]{:S(2)}, u32[]{:S(2)}) async-start(bf16[16,256,128]{2,1,0:T(8,128)(2,1)} %bitcast.45), calls=%async_computation | async-start | bytes 2097152 | tf_op jit(solution)/shard_map/all_to_all | solution.py:21
  8.5 2.9 %collective-permute-start = (f32[1,3,16,128]{3,2,1,0:T(8,128)S(1)}, f32[1,3,16,128]{3,2,1,0:T(8,128)S(1)}, u32[]{:S(2)}, u32[]{:S(2)}) collective-permute-start(f32[1,3,16,128]{3,2,1,0:T(8,128)S(1)} %get-tuple-element.19), channel_id=1, source_target_pairs={{0,2},{2,0},{4,6},{6,4},{8,10},{10,8},{12,14},{14,12},{1,3},{3,1},... | collective-permute-start | bytes 73736 | tf_op jit(solution)/shard_map/ppermute | solution.py:32
  11.5 4.8 %collective-permute-start.1 = (f32[2,3,16,128]{3,2,0,1:T(8,128)S(1)}, f32[2,3,16,128]{3,2,0,1:T(8,128)S(1)}, u32[]{:S(2)}, u32[]{:S(2)}) collective-permute-start(f32[2,3,16,128]{3,2,0,1:T(8,128)S(1)} %broadcast_select_fusion.2), channel_id=1, source_target_pairs={{0,4},{2,6},{4,0},{6,2},{8,12},{10,14},{12,8},{14,10},{1,5},{3,7},... | collective-permute-start | bytes 147464 | tf_op jit(solution)/shard_map/ppermute | solution.py:32
  16.4 8.3 %collective-permute-start.2 = (f32[4,3,16,128]{3,2,0,1:T(8,128)S(1)}, f32[4,3,16,128]{3,2,0,1:T(8,128)S(1)}, u32[]{:S(2)}, u32[]{:S(2)}) collective-permute-start(f32[4,3,16,128]{3,2,0,1:T(8,128)S(1)} %broadcast_select_fusion.1), channel_id=1, source_target_pairs={{0,8},{2,10},{4,12},{6,14},{8,0},{10,2},{12,4},{14,6},{1,9},{3,11}... | collective-permute-start | bytes 294920 | tf_op jit(solution)/shard_map/ppermute | solution.py:32
  25.1 4.8 %collective-permute-start.3 = (f32[8,16,128]{2,1,0:T(8,128)S(1)}, f32[8,16,128]{2,1,0:T(8,128)S(1)}, u32[]{:S(2)}, u32[]{:S(2)}) collective-permute-start(f32[8,16,128]{2,1,0:T(8,128)S(1)} %dynamic-slice_bitcast_fusion), channel_id=1, source_target_pairs={{0,1},{1,0},{2,3},{3,2},{4,5},{5,4},{6,7},{7,6},{8,9},{9,8},{10,11... | collective-permute-start | bytes 196616 | tf_op jit(solution)/shard_map/ppermute | solution.py:61
  54.7 15.8 %all-to-all-start.2 = ((f32[32,1,128]{2,1,0:T(1,128)}), f32[32,1,128]{2,1,0:T(1,128)S(1)}, u32[]{:S(2)}, u32[]{:S(2)}) async-start(f32[32,1,128]{2,1,0:T(1,128)} %broadcast_in_dim.143), calls=%async_computation.2 | async-start | bytes 32768 | tf_op jit(solution)/shard_map/all_to_all | solution.py:21
  72.8 14.3 %all-to-all-start.3 = ((bf16[16,128,128]{2,1,0:T(8,128)(2,1)}), bf16[16,128,128]{2,1,0:T(8,128)(2,1)S(1)}, u32[]{:S(2)}, u32[]{:S(2)}) async-start(bf16[16,128,128]{2,1,0:T(8,128)(2,1)} %broadcast_in_dim.144), calls=%async_computation.3 | async-start | bytes 1048576 | tf_op jit(solution)/shard_map/all_to_all | solution.py:21
  87.1 3.3 %collective-permute-start.4 = (bf16[16,8,1,16,128]{4,3,1,0,2:T(8,128)(2,1)S(1)}, bf16[16,8,1,16,128]{4,3,1,0,2:T(8,128)(2,1)S(1)}, u32[]{:S(2)}, u32[]{:S(2)}) collective-permute-start(bf16[16,8,1,16,128]{4,3,1,0,2:T(8,128)(2,1)S(1)} %bitcast.43), channel_id=1, source_target_pairs={{0,1},{1,0},{2,3},{3,2},{4,5},{5,4},{6,7},{7,6},{8,9},{9,8},{10,11... | collective-permute-start | bytes 1572872 | tf_op jit(solution)/shard_map/ppermute | solution.py:75
  88.8 3.0 %copy-start.5 = (f32[16]{0:T(128)}, f32[16]{0:T(128)S(1)}, u32[]{:S(2)}) copy-start(f32[16]{0:T(128)S(1)} %broadcast_add_fusion) | copy-start | bytes 196
  88.8 3.0 %copy-start.6 = (f32[16]{0:T(128)}, f32[16]{0:T(128)S(1)}, u32[]{:S(2)}) copy-start(f32[16]{0:T(128)S(1)} %broadcast_add_fusion.1) | copy-start | bytes 196

commit v3 on v2

--- a/solution.py
+++ b/solution.py
@@ -25,13 +25,29 @@
     return exchange(jnp.broadcast_to(x, (lax.axis_size(axes), *x.shape)), axes)
 
 
-def doubled(x, axis):
-    count = lax.axis_size(axis)
-    index = lax.axis_index(axis)
-    for level in range(count.bit_length() - 1):
-        other = lax.ppermute(x, axis, [(i, i ^ 1 << level) for i in range(count)])
-        mine = jnp.arange(2) == (index >> level & 1)
-        x = jnp.where(mine[:, None, None, None, None], x, other).reshape(-1, *x.shape[1:])
+def from_partner(x, axis, flip):
+    return lax.ppermute(x, axis, [(i, i ^ flip) for i in range(lax.axis_size(axis))])
+
+
+def flips(axis):
+    levels = lax.axis_size(axis).bit_length() - 1
+    return [(3 << level - 1 if level > 1 else 1 << level, level) for level in range(levels)]
+
+
+def summed(x, axis):
+    for flip, _ in flips(axis):
+        x = x + from_partner(x, axis, flip)
+    return x
+
+
+def gathered(x, axis):
+    x = x[None]
+    place = lax.axis_index(axis)[None]
+    for flip, level in reversed(flips(axis)):
+        other = from_partner(x, axis, flip)
+        mine = jnp.arange(2) == (place[:, None] >> level & 1)
+        place = jnp.where(mine, place[:, None], place[:, None] ^ flip).reshape(-1)
+        x = jnp.where(mine[:, :, None, None, None], x[:, None], other[:, None]).reshape(-1, *x.shape[1:])
     return x
 
 
@@ -48,19 +64,18 @@
     rows = master.shape[0]
     planes, line, cores = lax.axis_size(("y", "x")), lax.axis_size("z"), lax.axis_size("c")
     held = line * rows
-    swap = [(0, 1), (1, 0)]
     first = first_q.astype(jnp.float32) * first_scale[:, None]
     second = second_q.astype(jnp.float32) * second_scale[:, None]
 
     arrived = exchange(grads[0].reshape(planes, line * cores * rows, width), ("y", "x"))
-    states = doubled(jnp.stack([master, first, second])[None], "z")
+    states = gathered(jnp.stack([master, first, second]), "z")
     arrived, states = lax.optimization_barrier((arrived, states))
     both = arrived.astype(jnp.float32).sum(axis=0).reshape(line, cores, rows, width)
     core = lax.axis_index("c")
     kept, sent = (lax.dynamic_index_in_dim(both, i, 1, False) for i in (core, 1 - core))
-    part = (kept + lax.ppermute(sent, "c", swap)).reshape(held, width)
+    part = (kept + from_partner(sent, "c", 1)).reshape(held, width)
 
-    total = sent_to_all(part, "z").sum(axis=0)
+    total = summed(part, "z")
     line_master, line_first, line_second = (
         states[:, i].reshape(held, width) for i in range(3)
     )
@@ -72,7 +87,7 @@
     line_new, _, _ = advance(factor * total, line_master, line_first, line_second)
     weights = sent_to_all(line_new.astype(jnp.bfloat16), ("y", "x"))
     weights = weights.reshape(planes, line, 1, rows, width)
-    partner = lax.ppermute(weights, "c", swap)
+    partner = from_partner(weights, "c", 1)
     mine = jnp.arange(cores) == lax.axis_index("c")
     weights = jnp.where(mine[:, None, None], weights, partner).reshape(blocks, width)
 

time: 92.2 us -> 82.7 us (0.90)
  blocking collectives: 24 us -> 0 us
  waiting for transfers between devices: 23 us -> 30.9 us
  starting transfers between devices: 36.8 us -> 43.1 us
    all_to_all x1 -> x0, blocking collectives: 24 us -> none  [exchange(): return lax.all_to_all(x, axes, split_axis=0, concat_axis=0, tiled=True)]
    ppermute x5 -> x8, waiting for transfers between devices: 6.55 us -> 14.1 us  [from_partner(): lax.ppermute(x, axis, [(i, i ^ flip) for i in range(lax.axis_size(axis))])]
    ppermute x5 -> x8, starting transfers between devices: 16.6 us -> 21.9 us  [from_partner(): lax.ppermute(x, axis, [(i, i ^ flip) for i in range(lax.axis_size(axis))])]
    all_to_all x3, starting transfers between devices: 20.2 us -> 21.2 us  [exchange(): return lax.all_to_all(x, axes, split_axis=0, concat_axis=0, tiled=True)]
  transfers between devices with their start and end apart: 8 -> 11, of which waited for: 7 -> 11; matrix products, arithmetic and copies ran while one was open for 3% -> 3% of each run, Pallas kernels for 0% -> 0%
where the time goes in v3:
time: 82.7 us; the launch traced here: 82.3 us
  starting transfers between devices  43.1 us (52%)
  waiting for transfers between devices  30.9 us (37%)
  other arithmetic  4.36 us (5%)
  local copies, waits for them, and re-layouts  2.32 us (3%)
  between operations  1.56 us (2%)
    ppermute x8, starting transfers between devices, from_partner(): lax.ppermute(x, axis, [(i, i ^ flip) for i in range(lax.axis_size(axis))])  21.9 us
    all_to_all x3, starting transfers between devices, exchange(): return lax.all_to_all(x, axes, split_axis=0, concat_axis=0, tiled=True)  21.2 us
    all_to_all x3, waiting for transfers between devices, exchange(): return lax.all_to_all(x, axes, split_axis=0, concat_axis=0, tiled=True)  16.8 us
    ppermute x8, waiting for transfers between devices, from_partner(): lax.ppermute(x, axis, [(i, i ^ flip) for i in range(lax.axis_size(axis))])  14.1 us
  transfers between devices with their start and end apart: 11, of which 11 were waited for; matrix products, arithmetic and copies ran while one was open for 3% of the time, Pallas kernels for 0%

profile of v3, /device:TPU:1, one launch (start us, length us, event | category | flops | bytes accessed | tf_op | source)
XLA Modules:
  0.0 82.3 jit_solution(16829588535526467406)
XLA Ops:
  0.7 7.7 %all-to-all-start = ((bf16[16,256,128]{2,1,0:T(8,128)(2,1)}), bf16[16,256,128]{2,1,0:T(8,128)(2,1)S(1)}, u32[]{:S(2)}, u32[]{:S(2)}) async-start(bf16[16,256,128]{2,1,0:T(8,128)(2,1)} %bitcast.46), calls=%async_computation | async-start | bytes 2097152 | tf_op jit(solution)/shard_map/all_to_all | solution.py:21
  8.4 0.0 copy-done
  8.4 0.0 copy-done.1
  8.4 0.0 copy-done.3
  8.4 0.0 copy-done.4
  8.4 0.1 fusion.10
  8.5 6.1 %collective-permute-start = (f32[1,3,16,128]{3,2,1,0:T(8,128)S(1)}, f32[1,3,16,128]{3,2,1,0:T(8,128)S(1)}, u32[]{:S(2)}, u32[]{:S(2)}) collective-permute-start(f32[1,3,16,128]{3,2,1,0:T(8,128)S(1)} %get-tuple-element.23), channel_id=1, source_target_pairs={{0,12},{2,14},{4,8},{6,10},{8,4},{10,6},{12,0},{14,2},{1,13},{3,15... | collective-permute-start | bytes 73736 | tf_op jit(solution)/shard_map/ppermute | solution.py:29
  14.7 0.1 iota_compare_fusion.1
  14.7 0.1 broadcast_in_dim.185
  14.8 0.1 broadcast_in_dim.186
  14.9 0.1 eq.86
  15.0 0.1 broadcast_in_dim.183
  15.0 0.1 broadcast_in_dim.184
  15.1 1.0 %collective-permute-done = f32[1,3,16,128]{3,2,1,0:T(8,128)S(1)} collective-permute-done((f32[1,3,16,128]{3,2,1,0:T(8,128)S(1)}, f32[1,3,16,128]{3,2,1,0:T(8,128)S(1)}, u32[]{:S(2)}, u32[]{:S(2)}) %collective-permute-start) | collective-permute-done | bytes 24608 | tf_op jit(solution)/shard_map/ppermute | solution.py:29
  16.2 0.1 broadcast_select_fusion.2
  16.2 0.9 %collective-permute-start.1 = (f32[2,3,16,128]{3,2,0,1:T(8,128)S(1)}, f32[2,3,16,128]{3,2,0,1:T(8,128)S(1)}, u32[]{:S(2)}, u32[]{:S(2)}) collective-permute-start(f32[2,3,16,128]{3,2,0,1:T(8,128)S(1)} %broadcast_select_fusion.2), channel_id=1, source_target_pairs={{0,4},{2,6},{4,0},{6,2},{8,12},{10,14},{12,8},{14,10},{1,5},{3,7},... | collective-permute-start | bytes 147464 | tf_op jit(solution)/shard_map/ppermute | solution.py:29
  17.1 3.3 %collective-permute-done.1 = f32[2,3,16,128]{3,2,0,1:T(8,128)S(1)} collective-permute-done((f32[2,3,16,128]{3,2,0,1:T(8,128)S(1)}, f32[2,3,16,128]{3,2,0,1:T(8,128)S(1)}, u32[]{:S(2)}, u32[]{:S(2)}) %collective-permute-start.1) | collective-permute-done | bytes 49184 | tf_op jit(solution)/shard_map/ppermute | solution.py:29
  20.4 0.1 broadcast_select_fusion.1
  20.5 0.8 collective-permute-start.2
  21.3 0.1 iota_compare_fusion
  21.3 0.1 eq.89
  21.4 2.6 %collective-permute-done.2 = f32[4,3,16,128]{3,2,0,1:T(8,128)S(1)} collective-permute-done((f32[4,3,16,128]{3,2,0,1:T(8,128)S(1)}, f32[4,3,16,128]{3,2,0,1:T(8,128)S(1)}, u32[]{:S(2)}, u32[]{:S(2)}) %collective-permute-start.2) | collective-permute-done | bytes 98336 | tf_op jit(solution)/shard_map/ppermute | solution.py:29
  24.1 0.1 broadcast_select_fusion
  24.1 0.3 all-to-all-done
  24.4 0.1 convert_reduce_fusion
  24.6 3.3 %collective-permute-start.3 = (f32[8,16,128]{2,1,0:T(8,128)S(1)}, f32[8,16,128]{2,1,0:T(8,128)S(1)}, u32[]{:S(2)}, u32[]{:S(2)}) collective-permute-start(f32[8,16,128]{2,1,0:T(8,128)S(1)} %dynamic-slice_bitcast_fusion), channel_id=1, source_target_pairs={{0,1},{1,0},{2,3},{3,2},{4,5},{5,4},{6,7},{7,6},{8,9},{9,8},{10,11... | collective-permute-start | bytes 196616 | tf_op jit(solution)/shard_map/ppermute | solution.py:29
  27.9 0.9 %collective-permute-done.3 = f32[8,16,128]{2,1,0:T(8,128)S(1)} collective-permute-done((f32[8,16,128]{2,1,0:T(8,128)S(1)}, f32[8,16,128]{2,1,0:T(8,128)S(1)}, u32[]{:S(2)}, u32[]{:S(2)}) %collective-permute-start.3) | collective-permute-done | bytes 65568 | tf_op jit(solution)/shard_map/ppermute | solution.py:29
  28.9 1.1 %collective-permute-start.4 = (f32[128,128]{1,0:T(8,128)S(1)}, f32[128,128]{1,0:T(8,128)S(1)}, u32[]{:S(2)}, u32[]{:S(2)}) collective-permute-start(f32[128,128]{1,0:T(8,128)S(1)} %bitcast.54), channel_id=1, source_target_pairs={{0,2},{2,0},{4,6},{6,4},{8,10},{10,8},{12,14},{14,12},{1,3},{3,1},... | collective-permute-start | bytes 196616 | tf_op jit(solution)/shard_map/ppermute | solution.py:29
  29.9 2.1 %collective-permute-done.4 = f32[128,128]{1,0:T(8,128)S(1)} collective-permute-done((f32[128,128]{1,0:T(8,128)S(1)}, f32[128,128]{1,0:T(8,128)S(1)}, u32[]{:S(2)}, u32[]{:S(2)}) %collective-permute-start.4) | collective-permute-done | bytes 65568 | tf_op jit(solution)/shard_map/ppermute | solution.py:29
  32.1 3.0 %collective-permute-start.5 = (f32[128,128]{1,0:T(8,128)S(1)}, f32[128,128]{1,0:T(8,128)S(1)}, u32[]{:S(2)}, u32[]{:S(2)}) collective-permute-start(f32[128,128]{1,0:T(8,128)S(1)} %bitcast_add_fusion.2), channel_id=1, source_target_pairs={{0,4},{2,6},{4,0},{6,2},{8,12},{10,14},{12,8},{14,10},{1,5},{3,7},... | collective-permute-start | bytes 196616 | tf_op jit(solution)/shard_map/ppermute | solution.py:29
  35.0 1.7 %collective-permute-done.5 = f32[128,128]{1,0:T(8,128)S(1)} collective-permute-done((f32[128,128]{1,0:T(8,128)S(1)}, f32[128,128]{1,0:T(8,128)S(1)}, u32[]{:S(2)}, u32[]{:S(2)}) %collective-permute-start.5) | collective-permute-done | bytes 65568 | tf_op jit(solution)/shard_map/ppermute | solution.py:29
  36.7 5.0 %collective-permute-start.6 = (f32[128,128]{1,0:T(8,128)S(1)}, f32[128,128]{1,0:T(8,128)S(1)}, u32[]{:S(2)}, u32[]{:S(2)}) collective-permute-start(f32[128,128]{1,0:T(8,128)S(1)} %add.68), channel_id=1, source_target_pairs={{0,12},{2,14},{4,8},{6,10},{8,4},{10,6},{12,0},{14,2},{1,13},{3,15... | collective-permute-start | bytes 196616 | tf_op jit(solution)/shard_map/ppermute | solution.py:29
  41.7 1.7 %collective-permute-done.6 = f32[128,128]{1,0:T(8,128)S(1)} collective-permute-done((f32[128,128]{1,0:T(8,128)S(1)}, f32[128,128]{1,0:T(8,128)S(1)}, u32[]{:S(2)}, u32[]{:S(2)}) %collective-permute-start.6) | collective-permute-done | bytes 65568 | tf_op jit(solution)/shard_map/ppermute | solution.py:29
  43.5 0.6 broadcast_in_dim.202
  44.1 9.9 %all-to-all-start.1 = ((f32[32,1,128]{2,1,0:T(1,128)}), f32[32,1,128]{2,1,0:T(1,128)S(1)}, u32[]{:S(2)}, u32[]{:S(2)}) async-start(f32[32,1,128]{2,1,0:T(1,128)} %broadcast_in_dim.202), calls=%async_computation.1 | async-start | bytes 32768 | tf_op jit(solution)/shard_map/all_to_all | solution.py:21
  54.1 6.9 %all-to-all-done.1 = f32[32,1,128]{2,1,0:T(1,128)S(1)} async-done(((f32[32,1,128]{2,1,0:T(1,128)}), f32[32,1,128]{2,1,0:T(1,128)S(1)}, u32[]{:S(2)}, u32[]{:S(2)}) %all-to-all-start.1) | async-done | bytes 16416 | tf_op jit(solution)/shard_map/all_to_all | solution.py:21
  60.9 0.6 reduce_sum.29
  62.3 0.1 fusion.8
  62.3 0.9 %broadcast_in_dim.203 = bf16[16,128,128]{2,1,0:T(8,128)(2,1)} broadcast(bf16[128,128]{1,0:T(8,128)(2,1)S(1)} %fusion.8), dimensions={1,2} | broadcast | bytes 557056 | tf_op jit(solution)/shard_map/broadcast_in_dim | solution.py:25
  63.2 3.6 %all-to-all-start.2 = ((bf16[16,128,128]{2,1,0:T(8,128)(2,1)}), bf16[16,128,128]{2,1,0:T(8,128)(2,1)S(1)}, u32[]{:S(2)}, u32[]{:S(2)}) async-start(bf16[16,128,128]{2,1,0:T(8,128)(2,1)} %broadcast_in_dim.203), calls=%async_computation.2 | async-start | bytes 1048576 | tf_op jit(solution)/shard_map/all_to_all | solution.py:21
  66.8 0.1 broadcast_in_dim.178
  66.9 0.1 broadcast_in_dim.179
  67.1 0.8 abs_reduce_fusion
  67.9 9.6 %all-to-all-done.2 = bf16[16,128,128]{2,1,0:T(8,128)(2,1)S(1)} async-done(((bf16[16,128,128]{2,1,0:T(8,128)(2,1)}), bf16[16,128,128]{2,1,0:T(8,128)(2,1)S(1)}, u32[]{:S(2)}, u32[]{:S(2)}) %all-to-all-start.2) | async-done | bytes 524320 | tf_op jit(solution)/shard_map/all_to_all | solution.py:21
  77.5 1.8 %collective-permute-start.7 = (bf16[16,8,1,16,128]{4,3,1,0,2:T(8,128)(2,1)S(1)}, bf16[16,8,1,16,128]{4,3,1,0,2:T(8,128)(2,1)S(1)}, u32[]{:S(2)}, u32[]{:S(2)}) collective-permute-start(bf16[16,8,1,16,128]{4,3,1,0,2:T(8,128)(2,1)S(1)} %bitcast.44), channel_id=1, source_target_pairs={{0,1},{1,0},{2,3},{3,2},{4,5},{5,4},{6,7},{7,6},{8,9},{9,8},{10,11... | collective-permute-start | bytes 1572872 | tf_op jit(solution)/shard_map/ppermute | solution.py:29
  79.3 0.7 divide_convert_fusion
  80.0 0.8 %collective-permute-done.7 = bf16[16,8,1,16,128]{4,3,1,0,2:T(8,128)(2,1)S(1)} collective-permute-done((bf16[16,8,1,16,128]{4,3,1,0,2:T(8,128)(2,1)S(1)}, bf16[16,8,1,16,128]{4,3,1,0,2:T(8,128)(2,1)S(1)}, u32[]{:S(2)}, u32[]{:S(2)}) %collective-permute-start.7) | collective-permute-done | bytes 524320 | tf_op jit(solution)/shard_map/ppermute | solution.py:29
  80.8 1.5 %bitcast_select_fusion = bf16[4096,128]{1,0:T(8,128)(2,1)} fusion(pred[4096]{0:T(1024)(128)(4,1)S(1)} %broadcast_in_dim.179, bf16[16,8,16,128]{3,2,1,0:T(8,128)(2,1)S(1)} %bitcast.51, bf16[16,8,16,128]{3,2,1,0:T(8,128)(2,1)S(1)} %bitcast.45), kind=kLoop, calls=%fused_computation.1 | loop fusion | flops 524288 | bytes 2101248 | tf_op jit(solution)/shard_map/jit(_where)/select_n | solution.py:92
  (28 shorter events, 0.2 us)
Async XLA Ops:
  0.6 7.8 %copy-start = (bf16[16,128]{1,0:T(8,128)(2,1)S(1)}, bf16[16,128]{1,0:T(8,128)(2,1)}, u32[]{:S(2)}) copy-start(bf16[16,128]{1,0:T(8,128)(2,1)} %param.10) | copy-start | bytes 12292
  0.6 7.8 %copy-start.1 = (bf16[16,128]{1,0:T(8,128)(2,1)S(1)}, bf16[16,128]{1,0:T(8,128)(2,1)}, u32[]{:S(2)}) copy-start(bf16[16,128]{1,0:T(8,128)(2,1)} %param.8) | copy-start | bytes 12292
  0.7 7.8 %copy-start.3 = (f32[16]{0:T(128)S(1)}, f32[16]{0:T(128)}, u32[]{:S(2)}) copy-start(f32[16]{0:T(128)} %param.11) | copy-start | bytes 196
  0.7 7.8 %copy-start.4 = (f32[16]{0:T(128)S(1)}, f32[16]{0:T(128)}, u32[]{:S(2)}) copy-start(f32[16]{0:T(128)} %param.9) | copy-start | bytes 196
  0.7 7.9 %copy-start.2 = (f32[16,128]{1,0:T(8,128)S(1)}, f32[16,128]{1,0:T(8,128)}, u32[]{:S(2)}) copy-start(f32[16,128]{1,0:T(8,128)} %param.7) | copy-start | bytes 24580
  0.7 23.8 %all-to-all-start = ((bf16[16,256,128]{2,1,0:T(8,128)(2,1)}), bf16[16,256,128]{2,1,0:T(8,128)(2,1)S(1)}, u32[]{:S(2)}, u32[]{:S(2)}) async-start(bf16[16,256,128]{2,1,0:T(8,128)(2,1)} %bitcast.46), calls=%async_computation | async-start | bytes 2097152 | tf_op jit(solution)/shard_map/all_to_all | solution.py:21
  8.5 7.6 %collective-permute-start = (f32[1,3,16,128]{3,2,1,0:T(8,128)S(1)}, f32[1,3,16,128]{3,2,1,0:T(8,128)S(1)}, u32[]{:S(2)}, u32[]{:S(2)}) collective-permute-start(f32[1,3,16,128]{3,2,1,0:T(8,128)S(1)} %get-tuple-element.23), channel_id=1, source_target_pairs={{0,12},{2,14},{4,8},{6,10},{8,4},{10,6},{12,0},{14,2},{1,13},{3,15... | collective-permute-start | bytes 73736 | tf_op jit(solution)/shard_map/ppermute | solution.py:29
  16.2 4.2 %collective-permute-start.1 = (f32[2,3,16,128]{3,2,0,1:T(8,128)S(1)}, f32[2,3,16,128]{3,2,0,1:T(8,128)S(1)}, u32[]{:S(2)}, u32[]{:S(2)}) collective-permute-start(f32[2,3,16,128]{3,2,0,1:T(8,128)S(1)} %broadcast_select_fusion.2), channel_id=1, source_target_pairs={{0,4},{2,6},{4,0},{6,2},{8,12},{10,14},{12,8},{14,10},{1,5},{3,7},... | collective-permute-start | bytes 147464 | tf_op jit(solution)/shard_map/ppermute | solution.py:29
  20.5 3.5 %collective-permute-start.2 = (f32[4,3,16,128]{3,2,0,1:T(8,128)S(1)}, f32[4,3,16,128]{3,2,0,1:T(8,128)S(1)}, u32[]{:S(2)}, u32[]{:S(2)}) collective-permute-start(f32[4,3,16,128]{3,2,0,1:T(8,128)S(1)} %broadcast_select_fusion.1), channel_id=1, source_target_pairs={{0,2},{2,0},{4,6},{6,4},{8,10},{10,8},{12,14},{14,12},{1,3},{3,1},... | collective-permute-start | bytes 294920 | tf_op jit(solution)/shard_map/ppermute | solution.py:29
  24.6 4.2 %collective-permute-start.3 = (f32[8,16,128]{2,1,0:T(8,128)S(1)}, f32[8,16,128]{2,1,0:T(8,128)S(1)}, u32[]{:S(2)}, u32[]{:S(2)}) collective-permute-start(f32[8,16,128]{2,1,0:T(8,128)S(1)} %dynamic-slice_bitcast_fusion), channel_id=1, source_target_pairs={{0,1},{1,0},{2,3},{3,2},{4,5},{5,4},{6,7},{7,6},{8,9},{9,8},{10,11... | collective-permute-start | bytes 196616 | tf_op jit(solution)/shard_map/ppermute | solution.py:29
  28.9 3.2 %collective-permute-start.4 = (f32[128,128]{1,0:T(8,128)S(1)}, f32[128,128]{1,0:T(8,128)S(1)}, u32[]{:S(2)}, u32[]{:S(2)}) collective-permute-start(f32[128,128]{1,0:T(8,128)S(1)} %bitcast.54), channel_id=1, source_target_pairs={{0,2},{2,0},{4,6},{6,4},{8,10},{10,8},{12,14},{14,12},{1,3},{3,1},... | collective-permute-start | bytes 196616 | tf_op jit(solution)/shard_map/ppermute | solution.py:29
  32.1 4.6 %collective-permute-start.5 = (f32[128,128]{1,0:T(8,128)S(1)}, f32[128,128]{1,0:T(8,128)S(1)}, u32[]{:S(2)}, u32[]{:S(2)}) collective-permute-start(f32[128,128]{1,0:T(8,128)S(1)} %bitcast_add_fusion.2), channel_id=1, source_target_pairs={{0,4},{2,6},{4,0},{6,2},{8,12},{10,14},{12,8},{14,10},{1,5},{3,7},... | collective-permute-start | bytes 196616 | tf_op jit(solution)/shard_map/ppermute | solution.py:29
  36.7 6.8 %collective-permute-start.6 = (f32[128,128]{1,0:T(8,128)S(1)}, f32[128,128]{1,0:T(8,128)S(1)}, u32[]{:S(2)}, u32[]{:S(2)}) collective-permute-start(f32[128,128]{1,0:T(8,128)S(1)} %add.68), channel_id=1, source_target_pairs={{0,12},{2,14},{4,8},{6,10},{8,4},{10,6},{12,0},{14,2},{1,13},{3,15... | collective-permute-start | bytes 196616 | tf_op jit(solution)/shard_map/ppermute | solution.py:29
  44.1 16.8 %all-to-all-start.1 = ((f32[32,1,128]{2,1,0:T(1,128)}), f32[32,1,128]{2,1,0:T(1,128)S(1)}, u32[]{:S(2)}, u32[]{:S(2)}) async-start(f32[32,1,128]{2,1,0:T(1,128)} %broadcast_in_dim.202), calls=%async_computation.1 | async-start | bytes 32768 | tf_op jit(solution)/shard_map/all_to_all | solution.py:21
  63.2 14.3 %all-to-all-start.2 = ((bf16[16,128,128]{2,1,0:T(8,128)(2,1)}), bf16[16,128,128]{2,1,0:T(8,128)(2,1)S(1)}, u32[]{:S(2)}, u32[]{:S(2)}) async-start(bf16[16,128,128]{2,1,0:T(8,128)(2,1)} %broadcast_in_dim.203), calls=%async_computation.2 | async-start | bytes 1048576 | tf_op jit(solution)/shard_map/all_to_all | solution.py:21
  77.5 3.3 %collective-permute-start.7 = (bf16[16,8,1,16,128]{4,3,1,0,2:T(8,128)(2,1)S(1)}, bf16[16,8,1,16,128]{4,3,1,0,2:T(8,128)(2,1)S(1)}, u32[]{:S(2)}, u32[]{:S(2)}) collective-permute-start(bf16[16,8,1,16,128]{4,3,1,0,2:T(8,128)(2,1)S(1)} %bitcast.44), channel_id=1, source_target_pairs={{0,1},{1,0},{2,3},{3,2},{4,5},{5,4},{6,7},{7,6},{8,9},{9,8},{10,11... | collective-permute-start | bytes 1572872 | tf_op jit(solution)/shard_map/ppermute | solution.py:29
  79.3 3.0 %copy-start.5 = (f32[16]{0:T(128)}, f32[16]{0:T(128)S(1)}, u32[]{:S(2)}) copy-start(f32[16]{0:T(128)S(1)} %broadcast_add_fusion) | copy-start | bytes 196
  79.3 3.0 %copy-start.6 = (f32[16]{0:T(128)}, f32[16]{0:T(128)S(1)}, u32[]{:S(2)}) copy-start(f32[16]{0:T(128)S(1)} %broadcast_add_fusion.1) | copy-start | bytes 196

commit v4 on v1

--- a/solution.py
+++ b/solution.py
@@ -25,6 +25,34 @@
     return exchange(jnp.broadcast_to(x, (lax.axis_size(axes), *x.shape)), axes)
 
 
+def swapped(x):
+    return lax.ppermute(x, "c", [(0, 1), (1, 0)])
+
+
+def from_partner(x, flip):
+    line = lax.axis_size("z")
+    route = [(2 * z + c, 2 * (z ^ flip) + 1 - c) for z in range(line) for c in range(2)]
+    return lax.ppermute(x, ("z", "c"), route)
+
+
+FLIPS = ((1, 0), (2, 1), (6, 2))
+
+
+def summed(x):
+    for flip, _ in FLIPS:
+        x = x + from_partner(x, flip)
+    return x
+
+
+def doubled(x, place, step):
+    flip, level = step
+    other = from_partner(x, flip)
+    mine = jnp.arange(2) == (place[:, None] >> level & 1)
+    place = jnp.where(mine, place[:, None], place[:, None] ^ flip).reshape(-1)
+    x = jnp.where(mine[:, :, None, None, None], x[:, None], other[:, None])
+    return x.reshape(-1, *x.shape[2:]), place
+
+
 def advance(clipped, master, first, second):
     first_new = beta_one * first + (1.0 - beta_one) * clipped
     second_new = beta_two * second + (1.0 - beta_two) * clipped * clipped
@@ -41,30 +69,41 @@
     first = first_q.astype(jnp.float32) * first_scale[:, None]
     second = second_q.astype(jnp.float32) * second_scale[:, None]
 
-    local = grads[0].reshape(planes, line, cores, rows, width).swapaxes(1, 2)
-    arrived = exchange(local.reshape(planes * cores, held, width), ("y", "x", "c"))
-    part = arrived.astype(jnp.float32).sum(axis=0)
+    z, core = lax.axis_index("z"), lax.axis_index("c")
+    odd = (z ^ z >> 1) & 1
+    here = core ^ odd
 
-    packed = jnp.concatenate([part, master, first, second], axis=0)
-    shared = sent_to_all(packed, "z")
-    total = shared[:, :held].sum(axis=0)
-    states = shared[:, held:].reshape(line, 3, rows, width)
+    arrived = exchange(grads[0].reshape(planes, line * cores * rows, width), ("y", "x"))
+    states = jnp.stack([master, first, second])
+    states = jnp.where(odd == 1, swapped(states), states)[None]
+    place = z[None]
+    for step in FLIPS[:0:-1]:
+        states, place = doubled(states, place, step)
+    arrived, states = lax.optimization_barrier((arrived, states))
+    both = arrived.astype(jnp.float32).sum(axis=0).reshape(line, cores, rows, width)
+    kept, sent = (lax.dynamic_index_in_dim(both, i, 1, False) for i in (here, 1 - here))
+    part = (kept + swapped(sent)).reshape(held, width)
+
+    total = summed(part)
+    total, states = lax.optimization_barrier((total, states))
+    norms = sent_to_all(jnp.sum(total * total, axis=0, keepdims=True), ("y", "x", "c"))
+    norms = norms.reshape(planes, cores, width)
+    norms = norms[:, 0] + norms[:, 1]
+    states, _ = doubled(states, place, FLIPS[0])
     line_master, line_first, line_second = (
         states[:, i].reshape(held, width) for i in range(3)
     )
-
-    squares = sent_to_all(jnp.sum(total * total, axis=0, keepdims=True), ("y", "x", "c")).sum()
     limit = clip_rms * jnp.sqrt(jnp.float32(blocks * width))
-    factor = jnp.minimum(1.0, limit / (jnp.sqrt(squares) + 1e-06))
+    factor = jnp.minimum(1.0, limit / (jnp.sqrt(norms.sum()) + 1e-06))
 
     line_new, _, _ = advance(factor * total, line_master, line_first, line_second)
     weights = sent_to_all(line_new.astype(jnp.bfloat16), ("y", "x"))
     weights = weights.reshape(planes, line, 1, rows, width)
-    partner = lax.ppermute(weights, "c", [(0, 1), (1, 0)])
-    mine = jnp.arange(cores) == lax.axis_index("c")
-    weights = jnp.where(mine[:, None, None], weights, partner).reshape(blocks, width)
+    mine = jnp.arange(cores) == here
+    weights = jnp.where(mine[:, None, None], weights, swapped(weights)).reshape(blocks, width)
 
-    own = lax.dynamic_slice_in_dim(total, lax.axis_index("z") * rows, rows, 0)
+    own = lax.dynamic_slice_in_dim(total, z * rows, rows, 0)
+    own = jnp.where(odd == 1, swapped(own), own)
     master_new, first_new, second_new = advance(factor * own, master, first, second)
     first_scale_new = jnp.max(jnp.abs(first_new), axis=1) + 1e-08
     second_scale_new = jnp.max(jnp.abs(second_new), axis=1) + 1e-08

time: 92.8 us -> 80.4 us (0.87)
  blocking collectives: 28.8 us -> 0 us
  starting transfers between devices: 19.6 us -> 43.6 us
  waiting for transfers between devices: 34.2 us -> 28.7 us
  local copies, waits for them, and re-layouts: 4.3 us -> 2.33 us
    all_to_all x1 -> x0, blocking collectives: 28.8 us -> none  [exchange(): return lax.all_to_all(x, axes, split_axis=0, concat_axis=0, tiled=True)]
    ppermute x1 -> x10, starting transfers between devices: 1.76 us -> 27.6 us  [the longest x6 21.7 us: from_partner(): return lax.ppermute(x, ('z', 'c'), route)]
    all_to_all x3, waiting for transfers between devices: 33.4 us -> 13.3 us  [exchange(): return lax.all_to_all(x, axes, split_axis=0, concat_axis=0, tiled=True)]
    ppermute x1 -> x10, waiting for transfers between devices: 0.84 us -> 15.4 us  [the longest x6 12.2 us: from_partner(): return lax.ppermute(x, ('z', 'c'), route)]
    transpose x1 -> x0, local copies, waits for them, and re-layouts: 2.45 us -> none  [shards(): local = grads[0].reshape(planes, line, cores, rows, width).swapaxes(1, 2)]
    all_to_all x3, starting transfers between devices: 17.8 us -> 16 us  [exchange(): return lax.all_to_all(x, axes, split_axis=0, concat_axis=0, tiled=True)]
  transfers between devices with their start and end apart: 4 -> 13, of which waited for: 4 -> 12; matrix products, arithmetic and copies ran while one was open for 2% -> 3% of each run, Pallas kernels for 0% -> 0%
where the time goes in v4:
time: 80.4 us; the launch traced here: 80 us
  starting transfers between devices  43.6 us (54%)
  waiting for transfers between devices  28.7 us (36%)
  other arithmetic  3.76 us (5%)
  local copies, waits for them, and re-layouts  2.33 us (3%)
  between operations  1.59 us (2%)
    ppermute x6, starting transfers between devices, from_partner(): return lax.ppermute(x, ('z', 'c'), route)  21.7 us
    all_to_all x3, starting transfers between devices, exchange(): return lax.all_to_all(x, axes, split_axis=0, concat_axis=0, tiled=True)  16 us
    all_to_all x3, waiting for transfers between devices, exchange(): return lax.all_to_all(x, axes, split_axis=0, concat_axis=0, tiled=True)  13.3 us
    ppermute x6, waiting for transfers between devices, from_partner(): return lax.ppermute(x, ('z', 'c'), route)  12.2 us
    ppermute x4, starting transfers between devices, swapped(): return lax.ppermute(x, 'c', [(0, 1), (1, 0)])  5.94 us
    ppermute x4, waiting for transfers between devices, swapped(): return lax.ppermute(x, 'c', [(0, 1), (1, 0)])  3.15 us
  transfers between devices with their start and end apart: 13, of which 12 were waited for; matrix products, arithmetic and copies ran while one was open for 3% of the time, Pallas kernels for 0%

profile of v4, /device:TPU:1, one launch (start us, length us, event | category | flops | bytes accessed | tf_op | source)
XLA Modules:
  0.0 80.0 jit_solution(5080118110207355902)
XLA Ops:
  0.7 7.7 %all-to-all-start = ((bf16[16,256,128]{2,1,0:T(8,128)(2,1)}), bf16[16,256,128]{2,1,0:T(8,128)(2,1)S(1)}, u32[]{:S(2)}, u32[]{:S(2)}) async-start(bf16[16,256,128]{2,1,0:T(8,128)(2,1)} %bitcast.47), calls=%async_computation | async-start | bytes 2097152 | tf_op jit(solution)/shard_map/all_to_all | solution.py:21
  8.4 0.1 fusion.10
  8.5 1.0 %collective-permute-start = (f32[3,16,128]{2,1,0:T(8,128)S(1)}, f32[3,16,128]{2,1,0:T(8,128)S(1)}, u32[]{:S(2)}, u32[]{:S(2)}) collective-permute-start(f32[3,16,128]{2,1,0:T(8,128)S(1)} %pad_maximum_fusion), channel_id=1, source_target_pairs={{0,1},{1,0},{2,3},{3,2},{4,5},{5,4},{6,7},{7,6},{8,9},{9,8},{10,11... | collective-permute-start | bytes 73736 | tf_op jit(solution)/shard_map/ppermute | solution.py:29
  9.6 0.8 %collective-permute-done = f32[3,16,128]{2,1,0:T(8,128)S(1)} collective-permute-done((f32[3,16,128]{2,1,0:T(8,128)S(1)}, f32[3,16,128]{2,1,0:T(8,128)S(1)}, u32[]{:S(2)}, u32[]{:S(2)}) %collective-permute-start) | collective-permute-done | bytes 24608 | tf_op jit(solution)/shard_map/ppermute | solution.py:29
  10.4 6.3 %collective-permute-start.1 = (f32[1,3,16,128]{3,2,1,0:T(8,128)S(1)}, f32[1,3,16,128]{3,2,1,0:T(8,128)S(1)}, u32[]{:S(2)}, u32[]{:S(2)}) collective-permute-start(f32[1,3,16,128]{3,2,1,0:T(8,128)S(1)} %fusion.13), channel_id=1, source_target_pairs={{0,13},{1,12},{2,15},{3,14},{4,9},{5,8},{6,11},{7,10},{8,5},{9,4},... | collective-permute-start | bytes 73736 | tf_op jit(solution)/shard_map/ppermute | solution.py:35
  16.7 1.8 %collective-permute-done.1 = f32[1,3,16,128]{3,2,1,0:T(8,128)S(1)} collective-permute-done((f32[1,3,16,128]{3,2,1,0:T(8,128)S(1)}, f32[1,3,16,128]{3,2,1,0:T(8,128)S(1)}, u32[]{:S(2)}, u32[]{:S(2)}) %collective-permute-start.1) | collective-permute-done | bytes 24608 | tf_op jit(solution)/shard_map/ppermute | solution.py:35
  18.5 0.1 broadcast_select_fusion.2
  18.5 1.0 %collective-permute-start.2 = (f32[2,3,16,128]{3,2,0,1:T(8,128)S(1)}, f32[2,3,16,128]{3,2,0,1:T(8,128)S(1)}, u32[]{:S(2)}, u32[]{:S(2)}) collective-permute-start(f32[2,3,16,128]{3,2,0,1:T(8,128)S(1)} %broadcast_select_fusion.2), channel_id=1, source_target_pairs={{0,5},{1,4},{2,7},{3,6},{4,1},{5,0},{6,3},{7,2},{8,13},{9,12},{10,... | collective-permute-start | bytes 147464 | tf_op jit(solution)/shard_map/ppermute | solution.py:35
  19.5 0.1 iota_compare_fusion.1
  19.6 0.1 eq.90
  19.7 4.1 %collective-permute-done.2 = f32[2,3,16,128]{3,2,0,1:T(8,128)S(1)} collective-permute-done((f32[2,3,16,128]{3,2,0,1:T(8,128)S(1)}, f32[2,3,16,128]{3,2,0,1:T(8,128)S(1)}, u32[]{:S(2)}, u32[]{:S(2)}) %collective-permute-start.2) | collective-permute-done | bytes 49184 | tf_op jit(solution)/shard_map/ppermute | solution.py:35
  23.8 0.1 broadcast_select_fusion.1
  23.9 0.6 all-to-all-done
  24.4 0.1 convert_reduce_fusion
  24.6 2.7 %collective-permute-start.3 = (f32[8,16,128]{2,1,0:T(8,128)S(1)}, f32[8,16,128]{2,1,0:T(8,128)S(1)}, u32[]{:S(2)}, u32[]{:S(2)}) collective-permute-start(f32[8,16,128]{2,1,0:T(8,128)S(1)} %dynamic-slice_bitcast_fusion), channel_id=1, source_target_pairs={{0,1},{1,0},{2,3},{3,2},{4,5},{5,4},{6,7},{7,6},{8,9},{9,8},{10,11... | collective-permute-start | bytes 196616 | tf_op jit(solution)/shard_map/ppermute | solution.py:29
  27.3 0.9 %collective-permute-done.3 = f32[8,16,128]{2,1,0:T(8,128)S(1)} collective-permute-done((f32[8,16,128]{2,1,0:T(8,128)S(1)}, f32[8,16,128]{2,1,0:T(8,128)S(1)}, u32[]{:S(2)}, u32[]{:S(2)}) %collective-permute-start.3) | collective-permute-done | bytes 65568 | tf_op jit(solution)/shard_map/ppermute | solution.py:29
  28.2 2.0 %collective-permute-start.4 = (f32[128,128]{1,0:T(8,128)S(1)}, f32[128,128]{1,0:T(8,128)S(1)}, u32[]{:S(2)}, u32[]{:S(2)}) collective-permute-start(f32[128,128]{1,0:T(8,128)S(1)} %bitcast.55), channel_id=1, source_target_pairs={{0,3},{1,2},{2,1},{3,0},{4,7},{5,6},{6,5},{7,4},{8,11},{9,10},{10,... | collective-permute-start | bytes 196616 | tf_op jit(solution)/shard_map/ppermute | solution.py:35
  30.2 2.2 %collective-permute-done.4 = f32[128,128]{1,0:T(8,128)S(1)} collective-permute-done((f32[128,128]{1,0:T(8,128)S(1)}, f32[128,128]{1,0:T(8,128)S(1)}, u32[]{:S(2)}, u32[]{:S(2)}) %collective-permute-start.4) | collective-permute-done | bytes 65568 | tf_op jit(solution)/shard_map/ppermute | solution.py:35
  32.4 3.2 %collective-permute-start.5 = (f32[128,128]{1,0:T(8,128)S(1)}, f32[128,128]{1,0:T(8,128)S(1)}, u32[]{:S(2)}, u32[]{:S(2)}) collective-permute-start(f32[128,128]{1,0:T(8,128)S(1)} %bitcast_add_fusion.2), channel_id=1, source_target_pairs={{0,5},{1,4},{2,7},{3,6},{4,1},{5,0},{6,3},{7,2},{8,13},{9,12},{10,... | collective-permute-start | bytes 196616 | tf_op jit(solution)/shard_map/ppermute | solution.py:35
  35.5 0.1 broadcast_in_dim.186
  35.6 0.1 broadcast_in_dim.187
  35.7 0.1 broadcast_in_dim.184
  35.8 0.1 broadcast_in_dim.185
  35.8 2.0 %collective-permute-done.5 = f32[128,128]{1,0:T(8,128)S(1)} collective-permute-done((f32[128,128]{1,0:T(8,128)S(1)}, f32[128,128]{1,0:T(8,128)S(1)}, u32[]{:S(2)}, u32[]{:S(2)}) %collective-permute-start.5) | collective-permute-done | bytes 65568 | tf_op jit(solution)/shard_map/ppermute | solution.py:35
  37.8 6.0 %collective-permute-start.6 = (f32[128,128]{1,0:T(8,128)S(1)}, f32[128,128]{1,0:T(8,128)S(1)}, u32[]{:S(2)}, u32[]{:S(2)}) collective-permute-start(f32[128,128]{1,0:T(8,128)S(1)} %add.72), channel_id=1, source_target_pairs={{0,13},{1,12},{2,15},{3,14},{4,9},{5,8},{6,11},{7,10},{8,5},{9,4},... | collective-permute-start | bytes 196616 | tf_op jit(solution)/shard_map/ppermute | solution.py:35
  43.9 2.2 %collective-permute-done.6 = f32[128,128]{1,0:T(8,128)S(1)} collective-permute-done((f32[128,128]{1,0:T(8,128)S(1)}, f32[128,128]{1,0:T(8,128)S(1)}, u32[]{:S(2)}, u32[]{:S(2)}) %collective-permute-start.6) | collective-permute-done | bytes 65568 | tf_op jit(solution)/shard_map/ppermute | solution.py:35
  46.1 0.6 broadcast_in_dim.203
  46.7 3.6 %all-to-all-start.1 = ((f32[32,1,128]{2,1,0:T(1,128)}), f32[32,1,128]{2,1,0:T(1,128)S(1)}, u32[]{:S(2)}, u32[]{:S(2)}) async-start(f32[32,1,128]{2,1,0:T(1,128)} %broadcast_in_dim.203), calls=%async_computation.1 | async-start | bytes 32768 | tf_op jit(solution)/shard_map/all_to_all | solution.py:21
  50.3 0.1 iota_compare_fusion
  50.4 0.1 eq.93
  50.5 3.3 %collective-permute-start.7 = (f32[4,3,16,128]{3,2,0,1:T(8,128)S(1)}, f32[4,3,16,128]{3,2,0,1:T(8,128)S(1)}, u32[]{:S(2)}, u32[]{:S(2)}) collective-permute-start(f32[4,3,16,128]{3,2,0,1:T(8,128)S(1)} %broadcast_select_fusion.1), channel_id=1, source_target_pairs={{0,3},{1,2},{2,1},{3,0},{4,7},{5,6},{6,5},{7,4},{8,11},{9,10},{10,... | collective-permute-start | bytes 294920 | tf_op jit(solution)/shard_map/ppermute | solution.py:35
  53.8 3.6 %all-to-all-done.1 = f32[32,1,128]{2,1,0:T(1,128)S(1)} async-done(((f32[32,1,128]{2,1,0:T(1,128)}), f32[32,1,128]{2,1,0:T(1,128)S(1)}, u32[]{:S(2)}, u32[]{:S(2)}) %all-to-all-start.1) | async-done | bytes 16416 | tf_op jit(solution)/shard_map/all_to_all | solution.py:21
  57.3 0.6 reduce_sum.29
  58.7 0.0 collective-permute-done.7
  58.7 0.1 broadcast_select_fusion
  58.8 0.1 fusion.8
  58.9 0.9 %broadcast_in_dim.204 = bf16[16,128,128]{2,1,0:T(8,128)(2,1)} broadcast(bf16[128,128]{1,0:T(8,128)(2,1)S(1)} %fusion.8), dimensions={1,2} | broadcast | bytes 557056 | tf_op jit(solution)/shard_map/broadcast_in_dim | solution.py:25
  59.8 4.7 %all-to-all-start.2 = ((bf16[16,128,128]{2,1,0:T(8,128)(2,1)}), bf16[16,128,128]{2,1,0:T(8,128)(2,1)S(1)}, u32[]{:S(2)}, u32[]{:S(2)}) async-start(bf16[16,128,128]{2,1,0:T(8,128)(2,1)} %broadcast_in_dim.204), calls=%async_computation.2 | async-start | bytes 1048576 | tf_op jit(solution)/shard_map/all_to_all | solution.py:21
  64.5 0.6 collective-permute-start.9
  65.1 0.1 broadcast_in_dim.179
  65.2 0.1 broadcast_in_dim.180
  65.4 0.6 collective-permute-done.9
  65.9 0.2 abs_reduce_fusion.1
  66.1 9.2 %all-to-all-done.2 = bf16[16,128,128]{2,1,0:T(8,128)(2,1)S(1)} async-done(((bf16[16,128,128]{2,1,0:T(8,128)(2,1)}), bf16[16,128,128]{2,1,0:T(8,128)(2,1)S(1)}, u32[]{:S(2)}, u32[]{:S(2)}) %all-to-all-start.2) | async-done | bytes 524320 | tf_op jit(solution)/shard_map/all_to_all | solution.py:21
  75.3 1.7 %collective-permute-start.8 = (bf16[16,8,1,16,128]{4,3,1,0,2:T(8,128)(2,1)S(1)}, bf16[16,8,1,16,128]{4,3,1,0,2:T(8,128)(2,1)S(1)}, u32[]{:S(2)}, u32[]{:S(2)}) collective-permute-start(bf16[16,8,1,16,128]{4,3,1,0,2:T(8,128)(2,1)S(1)} %bitcast.45), channel_id=1, source_target_pairs={{0,1},{1,0},{2,3},{3,2},{4,5},{5,4},{6,7},{7,6},{8,9},{9,8},{10,11... | collective-permute-start | bytes 1572872 | tf_op jit(solution)/shard_map/ppermute | solution.py:29
  77.0 0.7 divide_convert_fusion
  77.7 0.8 %collective-permute-done.8 = bf16[16,8,1,16,128]{4,3,1,0,2:T(8,128)(2,1)S(1)} collective-permute-done((bf16[16,8,1,16,128]{4,3,1,0,2:T(8,128)(2,1)S(1)}, bf16[16,8,1,16,128]{4,3,1,0,2:T(8,128)(2,1)S(1)}, u32[]{:S(2)}, u32[]{:S(2)}) %collective-permute-start.8) | collective-permute-done | bytes 524320 | tf_op jit(solution)/shard_map/ppermute | solution.py:29
  78.5 1.5 %bitcast_select_fusion = bf16[4096,128]{1,0:T(8,128)(2,1)} fusion(pred[4096]{0:T(1024)(128)(4,1)S(1)} %broadcast_in_dim.180, bf16[16,8,16,128]{3,2,1,0:T(8,128)(2,1)S(1)} %bitcast.52, bf16[16,8,16,128]{3,2,1,0:T(8,128)(2,1)S(1)} %bitcast.46), kind=kLoop, calls=%fused_computation.1 | loop fusion | flops 524288 | bytes 2101248 | tf_op jit(solution)/shard_map/jit(_where)/select_n | solution.py:103
  (37 shorter events, 0.2 us)
Async XLA Ops:
  0.6 7.8 %copy-start.1 = (bf16[16,128]{1,0:T(8,128)(2,1)S(1)}, bf16[16,128]{1,0:T(8,128)(2,1)}, u32[]{:S(2)}) copy-start(bf16[16,128]{1,0:T(8,128)(2,1)} %param.10) | copy-start | bytes 12292
  0.6 7.8 %copy-start.2 = (bf16[16,128]{1,0:T(8,128)(2,1)S(1)}, bf16[16,128]{1,0:T(8,128)(2,1)}, u32[]{:S(2)}) copy-start(bf16[16,128]{1,0:T(8,128)(2,1)} %param.8) | copy-start | bytes 12292
  0.7 7.8 %copy-start.3 = (f32[16]{0:T(128)S(1)}, f32[16]{0:T(128)}, u32[]{:S(2)}) copy-start(f32[16]{0:T(128)} %param.11) | copy-start | bytes 196
  0.7 7.8 %copy-start.4 = (f32[16]{0:T(128)S(1)}, f32[16]{0:T(128)}, u32[]{:S(2)}) copy-start(f32[16]{0:T(128)} %param.9) | copy-start | bytes 196
  0.7 7.9 %copy-start = (f32[16,128]{1,0:T(8,128)S(1)}, f32[16,128]{1,0:T(8,128)}, u32[]{:S(2)}) copy-start(f32[16,128]{1,0:T(8,128)} %param.7) | copy-start | bytes 24580
  0.7 23.8 %all-to-all-start = ((bf16[16,256,128]{2,1,0:T(8,128)(2,1)}), bf16[16,256,128]{2,1,0:T(8,128)(2,1)S(1)}, u32[]{:S(2)}, u32[]{:S(2)}) async-start(bf16[16,256,128]{2,1,0:T(8,128)(2,1)} %bitcast.47), calls=%async_computation | async-start | bytes 2097152 | tf_op jit(solution)/shard_map/all_to_all | solution.py:21
  8.5 1.9 %collective-permute-start = (f32[3,16,128]{2,1,0:T(8,128)S(1)}, f32[3,16,128]{2,1,0:T(8,128)S(1)}, u32[]{:S(2)}, u32[]{:S(2)}) collective-permute-start(f32[3,16,128]{2,1,0:T(8,128)S(1)} %pad_maximum_fusion), channel_id=1, source_target_pairs={{0,1},{1,0},{2,3},{3,2},{4,5},{5,4},{6,7},{7,6},{8,9},{9,8},{10,11... | collective-permute-start | bytes 73736 | tf_op jit(solution)/shard_map/ppermute | solution.py:29
  10.4 8.1 %collective-permute-start.1 = (f32[1,3,16,128]{3,2,1,0:T(8,128)S(1)}, f32[1,3,16,128]{3,2,1,0:T(8,128)S(1)}, u32[]{:S(2)}, u32[]{:S(2)}) collective-permute-start(f32[1,3,16,128]{3,2,1,0:T(8,128)S(1)} %fusion.13), channel_id=1, source_target_pairs={{0,13},{1,12},{2,15},{3,14},{4,9},{5,8},{6,11},{7,10},{8,5},{9,4},... | collective-permute-start | bytes 73736 | tf_op jit(solution)/shard_map/ppermute | solution.py:35
  18.5 5.2 %collective-permute-start.2 = (f32[2,3,16,128]{3,2,0,1:T(8,128)S(1)}, f32[2,3,16,128]{3,2,0,1:T(8,128)S(1)}, u32[]{:S(2)}, u32[]{:S(2)}) collective-permute-start(f32[2,3,16,128]{3,2,0,1:T(8,128)S(1)} %broadcast_select_fusion.2), channel_id=1, source_target_pairs={{0,5},{1,4},{2,7},{3,6},{4,1},{5,0},{6,3},{7,2},{8,13},{9,12},{10,... | collective-permute-start | bytes 147464 | tf_op jit(solution)/shard_map/ppermute | solution.py:35
  24.6 3.6 %collective-permute-start.3 = (f32[8,16,128]{2,1,0:T(8,128)S(1)}, f32[8,16,128]{2,1,0:T(8,128)S(1)}, u32[]{:S(2)}, u32[]{:S(2)}) collective-permute-start(f32[8,16,128]{2,1,0:T(8,128)S(1)} %dynamic-slice_bitcast_fusion), channel_id=1, source_target_pairs={{0,1},{1,0},{2,3},{3,2},{4,5},{5,4},{6,7},{7,6},{8,9},{9,8},{10,11... | collective-permute-start | bytes 196616 | tf_op jit(solution)/shard_map/ppermute | solution.py:29
  28.2 4.1 %collective-permute-start.4 = (f32[128,128]{1,0:T(8,128)S(1)}, f32[128,128]{1,0:T(8,128)S(1)}, u32[]{:S(2)}, u32[]{:S(2)}) collective-permute-start(f32[128,128]{1,0:T(8,128)S(1)} %bitcast.55), channel_id=1, source_target_pairs={{0,3},{1,2},{2,1},{3,0},{4,7},{5,6},{6,5},{7,4},{8,11},{9,10},{10,... | collective-permute-start | bytes 196616 | tf_op jit(solution)/shard_map/ppermute | solution.py:35
  32.4 5.4 %collective-permute-start.5 = (f32[128,128]{1,0:T(8,128)S(1)}, f32[128,128]{1,0:T(8,128)S(1)}, u32[]{:S(2)}, u32[]{:S(2)}) collective-permute-start(f32[128,128]{1,0:T(8,128)S(1)} %bitcast_add_fusion.2), channel_id=1, source_target_pairs={{0,5},{1,4},{2,7},{3,6},{4,1},{5,0},{6,3},{7,2},{8,13},{9,12},{10,... | collective-permute-start | bytes 196616 | tf_op jit(solution)/shard_map/ppermute | solution.py:35
  37.8 8.2 %collective-permute-start.6 = (f32[128,128]{1,0:T(8,128)S(1)}, f32[128,128]{1,0:T(8,128)S(1)}, u32[]{:S(2)}, u32[]{:S(2)}) collective-permute-start(f32[128,128]{1,0:T(8,128)S(1)} %add.72), channel_id=1, source_target_pairs={{0,13},{1,12},{2,15},{3,14},{4,9},{5,8},{6,11},{7,10},{8,5},{9,4},... | collective-permute-start | bytes 196616 | tf_op jit(solution)/shard_map/ppermute | solution.py:35
  46.7 10.6 %all-to-all-start.1 = ((f32[32,1,128]{2,1,0:T(1,128)}), f32[32,1,128]{2,1,0:T(1,128)S(1)}, u32[]{:S(2)}, u32[]{:S(2)}) async-start(f32[32,1,128]{2,1,0:T(1,128)} %broadcast_in_dim.203), calls=%async_computation.1 | async-start | bytes 32768 | tf_op jit(solution)/shard_map/all_to_all | solution.py:21
  50.5 8.2 %collective-permute-start.7 = (f32[4,3,16,128]{3,2,0,1:T(8,128)S(1)}, f32[4,3,16,128]{3,2,0,1:T(8,128)S(1)}, u32[]{:S(2)}, u32[]{:S(2)}) collective-permute-start(f32[4,3,16,128]{3,2,0,1:T(8,128)S(1)} %broadcast_select_fusion.1), channel_id=1, source_target_pairs={{0,3},{1,2},{2,1},{3,0},{4,7},{5,6},{6,5},{7,4},{8,11},{9,10},{10,... | collective-permute-start | bytes 294920 | tf_op jit(solution)/shard_map/ppermute | solution.py:35
  59.8 15.5 %all-to-all-start.2 = ((bf16[16,128,128]{2,1,0:T(8,128)(2,1)}), bf16[16,128,128]{2,1,0:T(8,128)(2,1)S(1)}, u32[]{:S(2)}, u32[]{:S(2)}) async-start(bf16[16,128,128]{2,1,0:T(8,128)(2,1)} %broadcast_in_dim.204), calls=%async_computation.2 | async-start | bytes 1048576 | tf_op jit(solution)/shard_map/all_to_all | solution.py:21
  64.5 1.4 %collective-permute-start.9 = (f32[16,128]{1,0:T(8,128)S(1)}, f32[16,128]{1,0:T(8,128)S(1)}, u32[]{:S(2)}, u32[]{:S(2)}) collective-permute-start(f32[16,128]{1,0:T(8,128)S(1)} %constant_dynamic-slice_fusion), channel_id=1, source_target_pairs={{0,1},{1,0},{2,3},{3,2},{4,5},{5,4},{6,7},{7,6},{8,9},{9,8},{10,11... | collective-permute-start | bytes 24584 | tf_op jit(solution)/shard_map/ppermute | solution.py:29
  75.3 3.2 %collective-permute-start.8 = (bf16[16,8,1,16,128]{4,3,1,0,2:T(8,128)(2,1)S(1)}, bf16[16,8,1,16,128]{4,3,1,0,2:T(8,128)(2,1)S(1)}, u32[]{:S(2)}, u32[]{:S(2)}) collective-permute-start(bf16[16,8,1,16,128]{4,3,1,0,2:T(8,128)(2,1)S(1)} %bitcast.45), channel_id=1, source_target_pairs={{0,1},{1,0},{2,3},{3,2},{4,5},{5,4},{6,7},{7,6},{8,9},{9,8},{10,11... | collective-permute-start | bytes 1572872 | tf_op jit(solution)/shard_map/ppermute | solution.py:29
  77.0 3.0 %copy-start.5 = (f32[16]{0:T(128)}, f32[16]{0:T(128)S(1)}, u32[]{:S(2)}) copy-start(f32[16]{0:T(128)S(1)} %broadcast_add_fusion.1) | copy-start | bytes 196
  77.0 3.0 %copy-start.6 = (f32[16]{0:T(128)}, f32[16]{0:T(128)S(1)}, u32[]{:S(2)}) copy-start(f32[16]{0:T(128)S(1)} %broadcast_add_fusion) | copy-start | bytes 196

commit v5 on v4

--- a/solution.py
+++ b/solution.py
@@ -1,6 +1,11 @@
+import functools
+import math
+
 import jax
 import jax.numpy as jnp
 from jax import lax
+from jax.experimental import pallas as pl
+from jax.experimental.pallas import tpu as pltpu
 from jax.sharding import Mesh
 from jax.sharding import PartitionSpec as P
 
@@ -61,6 +66,20 @@
     return master_new, first_new, second_new
 
 
+def clip_and_advance(limit, norms, total, states, weights, factors):
+    pairs = norms[...]
+    squares = jnp.sum(pairs[:, 0] + pairs[:, 1], keepdims=True)
+    factor = jnp.minimum(1.0, limit / (jnp.sqrt(squares) + 1e-06))
+    factors[...] = jnp.broadcast_to(factor, factors.shape)
+    line, _, rows, width = states.shape
+    for z in range(line):
+        place = pl.ds(z * rows, rows)
+        new, _, _ = advance(factor * total[place], states[z, 0], states[z, 1], states[z, 2])
+        new = new.astype(weights.dtype)
+        for plane in range(weights.shape[0]):
+            weights[plane, place] = new
+
+
 def shards(grads, master, first_q, first_scale, second_q, second_scale):
     blocks, width = grads.shape[1:]
     rows = master.shape[0]
@@ -87,24 +106,28 @@
     total = summed(part)
     total, states = lax.optimization_barrier((total, states))
     norms = sent_to_all(jnp.sum(total * total, axis=0, keepdims=True), ("y", "x", "c"))
-    norms = norms.reshape(planes, cores, width)
-    norms = norms[:, 0] + norms[:, 1]
     states, _ = doubled(states, place, FLIPS[0])
-    line_master, line_first, line_second = (
-        states[:, i].reshape(held, width) for i in range(3)
+    own = lax.dynamic_slice_in_dim(total, z * rows, rows, 0)
+    own = jnp.where(odd == 1, swapped(own), own)
+    states, own = lax.optimization_barrier((states, own))
+    limit = clip_rms * math.sqrt(blocks * width)
+    weights, factor = pl.pallas_call(
+        functools.partial(clip_and_advance, limit),
+        out_shape=(
+            jax.ShapeDtypeStruct((planes, held, width), jnp.bfloat16),
+            jax.ShapeDtypeStruct((8, width), jnp.float32),
+        ),
+        compiler_params=pltpu.CompilerParams(vmem_limit_bytes=4 << 20),
+    )(norms.reshape(planes, cores, width), total, states)
+
+    weights, factor, own, master, first, second, here = lax.optimization_barrier(
+        (exchange(weights, ("y", "x")), factor, own, master, first, second, here)
     )
-    limit = clip_rms * jnp.sqrt(jnp.float32(blocks * width))
-    factor = jnp.minimum(1.0, limit / (jnp.sqrt(norms.sum()) + 1e-06))
-
-    line_new, _, _ = advance(factor * total, line_master, line_first, line_second)
-    weights = sent_to_all(line_new.astype(jnp.bfloat16), ("y", "x"))
     weights = weights.reshape(planes, line, 1, rows, width)
     mine = jnp.arange(cores) == here
     weights = jnp.where(mine[:, None, None], weights, swapped(weights)).reshape(blocks, width)
 
-    own = lax.dynamic_slice_in_dim(total, z * rows, rows, 0)
-    own = jnp.where(odd == 1, swapped(own), own)
-    master_new, first_new, second_new = advance(factor * own, master, first, second)
+    master_new, first_new, second_new = advance(factor[:1] * own, master, first, second)
     first_scale_new = jnp.max(jnp.abs(first_new), axis=1) + 1e-08
     second_scale_new = jnp.max(jnp.abs(second_new), axis=1) + 1e-08
     first_q_new = (first_new / first_scale_new[:, None]).astype(jnp.bfloat16)

time: 80.4 us -> 79.7 us (level)
  blocking collectives: 0 us -> 16.4 us
  waiting for transfers between devices: 28.7 us -> 18.8 us
  starting transfers between devices: 43.6 us -> 38.7 us
  local copies, waits for them, and re-layouts: 2.33 us -> 1.4 us
    all_to_all x0 -> x1, blocking collectives: none -> 16.4 us  [exchange(): return lax.all_to_all(x, axes, split_axis=0, concat_axis=0, tiled=True)]
    all_to_all x3 -> x2, waiting for transfers between devices: 13.3 us -> 1.28 us  [exchange(): return lax.all_to_all(x, axes, split_axis=0, concat_axis=0, tiled=True)]
    all_to_all x3 -> x2, starting transfers between devices: 16 us -> 11.6 us  [exchange(): return lax.all_to_all(x, axes, split_axis=0, concat_axis=0, tiled=True)]
    ppermute x6, waiting for transfers between devices: 12.2 us -> 15.2 us  [from_partner(): return lax.ppermute(x, ('z', 'c'), route)]
    broadcast_in_dim x2 -> x1, local copies, waits for them, and re-layouts: 1.51 us -> 0.62 us  [sent_to_all(): return exchange(jnp.broadcast_to(x, (lax.axis_size(axes), *x.shape)), axes)]
    ppermute x4, waiting for transfers between devices: 3.15 us -> 2.32 us  [swapped(): return lax.ppermute(x, 'c', [(0, 1), (1, 0)])]
  transfers between devices with their start and end apart: 13 -> 12, of which waited for: 12 -> 11; matrix products, arithmetic and copies ran while one was open for 3% -> 3% of each run, Pallas kernels for 0% -> 0%
where the time goes in v5:
time: 79.7 us; the launch traced here: 79.4 us
  starting transfers between devices  38.7 us (49%)
  waiting for transfers between devices  18.8 us (24%)
  blocking collectives  16.4 us (21%)
  other arithmetic  3 us (4%)
  local copies, waits for them, and re-layouts  1.4 us (2%)
  between operations  0.82 us (1%)
    ppermute x6, starting transfers between devices, from_partner(): return lax.ppermute(x, ('z', 'c'), route)  21.5 us
    all_to_all x1, blocking collectives, exchange(): return lax.all_to_all(x, axes, split_axis=0, concat_axis=0, tiled=True)  16.4 us
    ppermute x6, waiting for transfers between devices, from_partner(): return lax.ppermute(x, ('z', 'c'), route)  15.2 us
    all_to_all x2, starting transfers between devices, exchange(): return lax.all_to_all(x, axes, split_axis=0, concat_axis=0, tiled=True)  11.6 us
    ppermute x4, starting transfers between devices, swapped(): return lax.ppermute(x, 'c', [(0, 1), (1, 0)])  5.67 us
    ppermute x4, waiting for transfers between devices, swapped(): return lax.ppermute(x, 'c', [(0, 1), (1, 0)])  2.32 us
  transfers between devices with their start and end apart: 12, of which 11 were waited for; matrix products, arithmetic and copies ran while one was open for 3% of the time, Pallas kernels for 0%

profile of v5, /device:TPU:1, one launch (start us, length us, event | category | flops | bytes accessed | tf_op | source)
XLA Modules:
  0.0 79.4 jit_solution(5066127614207499921)
XLA Ops:
  0.6 0.0 copy-start.1
  0.7 7.7 %all-to-all-start = ((bf16[16,256,128]{2,1,0:T(8,128)(2,1)}), bf16[16,256,128]{2,1,0:T(8,128)(2,1)S(1)}, u32[]{:S(2)}, u32[]{:S(2)}) async-start(bf16[16,256,128]{2,1,0:T(8,128)(2,1)} %bitcast.37), calls=%async_computation | async-start | bytes 2097152 | tf_op jit(solution)/shard_map/all_to_all | solution.py:26
  8.4 0.1 convert_multiply_fusion
  8.5 1.0 %collective-permute-start = (f32[3,16,128]{2,1,0:T(8,128)S(1)}, f32[3,16,128]{2,1,0:T(8,128)S(1)}, u32[]{:S(2)}, u32[]{:S(2)}) collective-permute-start(f32[3,16,128]{2,1,0:T(8,128)S(1)} %pad_maximum_fusion), channel_id=1, source_target_pairs={{0,1},{1,0},{2,3},{3,2},{4,5},{5,4},{6,7},{7,6},{8,9},{9,8},{10,11... | collective-permute-start | bytes 73736 | tf_op jit(solution)/shard_map/ppermute | solution.py:34
  9.6 0.8 %collective-permute-done = f32[3,16,128]{2,1,0:T(8,128)S(1)} collective-permute-done((f32[3,16,128]{2,1,0:T(8,128)S(1)}, f32[3,16,128]{2,1,0:T(8,128)S(1)}, u32[]{:S(2)}, u32[]{:S(2)}) %collective-permute-start) | collective-permute-done | bytes 24608 | tf_op jit(solution)/shard_map/ppermute | solution.py:34
  10.4 6.3 %collective-permute-start.1 = (f32[1,3,16,128]{3,2,1,0:T(8,128)S(1)}, f32[1,3,16,128]{3,2,1,0:T(8,128)S(1)}, u32[]{:S(2)}, u32[]{:S(2)}) collective-permute-start(f32[1,3,16,128]{3,2,1,0:T(8,128)S(1)} %fusion.4), channel_id=1, source_target_pairs={{0,13},{1,12},{2,15},{3,14},{4,9},{5,8},{6,11},{7,10},{8,5},{9,4},... | collective-permute-start | bytes 73736 | tf_op jit(solution)/shard_map/ppermute | solution.py:40
  16.7 1.8 %collective-permute-done.1 = f32[1,3,16,128]{3,2,1,0:T(8,128)S(1)} collective-permute-done((f32[1,3,16,128]{3,2,1,0:T(8,128)S(1)}, f32[1,3,16,128]{3,2,1,0:T(8,128)S(1)}, u32[]{:S(2)}, u32[]{:S(2)}) %collective-permute-start.1) | collective-permute-done | bytes 24608 | tf_op jit(solution)/shard_map/ppermute | solution.py:40
  18.5 0.1 broadcast_select_fusion
  18.6 1.0 %collective-permute-start.2 = (f32[2,3,16,128]{3,2,1,0:T(8,128)S(1)}, f32[2,3,16,128]{3,2,1,0:T(8,128)S(1)}, u32[]{:S(2)}, u32[]{:S(2)}) collective-permute-start(f32[2,3,16,128]{3,2,1,0:T(8,128)S(1)} %broadcast_select_fusion), channel_id=1, source_target_pairs={{0,5},{1,4},{2,7},{3,6},{4,1},{5,0},{6,3},{7,2},{8,13},{9,12},{10,... | collective-permute-start | bytes 147464 | tf_op jit(solution)/shard_map/ppermute | solution.py:40
  19.5 0.1 iota_compare_fusion.1
  19.6 0.1 eq.87
  19.7 4.1 %collective-permute-done.2 = f32[2,3,16,128]{3,2,1,0:T(8,128)S(1)} collective-permute-done((f32[2,3,16,128]{3,2,1,0:T(8,128)S(1)}, f32[2,3,16,128]{3,2,1,0:T(8,128)S(1)}, u32[]{:S(2)}, u32[]{:S(2)}) %collective-permute-start.2) | collective-permute-done | bytes 49184 | tf_op jit(solution)/shard_map/ppermute | solution.py:40
  23.8 0.1 bitcast_select_fusion.2
  23.8 0.6 all-to-all-done
  24.4 0.1 convert_reduce_fusion
  24.6 2.7 %collective-permute-start.3 = (f32[8,16,128]{2,1,0:T(8,128)S(1)}, f32[8,16,128]{2,1,0:T(8,128)S(1)}, u32[]{:S(2)}, u32[]{:S(2)}) collective-permute-start(f32[8,16,128]{2,1,0:T(8,128)S(1)} %dynamic-slice_bitcast_fusion), channel_id=1, source_target_pairs={{0,1},{1,0},{2,3},{3,2},{4,5},{5,4},{6,7},{7,6},{8,9},{9,8},{10,11... | collective-permute-start | bytes 196616 | tf_op jit(solution)/shard_map/ppermute | solution.py:34
  27.3 0.9 %collective-permute-done.3 = f32[8,16,128]{2,1,0:T(8,128)S(1)} collective-permute-done((f32[8,16,128]{2,1,0:T(8,128)S(1)}, f32[8,16,128]{2,1,0:T(8,128)S(1)}, u32[]{:S(2)}, u32[]{:S(2)}) %collective-permute-start.3) | collective-permute-done | bytes 65568 | tf_op jit(solution)/shard_map/ppermute | solution.py:34
  28.2 2.0 %collective-permute-start.4 = (f32[128,128]{1,0:T(8,128)S(1)}, f32[128,128]{1,0:T(8,128)S(1)}, u32[]{:S(2)}, u32[]{:S(2)}) collective-permute-start(f32[128,128]{1,0:T(8,128)S(1)} %bitcast.41), channel_id=1, source_target_pairs={{0,3},{1,2},{2,1},{3,0},{4,7},{5,6},{6,5},{7,4},{8,11},{9,10},{10,... | collective-permute-start | bytes 196616 | tf_op jit(solution)/shard_map/ppermute | solution.py:40
  30.2 0.1 broadcast_in_dim.191
  30.2 0.1 broadcast_in_dim.192
  30.3 0.1 broadcast_in_dim.189
  30.4 0.1 broadcast_in_dim.190
  30.5 1.9 %collective-permute-done.4 = f32[128,128]{1,0:T(8,128)S(1)} collective-permute-done((f32[128,128]{1,0:T(8,128)S(1)}, f32[128,128]{1,0:T(8,128)S(1)}, u32[]{:S(2)}, u32[]{:S(2)}) %collective-permute-start.4) | collective-permute-done | bytes 65568 | tf_op jit(solution)/shard_map/ppermute | solution.py:40
  32.4 3.2 %collective-permute-start.5 = (f32[128,128]{1,0:T(8,128)S(1)}, f32[128,128]{1,0:T(8,128)S(1)}, u32[]{:S(2)}, u32[]{:S(2)}) collective-permute-start(f32[128,128]{1,0:T(8,128)S(1)} %bitcast_add_fusion.1), channel_id=1, source_target_pairs={{0,5},{1,4},{2,7},{3,6},{4,1},{5,0},{6,3},{7,2},{8,13},{9,12},{10,... | collective-permute-start | bytes 196616 | tf_op jit(solution)/shard_map/ppermute | solution.py:40
  35.5 2.3 %collective-permute-done.5 = f32[128,128]{1,0:T(8,128)S(1)} collective-permute-done((f32[128,128]{1,0:T(8,128)S(1)}, f32[128,128]{1,0:T(8,128)S(1)}, u32[]{:S(2)}, u32[]{:S(2)}) %collective-permute-start.5) | collective-permute-done | bytes 65568 | tf_op jit(solution)/shard_map/ppermute | solution.py:40
  37.8 6.0 %collective-permute-start.6 = (f32[128,128]{1,0:T(8,128)S(1)}, f32[128,128]{1,0:T(8,128)S(1)}, u32[]{:S(2)}, u32[]{:S(2)}) collective-permute-start(f32[128,128]{1,0:T(8,128)S(1)} %add.53), channel_id=1, source_target_pairs={{0,13},{1,12},{2,15},{3,14},{4,9},{5,8},{6,11},{7,10},{8,5},{9,4},... | collective-permute-start | bytes 196616 | tf_op jit(solution)/shard_map/ppermute | solution.py:40
  43.9 0.1 iota_compare_fusion
  43.9 0.1 eq.92
  44.0 2.0 %collective-permute-done.6 = f32[128,128]{1,0:T(8,128)S(1)} collective-permute-done((f32[128,128]{1,0:T(8,128)S(1)}, f32[128,128]{1,0:T(8,128)S(1)}, u32[]{:S(2)}, u32[]{:S(2)}) %collective-permute-start.6) | collective-permute-done | bytes 65568 | tf_op jit(solution)/shard_map/ppermute | solution.py:40
  46.1 0.2 collective-permute-start.8
  46.3 0.6 broadcast_in_dim.188
  46.9 3.9 %all-to-all-start.1 = ((f32[32,1,128]{2,1,0:T(1,128)}), f32[32,1,128]{2,1,0:T(1,128)S(1)}, u32[]{:S(2)}, u32[]{:S(2)}) async-start(f32[32,1,128]{2,1,0:T(1,128)} %broadcast_in_dim.188), calls=%async_computation.1 | async-start | bytes 32768 | tf_op jit(solution)/shard_map/all_to_all | solution.py:26
  50.8 3.1 %collective-permute-start.7 = (f32[4,3,16,128]{3,2,1,0:T(8,128)S(1)}, f32[4,3,16,128]{3,2,1,0:T(8,128)S(1)}, u32[]{:S(2)}, u32[]{:S(2)}) collective-permute-start(f32[4,3,16,128]{3,2,1,0:T(8,128)S(1)} %bitcast_select_fusion.2), channel_id=1, source_target_pairs={{0,3},{1,2},{2,1},{3,0},{4,7},{5,6},{6,5},{7,4},{8,11},{9,10},{10,... | collective-permute-start | bytes 294920 | tf_op jit(solution)/shard_map/ppermute | solution.py:40
  53.9 0.0 collective-permute-done.8
  53.9 3.1 %collective-permute-done.7 = f32[4,3,16,128]{3,2,1,0:T(8,128)S(1)} collective-permute-done((f32[4,3,16,128]{3,2,1,0:T(8,128)S(1)}, f32[4,3,16,128]{3,2,1,0:T(8,128)S(1)}, u32[]{:S(2)}, u32[]{:S(2)}) %collective-permute-start.7) | collective-permute-done | bytes 98336 | tf_op jit(solution)/shard_map/ppermute | solution.py:40
  57.0 0.1 bitcast_select_fusion.1.states
  57.1 0.7 all-to-all-done.1
  57.8 0.2 shard_map.109
  58.0 16.4 %all_to_all.15 = bf16[16,128,128]{2,1,0:T(8,128)(2,1)S(1)} all-to-all(bf16[16,128,128]{2,1,0:T(8,128)(2,1)S(1)} %get-tuple-element.26), channel_id=1, replica_groups=mesh['y'=4,'x'=4,'z'=8,'c'=2] {'y','x'}, dimensions={0} | all-to-all | bytes 1048576 | tf_op jit(solution)/shard_map/all_to_all | solution.py:26
  74.5 0.1 abs_reduce_fusion.1
  74.6 0.0 copy-start.5
  74.6 1.7 %collective-permute-start.9 = (bf16[16,8,1,16,128]{4,3,1,0,2:T(8,128)(2,1)S(1)}, bf16[16,8,1,16,128]{4,3,1,0,2:T(8,128)(2,1)S(1)}, u32[]{:S(2)}, u32[]{:S(2)}) collective-permute-start(bf16[16,8,1,16,128]{4,3,1,0,2:T(8,128)(2,1)S(1)} %bitcast.35), channel_id=1, source_target_pairs={{0,1},{1,0},{2,3},{3,2},{4,5},{5,4},{6,7},{7,6},{8,9},{9,8},{10,11... | collective-permute-start | bytes 1572872 | tf_op jit(solution)/shard_map/ppermute | solution.py:34
  76.4 0.1 broadcast_in_dim.198
  76.5 0.1 broadcast_in_dim.199
  76.6 0.0 copy-start.6
  76.6 0.7 divide_convert_fusion
  77.3 0.6 collective-permute-done.9
  77.9 1.5 %bitcast_select_fusion = bf16[4096,128]{1,0:T(8,128)(2,1)} fusion(pred[4096]{0:T(1024)(128)(4,1)S(1)} %broadcast_in_dim.199, bf16[16,8,16,128]{3,2,1,0:T(8,128)(2,1)S(1)} %bitcast.40, bf16[16,8,16,128]{3,2,1,0:T(8,128)(2,1)S(1)} %bitcast.36), kind=kLoop, calls=%fused_computation.1 | loop fusion | flops 524288 | bytes 2101248 | tf_op jit(solution)/shard_map/jit(_where)/select_n | solution.py:128
  (30 shorter events, 0.2 us)
Async XLA Ops:
  0.6 7.8 %copy-start.1 = (bf16[16,128]{1,0:T(8,128)(2,1)S(1)}, bf16[16,128]{1,0:T(8,128)(2,1)}, u32[]{:S(2)}) copy-start(bf16[16,128]{1,0:T(8,128)(2,1)} %param.10) | copy-start | bytes 12292
  0.6 7.8 %copy-start.2 = (bf16[16,128]{1,0:T(8,128)(2,1)S(1)}, bf16[16,128]{1,0:T(8,128)(2,1)}, u32[]{:S(2)}) copy-start(bf16[16,128]{1,0:T(8,128)(2,1)} %param.8) | copy-start | bytes 12292
  0.7 7.8 %copy-start.3 = (f32[16]{0:T(128)S(1)}, f32[16]{0:T(128)}, u32[]{:S(2)}) copy-start(f32[16]{0:T(128)} %param.11) | copy-start | bytes 196
  0.7 7.8 %copy-start.4 = (f32[16]{0:T(128)S(1)}, f32[16]{0:T(128)}, u32[]{:S(2)}) copy-start(f32[16]{0:T(128)} %param.9) | copy-start | bytes 196
  0.7 7.9 %copy-start = (f32[16,128]{1,0:T(8,128)S(1)}, f32[16,128]{1,0:T(8,128)}, u32[]{:S(2)}) copy-start(f32[16,128]{1,0:T(8,128)} %param.7) | copy-start | bytes 24580
  0.7 23.8 %all-to-all-start = ((bf16[16,256,128]{2,1,0:T(8,128)(2,1)}), bf16[16,256,128]{2,1,0:T(8,128)(2,1)S(1)}, u32[]{:S(2)}, u32[]{:S(2)}) async-start(bf16[16,256,128]{2,1,0:T(8,128)(2,1)} %bitcast.37), calls=%async_computation | async-start | bytes 2097152 | tf_op jit(solution)/shard_map/all_to_all | solution.py:26
  8.5 1.9 %collective-permute-start = (f32[3,16,128]{2,1,0:T(8,128)S(1)}, f32[3,16,128]{2,1,0:T(8,128)S(1)}, u32[]{:S(2)}, u32[]{:S(2)}) collective-permute-start(f32[3,16,128]{2,1,0:T(8,128)S(1)} %pad_maximum_fusion), channel_id=1, source_target_pairs={{0,1},{1,0},{2,3},{3,2},{4,5},{5,4},{6,7},{7,6},{8,9},{9,8},{10,11... | collective-permute-start | bytes 73736 | tf_op jit(solution)/shard_map/ppermute | solution.py:34
  10.4 8.1 %collective-permute-start.1 = (f32[1,3,16,128]{3,2,1,0:T(8,128)S(1)}, f32[1,3,16,128]{3,2,1,0:T(8,128)S(1)}, u32[]{:S(2)}, u32[]{:S(2)}) collective-permute-start(f32[1,3,16,128]{3,2,1,0:T(8,128)S(1)} %fusion.4), channel_id=1, source_target_pairs={{0,13},{1,12},{2,15},{3,14},{4,9},{5,8},{6,11},{7,10},{8,5},{9,4},... | collective-permute-start | bytes 73736 | tf_op jit(solution)/shard_map/ppermute | solution.py:40
  18.6 5.2 %collective-permute-start.2 = (f32[2,3,16,128]{3,2,1,0:T(8,128)S(1)}, f32[2,3,16,128]{3,2,1,0:T(8,128)S(1)}, u32[]{:S(2)}, u32[]{:S(2)}) collective-permute-start(f32[2,3,16,128]{3,2,1,0:T(8,128)S(1)} %broadcast_select_fusion), channel_id=1, source_target_pairs={{0,5},{1,4},{2,7},{3,6},{4,1},{5,0},{6,3},{7,2},{8,13},{9,12},{10,... | collective-permute-start | bytes 147464 | tf_op jit(solution)/shard_map/ppermute | solution.py:40
  24.6 3.6 %collective-permute-start.3 = (f32[8,16,128]{2,1,0:T(8,128)S(1)}, f32[8,16,128]{2,1,0:T(8,128)S(1)}, u32[]{:S(2)}, u32[]{:S(2)}) collective-permute-start(f32[8,16,128]{2,1,0:T(8,128)S(1)} %dynamic-slice_bitcast_fusion), channel_id=1, source_target_pairs={{0,1},{1,0},{2,3},{3,2},{4,5},{5,4},{6,7},{7,6},{8,9},{9,8},{10,11... | collective-permute-start | bytes 196616 | tf_op jit(solution)/shard_map/ppermute | solution.py:34
  28.2 4.1 %collective-permute-start.4 = (f32[128,128]{1,0:T(8,128)S(1)}, f32[128,128]{1,0:T(8,128)S(1)}, u32[]{:S(2)}, u32[]{:S(2)}) collective-permute-start(f32[128,128]{1,0:T(8,128)S(1)} %bitcast.41), channel_id=1, source_target_pairs={{0,3},{1,2},{2,1},{3,0},{4,7},{5,6},{6,5},{7,4},{8,11},{9,10},{10,... | collective-permute-start | bytes 196616 | tf_op jit(solution)/shard_map/ppermute | solution.py:40
  32.4 5.4 %collective-permute-start.5 = (f32[128,128]{1,0:T(8,128)S(1)}, f32[128,128]{1,0:T(8,128)S(1)}, u32[]{:S(2)}, u32[]{:S(2)}) collective-permute-start(f32[128,128]{1,0:T(8,128)S(1)} %bitcast_add_fusion.1), channel_id=1, source_target_pairs={{0,5},{1,4},{2,7},{3,6},{4,1},{5,0},{6,3},{7,2},{8,13},{9,12},{10,... | collective-permute-start | bytes 196616 | tf_op jit(solution)/shard_map/ppermute | solution.py:40
  37.8 8.2 %collective-permute-start.6 = (f32[128,128]{1,0:T(8,128)S(1)}, f32[128,128]{1,0:T(8,128)S(1)}, u32[]{:S(2)}, u32[]{:S(2)}) collective-permute-start(f32[128,128]{1,0:T(8,128)S(1)} %add.53), channel_id=1, source_target_pairs={{0,13},{1,12},{2,15},{3,14},{4,9},{5,8},{6,11},{7,10},{8,5},{9,4},... | collective-permute-start | bytes 196616 | tf_op jit(solution)/shard_map/ppermute | solution.py:40
  46.1 7.8 %collective-permute-start.8 = (f32[16,128]{1,0:T(8,128)S(1)}, f32[16,128]{1,0:T(8,128)S(1)}, u32[]{:S(2)}, u32[]{:S(2)}) collective-permute-start(f32[16,128]{1,0:T(8,128)S(1)} %constant_dynamic-slice_fusion), channel_id=1, source_target_pairs={{0,1},{1,0},{2,3},{3,2},{4,5},{5,4},{6,7},{7,6},{8,9},{9,8},{10,11... | collective-permute-start | bytes 24584 | tf_op jit(solution)/shard_map/ppermute | solution.py:34
  46.9 10.9 %all-to-all-start.1 = ((f32[32,1,128]{2,1,0:T(1,128)}), f32[32,1,128]{2,1,0:T(1,128)S(1)}, u32[]{:S(2)}, u32[]{:S(2)}) async-start(f32[32,1,128]{2,1,0:T(1,128)} %broadcast_in_dim.188), calls=%async_computation.1 | async-start | bytes 32768 | tf_op jit(solution)/shard_map/all_to_all | solution.py:26
  50.8 6.2 %collective-permute-start.7 = (f32[4,3,16,128]{3,2,1,0:T(8,128)S(1)}, f32[4,3,16,128]{3,2,1,0:T(8,128)S(1)}, u32[]{:S(2)}, u32[]{:S(2)}) collective-permute-start(f32[4,3,16,128]{3,2,1,0:T(8,128)S(1)} %bitcast_select_fusion.2), channel_id=1, source_target_pairs={{0,3},{1,2},{2,1},{3,0},{4,7},{5,6},{6,5},{7,4},{8,11},{9,10},{10,... | collective-permute-start | bytes 294920 | tf_op jit(solution)/shard_map/ppermute | solution.py:40
  74.6 4.8 %copy-start.5 = (f32[16]{0:T(128)}, f32[16]{0:T(128)S(1)}, u32[]{:S(2)}) copy-start(f32[16]{0:T(128)S(1)} %broadcast_add_fusion.1) | copy-start | bytes 196
  74.6 3.3 %collective-permute-start.9 = (bf16[16,8,1,16,128]{4,3,1,0,2:T(8,128)(2,1)S(1)}, bf16[16,8,1,16,128]{4,3,1,0,2:T(8,128)(2,1)S(1)}, u32[]{:S(2)}, u32[]{:S(2)}) collective-permute-start(bf16[16,8,1,16,128]{4,3,1,0,2:T(8,128)(2,1)S(1)} %bitcast.35), channel_id=1, source_target_pairs={{0,1},{1,0},{2,3},{3,2},{4,5},{5,4},{6,7},{7,6},{8,9},{9,8},{10,11... | collective-permute-start | bytes 1572872 | tf_op jit(solution)/shard_map/ppermute | solution.py:34
  76.6 2.8 %copy-start.6 = (f32[16]{0:T(128)}, f32[16]{0:T(128)S(1)}, u32[]{:S(2)}) copy-start(f32[16]{0:T(128)S(1)} %broadcast_add_fusion) | copy-start | bytes 196

commit v6 on v5

--- a/solution.py
+++ b/solution.py
@@ -43,12 +43,6 @@
 FLIPS = ((1, 0), (2, 1), (6, 2))
 
 
-def summed(x):
-    for flip, _ in FLIPS:
-        x = x + from_partner(x, flip)
-    return x
-
-
 def doubled(x, place, step):
     flip, level = step
     other = from_partner(x, flip)
@@ -80,6 +74,33 @@
             weights[plane, place] = new
 
 
+def crosswise():
+    z = lax.axis_index("z")
+    return (z ^ z >> 1) & 1
+
+
+def lay(other, half, *refs):
+    out, sent = refs[-2:]
+    side = lax.axis_index("c") ^ crosswise() ^ other
+    copy = pltpu.make_async_copy(half, out.at[:, :, side], sent)
+    copy.start()
+    copy.wait()
+
+
+def laid(half, other, out):
+    planes, line, rows, width = half.shape
+    held = () if out is None else (out,)
+    return pl.pallas_call(
+        functools.partial(lay, other),
+        out_shape=jax.ShapeDtypeStruct((planes, line, 2, rows, width), half.dtype),
+        in_specs=[pl.BlockSpec(memory_space=pltpu.VMEM)] + [pl.BlockSpec(memory_space=pl.ANY)] * len(held),
+        out_specs=pl.BlockSpec(memory_space=pl.ANY),
+        scratch_shapes=[pltpu.SemaphoreType.DMA],
+        input_output_aliases={1: 0} if held else {},
+        compiler_params=pltpu.CompilerParams(vmem_limit_bytes=4 << 20),
+    )(half, *held)
+
+
 def shards(grads, master, first_q, first_scale, second_q, second_scale):
     blocks, width = grads.shape[1:]
     rows = master.shape[0]
@@ -88,9 +109,8 @@
     first = first_q.astype(jnp.float32) * first_scale[:, None]
     second = second_q.astype(jnp.float32) * second_scale[:, None]
 
-    z, core = lax.axis_index("z"), lax.axis_index("c")
-    odd = (z ^ z >> 1) & 1
-    here = core ^ odd
+    z, odd = lax.axis_index("z"), crosswise()
+    here = lax.axis_index("c") ^ odd
 
     arrived = exchange(grads[0].reshape(planes, line * cores * rows, width), ("y", "x"))
     states = jnp.stack([master, first, second])
@@ -103,13 +123,17 @@
     kept, sent = (lax.dynamic_index_in_dim(both, i, 1, False) for i in (here, 1 - here))
     part = (kept + swapped(sent)).reshape(held, width)
 
-    total = summed(part)
-    total, states = lax.optimization_barrier((total, states))
+    total, states = lax.optimization_barrier((part, states))
+    (last, _), *middle = FLIPS[::-1]
+    whole, _ = doubled(states, place, FLIPS[0])
+    for flip, _ in middle[::-1]:
+        total = total + from_partner(total, flip)
+    total, states = lax.optimization_barrier((total, whole))
+    total = total + from_partner(total, last)
     norms = sent_to_all(jnp.sum(total * total, axis=0, keepdims=True), ("y", "x", "c"))
-    states, _ = doubled(states, place, FLIPS[0])
-    own = lax.dynamic_slice_in_dim(total, z * rows, rows, 0)
-    own = jnp.where(odd == 1, swapped(own), own)
-    states, own = lax.optimization_barrier((states, own))
+    norms, total, states, master, first, second, z, odd = lax.optimization_barrier(
+        (norms, total, states, master, first, second, z, odd)
+    )
     limit = clip_rms * math.sqrt(blocks * width)
     weights, factor = pl.pallas_call(
         functools.partial(clip_and_advance, limit),
@@ -120,13 +144,15 @@
         compiler_params=pltpu.CompilerParams(vmem_limit_bytes=4 << 20),
     )(norms.reshape(planes, cores, width), total, states)
 
-    weights, factor, own, master, first, second, here = lax.optimization_barrier(
-        (exchange(weights, ("y", "x")), factor, own, master, first, second, here)
+    weights, factor, total, master, first, second, z, odd = lax.optimization_barrier(
+        (exchange(weights, ("y", "x")), factor, total, master, first, second, z, odd)
     )
-    weights = weights.reshape(planes, line, 1, rows, width)
-    mine = jnp.arange(cores) == here
-    weights = jnp.where(mine[:, None, None], weights, swapped(weights)).reshape(blocks, width)
+    weights = weights.reshape(planes, line, rows, width)
+    partner = swapped(weights)
+    weights = laid(partner, 1, laid(weights, 0, None)).reshape(blocks, width)
 
+    own = lax.dynamic_slice_in_dim(total, z * rows, rows, 0)
+    own = jnp.where(odd == 1, swapped(own), own)
     master_new, first_new, second_new = advance(factor[:1] * own, master, first, second)
     first_scale_new = jnp.max(jnp.abs(first_new), axis=1) + 1e-08
     second_scale_new = jnp.max(jnp.abs(second_new), axis=1) + 1e-08

time: 79.7 us -> 75.1 us (0.942)
  blocking collectives: 16.4 us -> 23.3 us
  starting transfers between devices: 38.7 us -> 32 us
  waiting for transfers between devices: 18.8 us -> 14.7 us
  Pallas kernels: 0.22 us -> 1.82 us
  other arithmetic: 3 us -> 1.51 us
  local copies, waits for them, and re-layouts: 1.4 us -> 0.54 us
    all_to_all x1 -> x2, blocking collectives: 16.4 us -> 23.3 us  [exchange(): return lax.all_to_all(x, axes, split_axis=0, concat_axis=0, tiled=True)]
    all_to_all x2 -> x1, starting transfers between devices: 11.6 us -> 7.72 us  [exchange(): return lax.all_to_all(x, axes, split_axis=0, concat_axis=0, tiled=True)]
    ppermute x6, starting transfers between devices: 21.5 us -> 18.5 us  [from_partner(): return lax.ppermute(x, ('z', 'c'), route)]
    ppermute x6, waiting for transfers between devices: 15.2 us -> 12.5 us  [from_partner(): return lax.ppermute(x, ('z', 'c'), route)]
    pallas_call x0 -> x2, Pallas kernels: none -> 1.6 us  [laid(): pl.pallas_call(functools.partial(lay, other), out_shape=jax.ShapeDtypeStr...]
    select_n x2 -> x0, other arithmetic: 1.49 us -> none  [the longest x1 1.48 us: shards(): jnp.where(mine[:, None, None], weights, swapped(weights))]
  transfers between devices with their start and end apart: 12 -> 11, of which waited for: 11 -> 9; matrix products, arithmetic and copies ran while one was open for 3% -> 2% of each run, Pallas kernels for 0% -> 1%
where the time goes in v6:
time: 75.1 us; the launch traced here: 74.8 us
  starting transfers between devices  32 us (43%)
  blocking collectives  23.3 us (31%)
  waiting for transfers between devices  14.7 us (20%)
  Pallas kernels  1.82 us (2%)
  other arithmetic  1.51 us (2%)
  between operations  0.83 us (1%)
    all_to_all x2, blocking collectives, exchange(): return lax.all_to_all(x, axes, split_axis=0, concat_axis=0, tiled=True)  23.3 us
    ppermute x6, starting transfers between devices, from_partner(): return lax.ppermute(x, ('z', 'c'), route)  18.5 us
    ppermute x6, waiting for transfers between devices, from_partner(): return lax.ppermute(x, ('z', 'c'), route)  12.5 us
    all_to_all x1, starting transfers between devices, exchange(): return lax.all_to_all(x, axes, split_axis=0, concat_axis=0, tiled=True)  7.72 us
    ppermute x4, starting transfers between devices, swapped(): return lax.ppermute(x, 'c', [(0, 1), (1, 0)])  5.84 us
    pallas_call x2, Pallas kernels, laid(): pl.pallas_call(functools.partial(lay, other), out_shape=jax.ShapeDtypeStr...  1.6 us
    ppermute x4, waiting for transfers between devices, swapped(): return lax.ppermute(x, 'c', [(0, 1), (1, 0)])  1.58 us
  transfers between devices with their start and end apart: 11, of which 9 were waited for; matrix products, arithmetic and copies ran while one was open for 2% of the time, Pallas kernels for 1%

profile of v6, /device:TPU:1, one launch (start us, length us, event | category | flops | bytes accessed | tf_op | source)
XLA Modules:
  0.0 74.8 jit_solution(10776710485838217740)
XLA Ops:
  0.6 0.0 copy-start.1
  0.6 0.0 copy-start.2
  0.7 7.7 %all-to-all-start = ((bf16[16,256,128]{2,1,0:T(8,128)(2,1)}), bf16[16,256,128]{2,1,0:T(8,128)(2,1)S(1)}, u32[]{:S(2)}, u32[]{:S(2)}) async-start(bf16[16,256,128]{2,1,0:T(8,128)(2,1)} %bitcast.32), calls=%async_computation | async-start | bytes 2097152 | tf_op jit(solution)/shard_map/all_to_all | solution.py:26
  8.4 0.1 convert_multiply_fusion
  8.5 1.0 %collective-permute-start = (f32[3,16,128]{2,1,0:T(8,128)S(1)}, f32[3,16,128]{2,1,0:T(8,128)S(1)}, u32[]{:S(2)}, u32[]{:S(2)}) collective-permute-start(f32[3,16,128]{2,1,0:T(8,128)S(1)} %pad_maximum_fusion), channel_id=1, source_target_pairs={{0,1},{1,0},{2,3},{3,2},{4,5},{5,4},{6,7},{7,6},{8,9},{9,8},{10,11... | collective-permute-start | bytes 73736 | tf_op jit(solution)/shard_map/ppermute | solution.py:34
  9.6 0.8 %collective-permute-done = f32[3,16,128]{2,1,0:T(8,128)S(1)} collective-permute-done((f32[3,16,128]{2,1,0:T(8,128)S(1)}, f32[3,16,128]{2,1,0:T(8,128)S(1)}, u32[]{:S(2)}, u32[]{:S(2)}) %collective-permute-start) | collective-permute-done | bytes 24608 | tf_op jit(solution)/shard_map/ppermute | solution.py:34
  10.4 6.3 %collective-permute-start.1 = (f32[1,3,16,128]{3,2,1,0:T(8,128)S(1)}, f32[1,3,16,128]{3,2,1,0:T(8,128)S(1)}, u32[]{:S(2)}, u32[]{:S(2)}) collective-permute-start(f32[1,3,16,128]{3,2,1,0:T(8,128)S(1)} %fusion.4), channel_id=1, source_target_pairs={{0,13},{1,12},{2,15},{3,14},{4,9},{5,8},{6,11},{7,10},{8,5},{9,4},... | collective-permute-start | bytes 73736 | tf_op jit(solution)/shard_map/ppermute | solution.py:40
  16.7 1.8 %collective-permute-done.1 = f32[1,3,16,128]{3,2,1,0:T(8,128)S(1)} collective-permute-done((f32[1,3,16,128]{3,2,1,0:T(8,128)S(1)}, f32[1,3,16,128]{3,2,1,0:T(8,128)S(1)}, u32[]{:S(2)}, u32[]{:S(2)}) %collective-permute-start.1) | collective-permute-done | bytes 24608 | tf_op jit(solution)/shard_map/ppermute | solution.py:40
  18.5 0.1 broadcast_select_fusion
  18.6 1.0 %collective-permute-start.2 = (f32[2,3,16,128]{3,2,1,0:T(8,128)S(1)}, f32[2,3,16,128]{3,2,1,0:T(8,128)S(1)}, u32[]{:S(2)}, u32[]{:S(2)}) collective-permute-start(f32[2,3,16,128]{3,2,1,0:T(8,128)S(1)} %broadcast_select_fusion), channel_id=1, source_target_pairs={{0,5},{1,4},{2,7},{3,6},{4,1},{5,0},{6,3},{7,2},{8,13},{9,12},{10,... | collective-permute-start | bytes 147464 | tf_op jit(solution)/shard_map/ppermute | solution.py:40
  19.5 0.1 iota_compare_fusion.1
  19.6 0.1 eq.83
  19.7 4.1 %collective-permute-done.2 = f32[2,3,16,128]{3,2,1,0:T(8,128)S(1)} collective-permute-done((f32[2,3,16,128]{3,2,1,0:T(8,128)S(1)}, f32[2,3,16,128]{3,2,1,0:T(8,128)S(1)}, u32[]{:S(2)}, u32[]{:S(2)}) %collective-permute-start.2) | collective-permute-done | bytes 49184 | tf_op jit(solution)/shard_map/ppermute | solution.py:40
  23.8 0.1 bitcast_select_fusion.1
  23.8 0.6 all-to-all-done
  24.4 0.1 convert_reduce_fusion
  24.6 2.7 %collective-permute-start.3 = (f32[8,16,128]{2,1,0:T(8,128)S(1)}, f32[8,16,128]{2,1,0:T(8,128)S(1)}, u32[]{:S(2)}, u32[]{:S(2)}) collective-permute-start(f32[8,16,128]{2,1,0:T(8,128)S(1)} %dynamic-slice_bitcast_fusion), channel_id=1, source_target_pairs={{0,1},{1,0},{2,3},{3,2},{4,5},{5,4},{6,7},{7,6},{8,9},{9,8},{10,11... | collective-permute-start | bytes 196616 | tf_op jit(solution)/shard_map/ppermute | solution.py:34
  27.3 0.1 broadcast_in_dim.153
  27.4 0.1 broadcast_in_dim.154
  27.4 0.1 broadcast_in_dim.151
  27.5 0.1 broadcast_in_dim.152
  27.6 0.6 collective-permute-done.3
  28.2 2.0 %collective-permute-start.4 = (f32[128,128]{1,0:T(8,128)S(1)}, f32[128,128]{1,0:T(8,128)S(1)}, u32[]{:S(2)}, u32[]{:S(2)}) collective-permute-start(f32[128,128]{1,0:T(8,128)S(1)} %bitcast.35), channel_id=1, source_target_pairs={{0,3},{1,2},{2,1},{3,0},{4,7},{5,6},{6,5},{7,4},{8,11},{9,10},{10,... | collective-permute-start | bytes 196616 | tf_op jit(solution)/shard_map/ppermute | solution.py:40
  30.2 0.1 collective-permute-start.6
  30.3 2.1 %collective-permute-done.4 = f32[128,128]{1,0:T(8,128)S(1)} collective-permute-done((f32[128,128]{1,0:T(8,128)S(1)}, f32[128,128]{1,0:T(8,128)S(1)}, u32[]{:S(2)}, u32[]{:S(2)}) %collective-permute-start.4) | collective-permute-done | bytes 65568 | tf_op jit(solution)/shard_map/ppermute | solution.py:40
  32.4 3.4 %collective-permute-start.5 = (f32[128,128]{1,0:T(8,128)S(1)}, f32[128,128]{1,0:T(8,128)S(1)}, u32[]{:S(2)}, u32[]{:S(2)}) collective-permute-start(f32[128,128]{1,0:T(8,128)S(1)} %add.52), channel_id=1, source_target_pairs={{0,5},{1,4},{2,7},{3,6},{4,1},{5,0},{6,3},{7,2},{8,13},{9,12},{10,... | collective-permute-start | bytes 196616 | tf_op jit(solution)/shard_map/ppermute | solution.py:40
  35.8 0.1 iota_compare_fusion
  35.9 0.1 eq.88
  35.9 0.0 collective-permute-done.6
  35.9 0.1 bitcast_select_fusion.states
  36.0 1.8 %collective-permute-done.5 = f32[128,128]{1,0:T(8,128)S(1)} collective-permute-done((f32[128,128]{1,0:T(8,128)S(1)}, f32[128,128]{1,0:T(8,128)S(1)}, u32[]{:S(2)}, u32[]{:S(2)}) %collective-permute-start.5) | collective-permute-done | bytes 65568 | tf_op jit(solution)/shard_map/ppermute | solution.py:40
  37.8 5.8 %collective-permute-start.7 = (f32[128,128]{1,0:T(8,128)S(1)}, f32[128,128]{1,0:T(8,128)S(1)}, u32[]{:S(2)}, u32[]{:S(2)}) collective-permute-start(f32[128,128]{1,0:T(8,128)S(1)} %add.53), channel_id=1, source_target_pairs={{0,13},{1,12},{2,15},{3,14},{4,9},{5,8},{6,11},{7,10},{8,5},{9,4},... | collective-permute-start | bytes 196616 | tf_op jit(solution)/shard_map/ppermute | solution.py:40
  43.6 2.8 %collective-permute-done.7 = f32[128,128]{1,0:T(8,128)S(1)} collective-permute-done((f32[128,128]{1,0:T(8,128)S(1)}, f32[128,128]{1,0:T(8,128)S(1)}, u32[]{:S(2)}, u32[]{:S(2)}) %collective-permute-start.7) | collective-permute-done | bytes 65568 | tf_op jit(solution)/shard_map/ppermute | solution.py:40
  46.4 10.2 %all_to_all.15 = f32[32,1,128]{2,1,0:T(1,128)S(1)} all-to-all(f32[32,1,128]{2,1,0:T(1,128)S(1)} %broadcast_in_dim.160), channel_id=1, replica_groups=mesh['y'=4,'x'=4,'z'=8,'c'=2] {'y','x','c'}, dimensions={0} | all-to-all | bytes 32768 | tf_op jit(solution)/shard_map/all_to_all | solution.py:26
  56.6 0.2 shard_map.109
  56.8 13.2 %all_to_all.16 = bf16[16,128,128]{2,1,0:T(8,128)(2,1)S(1)} all-to-all(bf16[16,128,128]{2,1,0:T(8,128)(2,1)S(1)} %get-tuple-element.39), channel_id=1, replica_groups=mesh['y'=4,'x'=4,'z'=8,'c'=2] {'y','x'}, dimensions={0} | all-to-all | bytes 1048576 | tf_op jit(solution)/shard_map/all_to_all | solution.py:26
  70.0 2.0 %collective-permute-start.9 = (f32[16,128]{1,0:T(8,128)S(1)}, f32[16,128]{1,0:T(8,128)S(1)}, u32[]{:S(2)}, u32[]{:S(2)}) collective-permute-start(f32[16,128]{1,0:T(8,128)S(1)} %constant_dynamic-slice_fusion), channel_id=1, source_target_pairs={{0,1},{1,0},{2,3},{3,2},{4,5},{5,4},{6,7},{7,6},{8,9},{9,8},{10,11... | collective-permute-start | bytes 24584 | tf_op jit(solution)/shard_map/ppermute | solution.py:34
  72.0 0.1 collective-permute-start.8
  72.1 0.8 %shard_map.110.refs_0_ = bf16[16,8,2,16,128]{4,3,2,1,0:T(8,128)(2,1)} custom-call(bf16[16,8,16,128]{3,2,1,0:T(8,128)(2,1)S(1)} %bitcast.29), custom_call_target="tpu_custom_call" | custom-call | tf_op jit(solution)/shard_map/pallas_call | solution.py:93
  72.9 0.0 collective-permute-done.9
  72.9 0.1 abs_reduce_fusion.1
  73.1 0.0 copy-start.5
  73.1 0.0 copy-start.6
  73.1 0.7 divide_convert_fusion
  73.8 0.2 collective-permute-done.8.half
  73.9 0.8 %shard_map.111 = bf16[16,8,2,16,128]{4,3,2,1,0:T(8,128)(2,1)} custom-call(bf16[16,8,16,128]{3,2,1,0:T(8,128)(2,1)S(1)} %collective-permute-done.8.half, bf16[16,8,2,16,128]{4,3,2,1,0:T(8,128)(2,1)} %shard_map.110.refs_0_), custom_call_target="tpu_custom_call", output_to_operand_aliasing={{}: (1, {})} | custom-call | tf_op jit(solution)/shard_map/pallas_call | solution.py:93
  74.7 0.0 copy-done.5
  74.7 0.0 copy-done.6
  (25 shorter events, 0.1 us)
Async XLA Ops:
  0.6 7.8 %copy-start.1 = (bf16[16,128]{1,0:T(8,128)(2,1)S(1)}, bf16[16,128]{1,0:T(8,128)(2,1)}, u32[]{:S(2)}) copy-start(bf16[16,128]{1,0:T(8,128)(2,1)} %param.10) | copy-start | bytes 12292
  0.6 7.8 %copy-start.2 = (bf16[16,128]{1,0:T(8,128)(2,1)S(1)}, bf16[16,128]{1,0:T(8,128)(2,1)}, u32[]{:S(2)}) copy-start(bf16[16,128]{1,0:T(8,128)(2,1)} %param.8) | copy-start | bytes 12292
  0.7 7.8 %copy-start.3 = (f32[16]{0:T(128)S(1)}, f32[16]{0:T(128)}, u32[]{:S(2)}) copy-start(f32[16]{0:T(128)} %param.11) | copy-start | bytes 196
  0.7 7.8 %copy-start.4 = (f32[16]{0:T(128)S(1)}, f32[16]{0:T(128)}, u32[]{:S(2)}) copy-start(f32[16]{0:T(128)} %param.9) | copy-start | bytes 196
  0.7 7.9 %copy-start = (f32[16,128]{1,0:T(8,128)S(1)}, f32[16,128]{1,0:T(8,128)}, u32[]{:S(2)}) copy-start(f32[16,128]{1,0:T(8,128)} %param.7) | copy-start | bytes 24580
  0.7 23.8 %all-to-all-start = ((bf16[16,256,128]{2,1,0:T(8,128)(2,1)}), bf16[16,256,128]{2,1,0:T(8,128)(2,1)S(1)}, u32[]{:S(2)}, u32[]{:S(2)}) async-start(bf16[16,256,128]{2,1,0:T(8,128)(2,1)} %bitcast.32), calls=%async_computation | async-start | bytes 2097152 | tf_op jit(solution)/shard_map/all_to_all | solution.py:26
  8.5 1.9 %collective-permute-start = (f32[3,16,128]{2,1,0:T(8,128)S(1)}, f32[3,16,128]{2,1,0:T(8,128)S(1)}, u32[]{:S(2)}, u32[]{:S(2)}) collective-permute-start(f32[3,16,128]{2,1,0:T(8,128)S(1)} %pad_maximum_fusion), channel_id=1, source_target_pairs={{0,1},{1,0},{2,3},{3,2},{4,5},{5,4},{6,7},{7,6},{8,9},{9,8},{10,11... | collective-permute-start | bytes 73736 | tf_op jit(solution)/shard_map/ppermute | solution.py:34
  10.4 8.1 %collective-permute-start.1 = (f32[1,3,16,128]{3,2,1,0:T(8,128)S(1)}, f32[1,3,16,128]{3,2,1,0:T(8,128)S(1)}, u32[]{:S(2)}, u32[]{:S(2)}) collective-permute-start(f32[1,3,16,128]{3,2,1,0:T(8,128)S(1)} %fusion.4), channel_id=1, source_target_pairs={{0,13},{1,12},{2,15},{3,14},{4,9},{5,8},{6,11},{7,10},{8,5},{9,4},... | collective-permute-start | bytes 73736 | tf_op jit(solution)/shard_map/ppermute | solution.py:40
  18.6 5.2 %collective-permute-start.2 = (f32[2,3,16,128]{3,2,1,0:T(8,128)S(1)}, f32[2,3,16,128]{3,2,1,0:T(8,128)S(1)}, u32[]{:S(2)}, u32[]{:S(2)}) collective-permute-start(f32[2,3,16,128]{3,2,1,0:T(8,128)S(1)} %broadcast_select_fusion), channel_id=1, source_target_pairs={{0,5},{1,4},{2,7},{3,6},{4,1},{5,0},{6,3},{7,2},{8,13},{9,12},{10,... | collective-permute-start | bytes 147464 | tf_op jit(solution)/shard_map/ppermute | solution.py:40
  24.6 3.6 %collective-permute-start.3 = (f32[8,16,128]{2,1,0:T(8,128)S(1)}, f32[8,16,128]{2,1,0:T(8,128)S(1)}, u32[]{:S(2)}, u32[]{:S(2)}) collective-permute-start(f32[8,16,128]{2,1,0:T(8,128)S(1)} %dynamic-slice_bitcast_fusion), channel_id=1, source_target_pairs={{0,1},{1,0},{2,3},{3,2},{4,5},{5,4},{6,7},{7,6},{8,9},{9,8},{10,11... | collective-permute-start | bytes 196616 | tf_op jit(solution)/shard_map/ppermute | solution.py:34
  28.2 4.1 %collective-permute-start.4 = (f32[128,128]{1,0:T(8,128)S(1)}, f32[128,128]{1,0:T(8,128)S(1)}, u32[]{:S(2)}, u32[]{:S(2)}) collective-permute-start(f32[128,128]{1,0:T(8,128)S(1)} %bitcast.35), channel_id=1, source_target_pairs={{0,3},{1,2},{2,1},{3,0},{4,7},{5,6},{6,5},{7,4},{8,11},{9,10},{10,... | collective-permute-start | bytes 196616 | tf_op jit(solution)/shard_map/ppermute | solution.py:40
  30.2 5.8 %collective-permute-start.6 = (f32[4,3,16,128]{3,2,1,0:T(8,128)S(1)}, f32[4,3,16,128]{3,2,1,0:T(8,128)S(1)}, u32[]{:S(2)}, u32[]{:S(2)}) collective-permute-start(f32[4,3,16,128]{3,2,1,0:T(8,128)S(1)} %bitcast_select_fusion.1), channel_id=1, source_target_pairs={{0,3},{1,2},{2,1},{3,0},{4,7},{5,6},{6,5},{7,4},{8,11},{9,10},{10,... | collective-permute-start | bytes 294920 | tf_op jit(solution)/shard_map/ppermute | solution.py:40
  32.4 5.4 %collective-permute-start.5 = (f32[128,128]{1,0:T(8,128)S(1)}, f32[128,128]{1,0:T(8,128)S(1)}, u32[]{:S(2)}, u32[]{:S(2)}) collective-permute-start(f32[128,128]{1,0:T(8,128)S(1)} %add.52), channel_id=1, source_target_pairs={{0,5},{1,4},{2,7},{3,6},{4,1},{5,0},{6,3},{7,2},{8,13},{9,12},{10,... | collective-permute-start | bytes 196616 | tf_op jit(solution)/shard_map/ppermute | solution.py:40
  37.8 8.5 %collective-permute-start.7 = (f32[128,128]{1,0:T(8,128)S(1)}, f32[128,128]{1,0:T(8,128)S(1)}, u32[]{:S(2)}, u32[]{:S(2)}) collective-permute-start(f32[128,128]{1,0:T(8,128)S(1)} %add.53), channel_id=1, source_target_pairs={{0,13},{1,12},{2,15},{3,14},{4,9},{5,8},{6,11},{7,10},{8,5},{9,4},... | collective-permute-start | bytes 196616 | tf_op jit(solution)/shard_map/ppermute | solution.py:40
  70.0 2.9 %collective-permute-start.9 = (f32[16,128]{1,0:T(8,128)S(1)}, f32[16,128]{1,0:T(8,128)S(1)}, u32[]{:S(2)}, u32[]{:S(2)}) collective-permute-start(f32[16,128]{1,0:T(8,128)S(1)} %constant_dynamic-slice_fusion), channel_id=1, source_target_pairs={{0,1},{1,0},{2,3},{3,2},{4,5},{5,4},{6,7},{7,6},{8,9},{9,8},{10,11... | collective-permute-start | bytes 24584 | tf_op jit(solution)/shard_map/ppermute | solution.py:34
  72.0 1.9 %collective-permute-start.8 = (bf16[16,8,16,128]{3,2,1,0:T(8,128)(2,1)S(1)}, bf16[16,8,16,128]{3,2,1,0:T(8,128)(2,1)S(1)}, u32[]{:S(2)}, u32[]{:S(2)}) collective-permute-start(bf16[16,8,16,128]{3,2,1,0:T(8,128)(2,1)S(1)} %bitcast.28), channel_id=1, source_target_pairs={{0,1},{1,0},{2,3},{3,2},{4,5},{5,4},{6,7},{7,6},{8,9},{9,8},{10,11... | collective-permute-start | bytes 1572872 | tf_op jit(solution)/shard_map/ppermute | solution.py:34
  73.1 1.7 %copy-start.5 = (f32[16]{0:T(128)}, f32[16]{0:T(128)S(1)}, u32[]{:S(2)}) copy-start(f32[16]{0:T(128)S(1)} %broadcast_add_fusion.1) | copy-start | bytes 196
  73.1 1.7 %copy-start.6 = (f32[16]{0:T(128)}, f32[16]{0:T(128)S(1)}, u32[]{:S(2)}) copy-start(f32[16]{0:T(128)S(1)} %broadcast_add_fusion) | copy-start | bytes 196

commit v7 on v5

v7 whole, which is shorter than its diff:
```python
import functools
import math

import jax
import jax.numpy as jnp
from jax import lax
from jax.experimental import pallas as pl
from jax.experimental.pallas import tpu as pltpu
from jax.sharding import Mesh
from jax.sharding import PartitionSpec as P

DP = ("y", "x", "z", "c")
PARTS = 4


beta_one = 0.9
beta_two = 0.95
learn_rate = 0.05
decay_rate = 0.1
adam_epsilon = 1e-08
clip_rms = 0.01
first_fix = 1.0 - 0.9**10
second_fix = 1.0 - 0.95**10


def exchange(x, axes):
    return lax.all_to_all(x, axes, split_axis=0, concat_axis=0, tiled=True)


def sent_to_all(x, axes):
    return exchange(jnp.broadcast_to(x, (lax.axis_size(axes), *x.shape)), axes)


def swapped(x):
    return lax.ppermute(x, "c", [(0, 1), (1, 0)])


def from_partner(x, flip):
    return lax.ppermute(x, "z", [(z, z ^ flip) for z in range(lax.axis_size("z"))])


FLIPS = ((1, 0), (2, 1), (6, 2))


def doubled(x, place, step):
    flip, level = step
    other = from_partner(x, flip)
    mine = jnp.arange(2) == (place[:, None] >> level & 1)
    place = jnp.where(mine, place[:, None], place[:, None] ^ flip).reshape(-1)
    x = jnp.where(mine[:, :, None, None, None], x[:, None], other[:, None])
    return x.reshape(-1, *x.shape[2:]), place


def advance(clipped, master, first, second):
    first_new = beta_one * first + (1.0 - beta_one) * clipped
    second_new = beta_two * second + (1.0 - beta_two) * clipped * clipped
    change = first_new / first_fix / (jnp.sqrt(second_new / second_fix) + adam_epsilon)
    master_new = master * (1.0 - learn_rate * decay_rate) - learn_rate * change
    return master_new, first_new, second_new


def clip_and_advance(limit, norms, total, states, weights, factors):
    squares = jnp.sum(norms[...], axis=0)
    factor = jnp.minimum(1.0, limit / (jnp.sqrt(jnp.sum(squares, axis=1, keepdims=True)) + 1e-06))
    factors[...] = jnp.broadcast_to(factor, factors.shape)
    line, _, rows, width = states.shape
    for z in range(line):
        place = pl.ds(z * rows, rows)
        new, _, _ = advance(factor * total[place], states[z, 0], states[z, 1], states[z, 2])
        new = new.astype(weights.dtype)
        for plane in range(weights.shape[0]):
            weights[plane, place] = new


def copies_of_half(half, out, other, sent):
    side = lax.axis_index("c") ^ other
    planes = half.shape[0] // PARTS
    spans = [pl.ds(part * planes, planes) for part in range(PARTS)]
    return [
        pltpu.make_async_copy(half.at[span], out.at[span, :, side], sent.at[part])
        for part, span in enumerate(spans)
    ]


def lay_and_advance(half, factor, total, states, out, *refs):
    results, held, sent = refs[:5], refs[5:10], refs[10]
    copies = copies_of_half(half, out, 0, sent)
    for copy in copies:
        copy.start()

    rows = states.shape[2]
    z = lax.axis_index("z")
    own = total[pl.ds(pl.multiple_of(z * rows, rows), rows)]
    held[0][...], *new = advance(factor[:1] * own, states[z, 0], states[z, 1], states[z, 2])
    square = (rows, rows)
    diagonal = lax.broadcasted_iota(jnp.int32, square, 0) == lax.broadcasted_iota(jnp.int32, square, 1)
    for moment, quotient, scale in zip(new, held[1::2], held[2::2]):
        largest = jnp.max(jnp.abs(moment), axis=1, keepdims=True) + 1e-08
        quotient[...] = (moment / largest).astype(quotient.dtype)
        scale[...] = jnp.sum(jnp.where(diagonal, largest, 0.0), axis=0, keepdims=True)
    for i, (result, kept) in enumerate(zip(results, held)):
        copies.append(pltpu.make_async_copy(kept, result, sent.at[PARTS + i]))
        copies[-1].start()
    for copy in copies:
        copy.wait()


def lay_other(half, _, out, sent):
    copies = copies_of_half(half, out, 1, sent)
    for copy in copies:
        copy.start()
    for copy in copies:
        copy.wait()


def shards(grads, master, first_q, first_scale, second_q, second_scale):
    blocks, width = grads.shape[1:]
    rows = master.shape[0]
    planes, line, cores = lax.axis_size(("y", "x")), lax.axis_size("z"), lax.axis_size("c")
    held = line * rows
    first = first_q.astype(jnp.float32) * first_scale[:, None]
    second = second_q.astype(jnp.float32) * second_scale[:, None]

    here = lax.axis_index("c")

    arrived = exchange(grads[0].reshape(planes, line * cores * rows, width), ("y", "x"))
    states = jnp.stack([master, first, second])[None]
    place = lax.axis_index("z")[None]
    for step in FLIPS[:0:-1]:
        states, place = doubled(states, place, step)
    arrived, states = lax.optimization_barrier((arrived, states))
    both = arrived.astype(jnp.float32).sum(axis=0).reshape(line, cores, rows, width)
    kept, sent = (lax.dynamic_index_in_dim(both, i, 1, False) for i in (here, 1 - here))
    part = (kept + swapped(sent)).reshape(held, width)

    total, states = lax.optimization_barrier((part, states))
    (last, _), *middle = FLIPS[::-1]
    whole, _ = doubled(states, place, FLIPS[0])
    for flip, _ in middle[::-1]:
        total = total + from_partner(total, flip)
    total, states = lax.optimization_barrier((total, whole))
    total = total + from_partner(total, last)
    norms = sent_to_all(jnp.sum(total * total, axis=0, keepdims=True), ("y", "x", "c"))
    norms, total, states = lax.optimization_barrier((norms, total, states))
    small = pltpu.CompilerParams(vmem_limit_bytes=4 << 20)
    weights, factor = pl.pallas_call(
        functools.partial(clip_and_advance, clip_rms * math.sqrt(blocks * width)),
        out_shape=(
            jax.ShapeDtypeStruct((planes, held, width), jnp.bfloat16),
            jax.ShapeDtypeStruct((8, width), jnp.float32),
        ),
        compiler_params=small,
    )(norms, total, states)

    weights, factor, total, states = lax.optimization_barrier(
        (exchange(weights, ("y", "x")), factor, total, states)
    )
    weights = weights.reshape(planes, line, rows, width)
    partner = swapped(weights)
    whole = jax.ShapeDtypeStruct((planes, line, cores, rows, width), jnp.bfloat16)
    own, scale = (rows, width), (1, rows)
    results = [(own, jnp.float32)] + [(own, jnp.bfloat16), (scale, jnp.float32)] * 2
    vmem, anywhere = (pl.BlockSpec(memory_space=space) for space in (pltpu.VMEM, pl.ANY))
    weights, *results = pl.pallas_call(
        lay_and_advance,
        out_shape=[whole] + [jax.ShapeDtypeStruct(*result) for result in results],
        in_specs=[vmem] * 4,
        out_specs=[anywhere] * 6,
        scratch_shapes=[pltpu.VMEM(*result) for result in results] + [pltpu.SemaphoreType.DMA((PARTS + 5,))],
        compiler_params=small,
    )(weights, factor, total, states)
    weights = pl.pallas_call(
        lay_other,
        out_shape=whole,
        in_specs=[vmem, anywhere],
        out_specs=anywhere,
        scratch_shapes=[pltpu.SemaphoreType.DMA((PARTS,))],
        input_output_aliases={1: 0},
        compiler_params=small,
    )(partner, weights)
    master_new, first_q_new, first_scale_new, second_q_new, second_scale_new = results
    weights = weights.reshape(blocks, width)
    return (weights, master_new, first_q_new, first_scale_new[0], second_q_new, second_scale_new[0])


def solution(mesh):
    torus = Mesh(mesh.devices.reshape(4, 4, 8, 2), DP)
    in_specs = (P(DP, None, None), P(DP, None), P(DP, None), P(DP), P(DP, None), P(DP))
    out_specs = (P(), P(DP, None), P(DP, None), P(DP), P(DP, None), P(DP))
    return jax.shard_map(
        shards, mesh=torus, in_specs=in_specs, out_specs=out_specs, check_vma=False
    )
```

time: 79.7 us -> 75.5 us (0.947)
  blocking collectives: 16.4 us -> 26.6 us
  starting transfers between devices: 38.7 us -> 29.4 us
  waiting for transfers between devices: 18.8 us -> 15.3 us
  other arithmetic: 3 us -> 0.68 us
  Pallas kernels: 0.22 us -> 1.89 us
  local copies, waits for them, and re-layouts: 1.4 us -> 0.53 us
    all_to_all x1 -> x2, blocking collectives: 16.4 us -> 26.6 us  [exchange(): return lax.all_to_all(x, axes, split_axis=0, concat_axis=0, tiled=True)]
    ppermute x6, waiting for transfers between devices: 15.2 us -> 10.1 us  [from_partner(): lax.ppermute(x, 'z', [(z, z ^ flip) for z in range(lax.axis_size('z'))])]
    ppermute x6, starting transfers between devices: 21.5 us -> 17 us  [from_partner(): lax.ppermute(x, 'z', [(z, z ^ flip) for z in range(lax.axis_size('z'))])]
    all_to_all x2 -> x1, starting transfers between devices: 11.6 us -> 7.72 us  [exchange(): return lax.all_to_all(x, axes, split_axis=0, concat_axis=0, tiled=True)]
    all_to_all x2 -> x1, waiting for transfers between devices: 1.28 us -> 3.97 us  [exchange(): return lax.all_to_all(x, axes, split_axis=0, concat_axis=0, tiled=True)]
    pallas_call x1 -> x3, Pallas kernels: 0.22 us -> 1.89 us  [the longest x1 0.88 us: shards(): pl.pallas_call(lay_and_advance, out_shape=[whole] + [jax.ShapeDtypeStruct...]
    select_n x3 -> x0, other arithmetic: 1.49 us -> none  [the longest x1 1.48 us: shards(): jnp.where(mine[:, None, None], weights, swapped(weights))]
    ppermute x4 -> x2, waiting for transfers between devices: 2.32 us -> 1.25 us  [swapped(): return lax.ppermute(x, 'c', [(0, 1), (1, 0)])]
  transfers between devices with their start and end apart: 12 -> 9, of which waited for: 11 -> 8; matrix products, arithmetic and copies ran while one was open for 3% -> 1% of each run, Pallas kernels for 0% -> 1%
where the time goes in v7:
time: 75.5 us; the launch traced here: 75.2 us
  starting transfers between devices  29.4 us (39%)
  blocking collectives  26.6 us (35%)
  waiting for transfers between devices  15.3 us (20%)
  Pallas kernels  1.89 us (3%)
  between operations  0.78 us (1%)
    all_to_all x2, blocking collectives, exchange(): return lax.all_to_all(x, axes, split_axis=0, concat_axis=0, tiled=True)  26.6 us
    ppermute x6, starting transfers between devices, from_partner(): lax.ppermute(x, 'z', [(z, z ^ flip) for z in range(lax.axis_size('z'))])  17 us
    ppermute x6, waiting for transfers between devices, from_partner(): lax.ppermute(x, 'z', [(z, z ^ flip) for z in range(lax.axis_size('z'))])  10.1 us
    all_to_all x1, starting transfers between devices, exchange(): return lax.all_to_all(x, axes, split_axis=0, concat_axis=0, tiled=True)  7.72 us
    ppermute x2, starting transfers between devices, swapped(): return lax.ppermute(x, 'c', [(0, 1), (1, 0)])  4.72 us
    all_to_all x1, waiting for transfers between devices, exchange(): return lax.all_to_all(x, axes, split_axis=0, concat_axis=0, tiled=True)  3.97 us
  transfers between devices with their start and end apart: 9, of which 8 were waited for; matrix products, arithmetic and copies ran while one was open for 1% of the time, Pallas kernels for 1%

profile of v7, /device:TPU:1, one launch (start us, length us, event | category | flops | bytes accessed | tf_op | source)
XLA Modules:
  0.0 75.2 jit_solution(8465522052575609101)
XLA Ops:
  0.6 0.0 copy-start.1
  0.6 0.0 copy-start.2
  0.7 0.0 copy-start.3
  0.7 0.0 copy-start.4
  0.7 0.0 copy-start
  0.7 7.7 %all-to-all-start = ((bf16[16,256,128]{2,1,0:T(8,128)(2,1)}), bf16[16,256,128]{2,1,0:T(8,128)(2,1)S(1)}, u32[]{:S(2)}, u32[]{:S(2)}) async-start(bf16[16,256,128]{2,1,0:T(8,128)(2,1)} %bitcast.29), calls=%async_computation | async-start | bytes 2097152 | tf_op jit(solution)/shard_map/all_to_all | solution.py:27
  8.4 0.0 copy-done.1
  8.4 0.0 copy-done.2
  8.4 0.0 copy-done.3
  8.4 0.0 copy-done.4
  8.4 0.1 multiply_bitcast_fusion
  8.5 0.0 copy-done
  8.5 6.1 %collective-permute-start = (f32[1,3,16,128]{3,2,1,0:T(8,128)S(1)}, f32[1,3,16,128]{3,2,1,0:T(8,128)S(1)}, u32[]{:S(2)}, u32[]{:S(2)}) collective-permute-start(f32[1,3,16,128]{3,2,1,0:T(8,128)S(1)} %get-tuple-element.53), channel_id=1, source_target_pairs={{0,12},{2,14},{4,8},{6,10},{8,4},{10,6},{12,0},{14,2},{1,13},{3,15... | collective-permute-start | bytes 73736 | tf_op jit(solution)/shard_map/ppermute | solution.py:39
  14.7 1.5 %collective-permute-done = f32[1,3,16,128]{3,2,1,0:T(8,128)S(1)} collective-permute-done((f32[1,3,16,128]{3,2,1,0:T(8,128)S(1)}, f32[1,3,16,128]{3,2,1,0:T(8,128)S(1)}, u32[]{:S(2)}, u32[]{:S(2)}) %collective-permute-start) | collective-permute-done | bytes 24608 | tf_op jit(solution)/shard_map/ppermute | solution.py:39
  16.2 0.1 broadcast_select_fusion
  16.2 0.9 %collective-permute-start.1 = (f32[2,3,16,128]{3,2,1,0:T(8,128)S(1)}, f32[2,3,16,128]{3,2,1,0:T(8,128)S(1)}, u32[]{:S(2)}, u32[]{:S(2)}) collective-permute-start(f32[2,3,16,128]{3,2,1,0:T(8,128)S(1)} %broadcast_select_fusion), channel_id=1, source_target_pairs={{0,4},{2,6},{4,0},{6,2},{8,12},{10,14},{12,8},{14,10},{1,5},{3,7},... | collective-permute-start | bytes 147464 | tf_op jit(solution)/shard_map/ppermute | solution.py:39
  17.1 0.1 iota_compare_fusion.1
  17.2 0.1 eq.77
  17.3 3.1 %collective-permute-done.1 = f32[2,3,16,128]{3,2,1,0:T(8,128)S(1)} collective-permute-done((f32[2,3,16,128]{3,2,1,0:T(8,128)S(1)}, f32[2,3,16,128]{3,2,1,0:T(8,128)S(1)}, u32[]{:S(2)}, u32[]{:S(2)}) %collective-permute-start.1) | collective-permute-done | bytes 49184 | tf_op jit(solution)/shard_map/ppermute | solution.py:39
  20.4 0.1 bitcast_select_fusion.1
  20.5 4.0 %all-to-all-done = bf16[16,256,128]{2,1,0:T(8,128)(2,1)S(1)} async-done(((bf16[16,256,128]{2,1,0:T(8,128)(2,1)}), bf16[16,256,128]{2,1,0:T(8,128)(2,1)S(1)}, u32[]{:S(2)}, u32[]{:S(2)}) %all-to-all-start) | async-done | bytes 1048608 | tf_op jit(solution)/shard_map/all_to_all | solution.py:27
  24.4 0.1 convert_reduce_fusion
  24.6 2.7 %collective-permute-start.2 = (f32[8,16,128]{2,1,0:T(8,128)S(1)}, f32[8,16,128]{2,1,0:T(8,128)S(1)}, u32[]{:S(2)}, u32[]{:S(2)}) collective-permute-start(f32[8,16,128]{2,1,0:T(8,128)S(1)} %dynamic-slice_bitcast_fusion), channel_id=1, source_target_pairs={{0,1},{1,0},{2,3},{3,2},{4,5},{5,4},{6,7},{7,6},{8,9},{9,8},{10,11... | collective-permute-start | bytes 196616 | tf_op jit(solution)/shard_map/ppermute | solution.py:35
  27.3 0.1 broadcast_in_dim.151
  27.4 0.1 broadcast_in_dim.152
  27.4 0.1 broadcast_in_dim.149
  27.5 0.1 broadcast_in_dim.150
  27.6 0.6 collective-permute-done.2
  28.2 1.7 %collective-permute-start.3 = (f32[128,128]{1,0:T(8,128)S(1)}, f32[128,128]{1,0:T(8,128)S(1)}, u32[]{:S(2)}, u32[]{:S(2)}) collective-permute-start(f32[128,128]{1,0:T(8,128)S(1)} %bitcast.33), channel_id=1, source_target_pairs={{0,2},{2,0},{4,6},{6,4},{8,10},{10,8},{12,14},{14,12},{1,3},{3,1},... | collective-permute-start | bytes 196616 | tf_op jit(solution)/shard_map/ppermute | solution.py:39
  29.9 0.1 collective-permute-start.5
  30.0 1.9 %collective-permute-done.3 = f32[128,128]{1,0:T(8,128)S(1)} collective-permute-done((f32[128,128]{1,0:T(8,128)S(1)}, f32[128,128]{1,0:T(8,128)S(1)}, u32[]{:S(2)}, u32[]{:S(2)}) %collective-permute-start.3) | collective-permute-done | bytes 65568 | tf_op jit(solution)/shard_map/ppermute | solution.py:39
  32.0 3.1 %collective-permute-start.4 = (f32[128,128]{1,0:T(8,128)S(1)}, f32[128,128]{1,0:T(8,128)S(1)}, u32[]{:S(2)}, u32[]{:S(2)}) collective-permute-start(f32[128,128]{1,0:T(8,128)S(1)} %add.23), channel_id=1, source_target_pairs={{0,4},{2,6},{4,0},{6,2},{8,12},{10,14},{12,8},{14,10},{1,5},{3,7},... | collective-permute-start | bytes 196616 | tf_op jit(solution)/shard_map/ppermute | solution.py:39
  35.0 0.1 iota_compare_fusion
  35.1 0.1 eq.81
  35.2 0.0 collective-permute-done.5
  35.2 0.1 bitcast_select_fusion.states
  35.3 1.4 %collective-permute-done.4 = f32[128,128]{1,0:T(8,128)S(1)} collective-permute-done((f32[128,128]{1,0:T(8,128)S(1)}, f32[128,128]{1,0:T(8,128)S(1)}, u32[]{:S(2)}, u32[]{:S(2)}) %collective-permute-start.4) | collective-permute-done | bytes 65568 | tf_op jit(solution)/shard_map/ppermute | solution.py:39
  36.7 5.0 %collective-permute-start.6 = (f32[128,128]{1,0:T(8,128)S(1)}, f32[128,128]{1,0:T(8,128)S(1)}, u32[]{:S(2)}, u32[]{:S(2)}) collective-permute-start(f32[128,128]{1,0:T(8,128)S(1)} %add.24), channel_id=1, source_target_pairs={{0,12},{2,14},{4,8},{6,10},{8,4},{10,6},{12,0},{14,2},{1,13},{3,15... | collective-permute-start | bytes 196616 | tf_op jit(solution)/shard_map/ppermute | solution.py:39
  41.7 2.2 %collective-permute-done.6 = f32[128,128]{1,0:T(8,128)S(1)} collective-permute-done((f32[128,128]{1,0:T(8,128)S(1)}, f32[128,128]{1,0:T(8,128)S(1)}, u32[]{:S(2)}, u32[]{:S(2)}) %collective-permute-start.6) | collective-permute-done | bytes 65568 | tf_op jit(solution)/shard_map/ppermute | solution.py:39
  44.0 13.4 %all_to_all.15.norms = f32[32,1,128]{2,1,0:T(1,128)S(1)} all-to-all(f32[32,1,128]{2,1,0:T(1,128)S(1)} %broadcast_in_dim.158), channel_id=1, replica_groups=mesh['y'=4,'x'=4,'z'=8,'c'=2] {'y','x','c'}, dimensions={0} | all-to-all | bytes 32768 | tf_op jit(solution)/shard_map/all_to_all | solution.py:27
  57.4 0.2 shard_map.109
  57.6 13.2 %all_to_all.16 = bf16[16,128,128]{2,1,0:T(8,128)(2,1)S(1)} all-to-all(bf16[16,128,128]{2,1,0:T(8,128)(2,1)S(1)} %get-tuple-element.36), channel_id=1, replica_groups=mesh['y'=4,'x'=4,'z'=8,'c'=2] {'y','x'}, dimensions={0} | all-to-all | bytes 1048576 | tf_op jit(solution)/shard_map/all_to_all | solution.py:27
  70.8 2.0 %collective-permute-start.7 = (bf16[16,8,16,128]{3,2,1,0:T(8,128)(2,1)S(1)}, bf16[16,8,16,128]{3,2,1,0:T(8,128)(2,1)S(1)}, u32[]{:S(2)}, u32[]{:S(2)}) collective-permute-start(bf16[16,8,16,128]{3,2,1,0:T(8,128)(2,1)S(1)} %bitcast.27), channel_id=1, source_target_pairs={{0,1},{1,0},{2,3},{3,2},{4,5},{5,4},{6,7},{7,6},{8,9},{9,8},{10,11... | collective-permute-start | bytes 1572872 | tf_op jit(solution)/shard_map/ppermute | solution.py:35
  72.8 0.9 %shard_map.110 = (bf16[16,8,2,16,128]{4,3,2,1,0:T(8,128)(2,1)}, f32[16,128]{1,0:T(8,128)}, bf16[16,128]{1,0:T(8,128)(2,1)}, f32[1,16]{1,0:T(1,128)}, bf16[16,128]{1,0:T(8,128)(2,1)}, /*index=5*/f32[1,16]{1,0:T(1,128)}) custom-call(bf16[16,8,16,128]{3,2,1,0:T(8,128)(2,1)S(1)} %bitcast.28, f32[8,128]{1,0:T(8,128)S(1)} %get-tuple-element.39.factor, ...), custom_call_target="tpu_custom_call" | custom-call | tf_op jit(solution)/shard_map/pallas_call | solution.py:164
  73.7 0.7 collective-permute-done.7.half
  74.4 0.8 %shard_map.111 = bf16[16,8,2,16,128]{4,3,2,1,0:T(8,128)(2,1)} custom-call(bf16[16,8,16,128]{3,2,1,0:T(8,128)(2,1)S(1)} %collective-permute-done.7.half, bf16[16,8,2,16,128]{4,3,2,1,0:T(8,128)(2,1)} %get-tuple-element.42._), custom_call_target="tpu_custom_call", output_to_operand_aliasing={{}: (1, {})} | custom-call | tf_op jit(solution)/shard_map/pallas_call | solution.py:172
  (11 shorter events, 0.1 us)
Async XLA Ops:
  0.6 7.8 %copy-start.1 = (bf16[16,128]{1,0:T(8,128)(2,1)S(1)}, bf16[16,128]{1,0:T(8,128)(2,1)}, u32[]{:S(2)}) copy-start(bf16[16,128]{1,0:T(8,128)(2,1)} %param.10) | copy-start | bytes 12292
  0.6 7.8 %copy-start.2 = (bf16[16,128]{1,0:T(8,128)(2,1)S(1)}, bf16[16,128]{1,0:T(8,128)(2,1)}, u32[]{:S(2)}) copy-start(bf16[16,128]{1,0:T(8,128)(2,1)} %param.8) | copy-start | bytes 12292
  0.7 7.8 %copy-start.3 = (f32[16]{0:T(128)S(1)}, f32[16]{0:T(128)}, u32[]{:S(2)}) copy-start(f32[16]{0:T(128)} %param.11) | copy-start | bytes 196
  0.7 7.8 %copy-start.4 = (f32[16]{0:T(128)S(1)}, f32[16]{0:T(128)}, u32[]{:S(2)}) copy-start(f32[16]{0:T(128)} %param.9) | copy-start | bytes 196
  0.7 7.9 %copy-start = (f32[16,128]{1,0:T(8,128)S(1)}, f32[16,128]{1,0:T(8,128)}, u32[]{:S(2)}) copy-start(f32[16,128]{1,0:T(8,128)} %param.7) | copy-start | bytes 24580
  0.7 23.8 %all-to-all-start = ((bf16[16,256,128]{2,1,0:T(8,128)(2,1)}), bf16[16,256,128]{2,1,0:T(8,128)(2,1)S(1)}, u32[]{:S(2)}, u32[]{:S(2)}) async-start(bf16[16,256,128]{2,1,0:T(8,128)(2,1)} %bitcast.29), calls=%async_computation | async-start | bytes 2097152 | tf_op jit(solution)/shard_map/all_to_all | solution.py:27
  8.5 7.6 %collective-permute-start = (f32[1,3,16,128]{3,2,1,0:T(8,128)S(1)}, f32[1,3,16,128]{3,2,1,0:T(8,128)S(1)}, u32[]{:S(2)}, u32[]{:S(2)}) collective-permute-start(f32[1,3,16,128]{3,2,1,0:T(8,128)S(1)} %get-tuple-element.53), channel_id=1, source_target_pairs={{0,12},{2,14},{4,8},{6,10},{8,4},{10,6},{12,0},{14,2},{1,13},{3,15... | collective-permute-start | bytes 73736 | tf_op jit(solution)/shard_map/ppermute | solution.py:39
  16.2 4.2 %collective-permute-start.1 = (f32[2,3,16,128]{3,2,1,0:T(8,128)S(1)}, f32[2,3,16,128]{3,2,1,0:T(8,128)S(1)}, u32[]{:S(2)}, u32[]{:S(2)}) collective-permute-start(f32[2,3,16,128]{3,2,1,0:T(8,128)S(1)} %broadcast_select_fusion), channel_id=1, source_target_pairs={{0,4},{2,6},{4,0},{6,2},{8,12},{10,14},{12,8},{14,10},{1,5},{3,7},... | collective-permute-start | bytes 147464 | tf_op jit(solution)/shard_map/ppermute | solution.py:39
  24.6 3.6 %collective-permute-start.2 = (f32[8,16,128]{2,1,0:T(8,128)S(1)}, f32[8,16,128]{2,1,0:T(8,128)S(1)}, u32[]{:S(2)}, u32[]{:S(2)}) collective-permute-start(f32[8,16,128]{2,1,0:T(8,128)S(1)} %dynamic-slice_bitcast_fusion), channel_id=1, source_target_pairs={{0,1},{1,0},{2,3},{3,2},{4,5},{5,4},{6,7},{7,6},{8,9},{9,8},{10,11... | collective-permute-start | bytes 196616 | tf_op jit(solution)/shard_map/ppermute | solution.py:35
  28.2 3.7 %collective-permute-start.3 = (f32[128,128]{1,0:T(8,128)S(1)}, f32[128,128]{1,0:T(8,128)S(1)}, u32[]{:S(2)}, u32[]{:S(2)}) collective-permute-start(f32[128,128]{1,0:T(8,128)S(1)} %bitcast.33), channel_id=1, source_target_pairs={{0,2},{2,0},{4,6},{6,4},{8,10},{10,8},{12,14},{14,12},{1,3},{3,1},... | collective-permute-start | bytes 196616 | tf_op jit(solution)/shard_map/ppermute | solution.py:39
  29.9 5.3 %collective-permute-start.5 = (f32[4,3,16,128]{3,2,1,0:T(8,128)S(1)}, f32[4,3,16,128]{3,2,1,0:T(8,128)S(1)}, u32[]{:S(2)}, u32[]{:S(2)}) collective-permute-start(f32[4,3,16,128]{3,2,1,0:T(8,128)S(1)} %bitcast_select_fusion.1), channel_id=1, source_target_pairs={{0,2},{2,0},{4,6},{6,4},{8,10},{10,8},{12,14},{14,12},{1,3},{3,1},... | collective-permute-start | bytes 294920 | tf_op jit(solution)/shard_map/ppermute | solution.py:39
  32.0 4.7 %collective-permute-start.4 = (f32[128,128]{1,0:T(8,128)S(1)}, f32[128,128]{1,0:T(8,128)S(1)}, u32[]{:S(2)}, u32[]{:S(2)}) collective-permute-start(f32[128,128]{1,0:T(8,128)S(1)} %add.23), channel_id=1, source_target_pairs={{0,4},{2,6},{4,0},{6,2},{8,12},{10,14},{12,8},{14,10},{1,5},{3,7},... | collective-permute-start | bytes 196616 | tf_op jit(solution)/shard_map/ppermute | solution.py:39
  36.7 7.2 %collective-permute-start.6 = (f32[128,128]{1,0:T(8,128)S(1)}, f32[128,128]{1,0:T(8,128)S(1)}, u32[]{:S(2)}, u32[]{:S(2)}) collective-permute-start(f32[128,128]{1,0:T(8,128)S(1)} %add.24), channel_id=1, source_target_pairs={{0,12},{2,14},{4,8},{6,10},{8,4},{10,6},{12,0},{14,2},{1,13},{3,15... | collective-permute-start | bytes 196616 | tf_op jit(solution)/shard_map/ppermute | solution.py:39
  70.8 3.6 %collective-permute-start.7 = (bf16[16,8,16,128]{3,2,1,0:T(8,128)(2,1)S(1)}, bf16[16,8,16,128]{3,2,1,0:T(8,128)(2,1)S(1)}, u32[]{:S(2)}, u32[]{:S(2)}) collective-permute-start(bf16[16,8,16,128]{3,2,1,0:T(8,128)(2,1)S(1)} %bitcast.27), channel_id=1, source_target_pairs={{0,1},{1,0},{2,3},{3,2},{4,5},{5,4},{6,7},{7,6},{8,9},{9,8},{10,11... | collective-permute-start | bytes 1572872 | tf_op jit(solution)/shard_map/ppermute | solution.py:35

commit v8 on v7

--- a/solution.py
+++ b/solution.py
@@ -134,12 +134,11 @@
     part = (kept + swapped(sent)).reshape(held, width)
 
     total, states = lax.optimization_barrier((part, states))
-    (last, _), *middle = FLIPS[::-1]
     whole, _ = doubled(states, place, FLIPS[0])
-    for flip, _ in middle[::-1]:
-        total = total + from_partner(total, flip)
-    total, states = lax.optimization_barrier((total, whole))
-    total = total + from_partner(total, last)
+    total = total + from_partner(total, 1)
+    others = [from_partner(total, flip) for flip in (2, 6, 4)]
+    others, states = lax.optimization_barrier((others, whole))
+    total = (total + others[0]) + (others[1] + others[2])
     norms = sent_to_all(jnp.sum(total * total, axis=0, keepdims=True), ("y", "x", "c"))
     norms, total, states = lax.optimization_barrier((norms, total, states))
     small = pltpu.CompilerParams(vmem_limit_bytes=4 << 20)

time: 75.5 us -> 75.3 us (level)
  waiting for transfers between devices: 15.3 us -> 16.1 us
    ppermute x6 -> x7, waiting for transfers between devices: 10.1 us -> 10.9 us  [from_partner(): lax.ppermute(x, 'z', [(z, z ^ flip) for z in range(lax.axis_size('z'))])]
    ppermute x6 -> x7, starting transfers between devices: 17 us -> 16.5 us  [from_partner(): lax.ppermute(x, 'z', [(z, z ^ flip) for z in range(lax.axis_size('z'))])]
  transfers between devices with their start and end apart: 9 -> 10, of which waited for: 8 -> 9; matrix products, arithmetic and copies ran while one was open for 1% -> 1% of each run, Pallas kernels for 1% -> 1%
where the time goes in v8:
time: 75.3 us; the launch traced here: 75 us
  starting transfers between devices  28.9 us (38%)
  blocking collectives  26.1 us (35%)
  waiting for transfers between devices  16.1 us (21%)
  Pallas kernels  1.89 us (3%)
  between operations  0.77 us (1%)
    all_to_all x2, blocking collectives, exchange(): return lax.all_to_all(x, axes, split_axis=0, concat_axis=0, tiled=True)  26.1 us
    ppermute x7, starting transfers between devices, from_partner(): lax.ppermute(x, 'z', [(z, z ^ flip) for z in range(lax.axis_size('z'))])  16.5 us
    ppermute x7, waiting for transfers between devices, from_partner(): lax.ppermute(x, 'z', [(z, z ^ flip) for z in range(lax.axis_size('z'))])  10.9 us
    all_to_all x1, starting transfers between devices, exchange(): return lax.all_to_all(x, axes, split_axis=0, concat_axis=0, tiled=True)  7.72 us
    ppermute x2, starting transfers between devices, swapped(): return lax.ppermute(x, 'c', [(0, 1), (1, 0)])  4.72 us
    all_to_all x1, waiting for transfers between devices, exchange(): return lax.all_to_all(x, axes, split_axis=0, concat_axis=0, tiled=True)  3.97 us
  transfers between devices with their start and end apart: 10, of which 9 were waited for; matrix products, arithmetic and copies ran while one was open for 1% of the time, Pallas kernels for 1%

profile of v8, /device:TPU:1, one launch (start us, length us, event | category | flops | bytes accessed | tf_op | source)
XLA Modules:
  0.0 75.0 jit_solution(6925262443587586152)
XLA Ops:
  0.6 0.0 copy-start.1
  0.6 0.0 copy-start.2
  0.7 0.0 copy-start.3
  0.7 0.0 copy-start.4
  0.7 0.0 copy-start
  0.7 7.7 %all-to-all-start = ((bf16[16,256,128]{2,1,0:T(8,128)(2,1)}), bf16[16,256,128]{2,1,0:T(8,128)(2,1)S(1)}, u32[]{:S(2)}, u32[]{:S(2)}) async-start(bf16[16,256,128]{2,1,0:T(8,128)(2,1)} %bitcast.29), calls=%async_computation | async-start | bytes 2097152 | tf_op jit(solution)/shard_map/all_to_all | solution.py:27
  8.4 0.0 copy-done.1
  8.4 0.0 copy-done.2
  8.4 0.0 copy-done.3
  8.4 0.0 copy-done.4
  8.4 0.1 multiply_bitcast_fusion
  8.5 0.0 copy-done
  8.5 6.1 %collective-permute-start = (f32[1,3,16,128]{3,2,1,0:T(8,128)S(1)}, f32[1,3,16,128]{3,2,1,0:T(8,128)S(1)}, u32[]{:S(2)}, u32[]{:S(2)}) collective-permute-start(f32[1,3,16,128]{3,2,1,0:T(8,128)S(1)} %get-tuple-element.57), channel_id=1, source_target_pairs={{0,12},{2,14},{4,8},{6,10},{8,4},{10,6},{12,0},{14,2},{1,13},{3,15... | collective-permute-start | bytes 73736 | tf_op jit(solution)/shard_map/ppermute | solution.py:39
  14.7 1.5 %collective-permute-done = f32[1,3,16,128]{3,2,1,0:T(8,128)S(1)} collective-permute-done((f32[1,3,16,128]{3,2,1,0:T(8,128)S(1)}, f32[1,3,16,128]{3,2,1,0:T(8,128)S(1)}, u32[]{:S(2)}, u32[]{:S(2)}) %collective-permute-start) | collective-permute-done | bytes 24608 | tf_op jit(solution)/shard_map/ppermute | solution.py:39
  16.2 0.1 broadcast_select_fusion
  16.2 0.9 %collective-permute-start.1 = (f32[2,3,16,128]{3,2,1,0:T(8,128)S(1)}, f32[2,3,16,128]{3,2,1,0:T(8,128)S(1)}, u32[]{:S(2)}, u32[]{:S(2)}) collective-permute-start(f32[2,3,16,128]{3,2,1,0:T(8,128)S(1)} %broadcast_select_fusion), channel_id=1, source_target_pairs={{0,4},{2,6},{4,0},{6,2},{8,12},{10,14},{12,8},{14,10},{1,5},{3,7},... | collective-permute-start | bytes 147464 | tf_op jit(solution)/shard_map/ppermute | solution.py:39
  17.1 0.1 iota_compare_fusion.1
  17.2 0.1 eq.77
  17.3 3.1 %collective-permute-done.1 = f32[2,3,16,128]{3,2,1,0:T(8,128)S(1)} collective-permute-done((f32[2,3,16,128]{3,2,1,0:T(8,128)S(1)}, f32[2,3,16,128]{3,2,1,0:T(8,128)S(1)}, u32[]{:S(2)}, u32[]{:S(2)}) %collective-permute-start.1) | collective-permute-done | bytes 49184 | tf_op jit(solution)/shard_map/ppermute | solution.py:39
  20.4 0.1 bitcast_select_fusion.1
  20.5 4.0 %all-to-all-done = bf16[16,256,128]{2,1,0:T(8,128)(2,1)S(1)} async-done(((bf16[16,256,128]{2,1,0:T(8,128)(2,1)}), bf16[16,256,128]{2,1,0:T(8,128)(2,1)S(1)}, u32[]{:S(2)}, u32[]{:S(2)}) %all-to-all-start) | async-done | bytes 1048608 | tf_op jit(solution)/shard_map/all_to_all | solution.py:27
  24.4 0.1 convert_reduce_fusion
  24.6 2.7 %collective-permute-start.2 = (f32[8,16,128]{2,1,0:T(8,128)S(1)}, f32[8,16,128]{2,1,0:T(8,128)S(1)}, u32[]{:S(2)}, u32[]{:S(2)}) collective-permute-start(f32[8,16,128]{2,1,0:T(8,128)S(1)} %dynamic-slice_bitcast_fusion), channel_id=1, source_target_pairs={{0,1},{1,0},{2,3},{3,2},{4,5},{5,4},{6,7},{7,6},{8,9},{9,8},{10,11... | collective-permute-start | bytes 196616 | tf_op jit(solution)/shard_map/ppermute | solution.py:35
  27.3 0.1 broadcast_in_dim.151
  27.4 0.1 broadcast_in_dim.152
  27.4 0.1 broadcast_in_dim.149
  27.5 0.1 broadcast_in_dim.150
  27.6 0.6 collective-permute-done.2
  28.2 1.7 %collective-permute-start.3 = (f32[128,128]{1,0:T(8,128)S(1)}, f32[128,128]{1,0:T(8,128)S(1)}, u32[]{:S(2)}, u32[]{:S(2)}) collective-permute-start(f32[128,128]{1,0:T(8,128)S(1)} %bitcast.33), channel_id=1, source_target_pairs={{0,2},{2,0},{4,6},{6,4},{8,10},{10,8},{12,14},{14,12},{1,3},{3,1},... | collective-permute-start | bytes 196616 | tf_op jit(solution)/shard_map/ppermute | solution.py:39
  29.9 0.1 collective-permute-start.7
  30.0 1.9 %collective-permute-done.3 = f32[128,128]{1,0:T(8,128)S(1)} collective-permute-done((f32[128,128]{1,0:T(8,128)S(1)}, f32[128,128]{1,0:T(8,128)S(1)}, u32[]{:S(2)}, u32[]{:S(2)}) %collective-permute-start.3) | collective-permute-done | bytes 65568 | tf_op jit(solution)/shard_map/ppermute | solution.py:39
  32.0 6.5 %collective-permute-start.6 = (f32[128,128]{1,0:T(8,128)S(1)}, f32[128,128]{1,0:T(8,128)S(1)}, u32[]{:S(2)}, u32[]{:S(2)}) collective-permute-start(f32[128,128]{1,0:T(8,128)S(1)} %add.26), channel_id=1, source_target_pairs={{0,8},{2,10},{4,12},{6,14},{8,0},{10,2},{12,4},{14,6},{1,9},{3,11}... | collective-permute-start | bytes 196616 | tf_op jit(solution)/shard_map/ppermute | solution.py:39
  38.4 0.0 collective-permute-start.5
  38.4 1.2 %collective-permute-start.4 = (f32[128,128]{1,0:T(8,128)S(1)}, f32[128,128]{1,0:T(8,128)S(1)}, u32[]{:S(2)}, u32[]{:S(2)}) collective-permute-start(f32[128,128]{1,0:T(8,128)S(1)} %add.26), channel_id=1, source_target_pairs={{0,4},{2,6},{4,0},{6,2},{8,12},{10,14},{12,8},{14,10},{1,5},{3,7},... | collective-permute-start | bytes 196616 | tf_op jit(solution)/shard_map/ppermute | solution.py:39
  39.6 0.1 iota_compare_fusion
  39.7 0.1 eq.81
  39.8 0.0 collective-permute-done.7
  39.8 0.1 bitcast_select_fusion.states
  39.9 1.2 %collective-permute-done.6 = f32[128,128]{1,0:T(8,128)S(1)} collective-permute-done((f32[128,128]{1,0:T(8,128)S(1)}, f32[128,128]{1,0:T(8,128)S(1)}, u32[]{:S(2)}, u32[]{:S(2)}) %collective-permute-start.6) | collective-permute-done | bytes 65568 | tf_op jit(solution)/shard_map/ppermute | solution.py:39
  41.0 2.7 %collective-permute-done.5 = f32[128,128]{1,0:T(8,128)S(1)} collective-permute-done((f32[128,128]{1,0:T(8,128)S(1)}, f32[128,128]{1,0:T(8,128)S(1)}, u32[]{:S(2)}, u32[]{:S(2)}) %collective-permute-start.5) | collective-permute-done | bytes 65568 | tf_op jit(solution)/shard_map/ppermute | solution.py:39
  43.7 0.5 collective-permute-done.4
  44.3 12.9 %all_to_all.15.norms = f32[32,1,128]{2,1,0:T(1,128)S(1)} all-to-all(f32[32,1,128]{2,1,0:T(1,128)S(1)} %broadcast_in_dim.158), channel_id=1, replica_groups=mesh['y'=4,'x'=4,'z'=8,'c'=2] {'y','x','c'}, dimensions={0} | all-to-all | bytes 32768 | tf_op jit(solution)/shard_map/all_to_all | solution.py:27
  57.2 0.2 shard_map.109
  57.4 13.2 %all_to_all.16 = bf16[16,128,128]{2,1,0:T(8,128)(2,1)S(1)} all-to-all(bf16[16,128,128]{2,1,0:T(8,128)(2,1)S(1)} %get-tuple-element.40), channel_id=1, replica_groups=mesh['y'=4,'x'=4,'z'=8,'c'=2] {'y','x'}, dimensions={0} | all-to-all | bytes 1048576 | tf_op jit(solution)/shard_map/all_to_all | solution.py:27
  70.6 2.0 %collective-permute-start.8 = (bf16[16,8,16,128]{3,2,1,0:T(8,128)(2,1)S(1)}, bf16[16,8,16,128]{3,2,1,0:T(8,128)(2,1)S(1)}, u32[]{:S(2)}, u32[]{:S(2)}) collective-permute-start(bf16[16,8,16,128]{3,2,1,0:T(8,128)(2,1)S(1)} %bitcast.27), channel_id=1, source_target_pairs={{0,1},{1,0},{2,3},{3,2},{4,5},{5,4},{6,7},{7,6},{8,9},{9,8},{10,11... | collective-permute-start | bytes 1572872 | tf_op jit(solution)/shard_map/ppermute | solution.py:35
  72.7 0.9 %shard_map.110 = (bf16[16,8,2,16,128]{4,3,2,1,0:T(8,128)(2,1)}, f32[16,128]{1,0:T(8,128)}, bf16[16,128]{1,0:T(8,128)(2,1)}, f32[1,16]{1,0:T(1,128)}, bf16[16,128]{1,0:T(8,128)(2,1)}, /*index=5*/f32[1,16]{1,0:T(1,128)}) custom-call(bf16[16,8,16,128]{3,2,1,0:T(8,128)(2,1)S(1)} %bitcast.28, f32[8,128]{1,0:T(8,128)S(1)} %get-tuple-element.43.factor, ...), custom_call_target="tpu_custom_call" | custom-call | tf_op jit(solution)/shard_map/pallas_call | solution.py:163
  73.5 0.7 collective-permute-done.8.half
  74.2 0.8 %shard_map.111 = bf16[16,8,2,16,128]{4,3,2,1,0:T(8,128)(2,1)} custom-call(bf16[16,8,16,128]{3,2,1,0:T(8,128)(2,1)S(1)} %collective-permute-done.8.half, bf16[16,8,2,16,128]{4,3,2,1,0:T(8,128)(2,1)} %get-tuple-element.46._), custom_call_target="tpu_custom_call", output_to_operand_aliasing={{}: (1, {})} | custom-call | tf_op jit(solution)/shard_map/pallas_call | solution.py:171
  (10 shorter events, 0.1 us)
Async XLA Ops:
  0.6 7.8 %copy-start.1 = (bf16[16,128]{1,0:T(8,128)(2,1)S(1)}, bf16[16,128]{1,0:T(8,128)(2,1)}, u32[]{:S(2)}) copy-start(bf16[16,128]{1,0:T(8,128)(2,1)} %param.10) | copy-start | bytes 12292
  0.6 7.8 %copy-start.2 = (bf16[16,128]{1,0:T(8,128)(2,1)S(1)}, bf16[16,128]{1,0:T(8,128)(2,1)}, u32[]{:S(2)}) copy-start(bf16[16,128]{1,0:T(8,128)(2,1)} %param.8) | copy-start | bytes 12292
  0.7 7.8 %copy-start.3 = (f32[16]{0:T(128)S(1)}, f32[16]{0:T(128)}, u32[]{:S(2)}) copy-start(f32[16]{0:T(128)} %param.11) | copy-start | bytes 196
  0.7 7.8 %copy-start.4 = (f32[16]{0:T(128)S(1)}, f32[16]{0:T(128)}, u32[]{:S(2)}) copy-start(f32[16]{0:T(128)} %param.9) | copy-start | bytes 196
  0.7 7.9 %copy-start = (f32[16,128]{1,0:T(8,128)S(1)}, f32[16,128]{1,0:T(8,128)}, u32[]{:S(2)}) copy-start(f32[16,128]{1,0:T(8,128)} %param.7) | copy-start | bytes 24580
  0.7 23.8 %all-to-all-start = ((bf16[16,256,128]{2,1,0:T(8,128)(2,1)}), bf16[16,256,128]{2,1,0:T(8,128)(2,1)S(1)}, u32[]{:S(2)}, u32[]{:S(2)}) async-start(bf16[16,256,128]{2,1,0:T(8,128)(2,1)} %bitcast.29), calls=%async_computation | async-start | bytes 2097152 | tf_op jit(solution)/shard_map/all_to_all | solution.py:27
  8.5 7.6 %collective-permute-start = (f32[1,3,16,128]{3,2,1,0:T(8,128)S(1)}, f32[1,3,16,128]{3,2,1,0:T(8,128)S(1)}, u32[]{:S(2)}, u32[]{:S(2)}) collective-permute-start(f32[1,3,16,128]{3,2,1,0:T(8,128)S(1)} %get-tuple-element.57), channel_id=1, source_target_pairs={{0,12},{2,14},{4,8},{6,10},{8,4},{10,6},{12,0},{14,2},{1,13},{3,15... | collective-permute-start | bytes 73736 | tf_op jit(solution)/shard_map/ppermute | solution.py:39
  16.2 4.2 %collective-permute-start.1 = (f32[2,3,16,128]{3,2,1,0:T(8,128)S(1)}, f32[2,3,16,128]{3,2,1,0:T(8,128)S(1)}, u32[]{:S(2)}, u32[]{:S(2)}) collective-permute-start(f32[2,3,16,128]{3,2,1,0:T(8,128)S(1)} %broadcast_select_fusion), channel_id=1, source_target_pairs={{0,4},{2,6},{4,0},{6,2},{8,12},{10,14},{12,8},{14,10},{1,5},{3,7},... | collective-permute-start | bytes 147464 | tf_op jit(solution)/shard_map/ppermute | solution.py:39
  24.6 3.6 %collective-permute-start.2 = (f32[8,16,128]{2,1,0:T(8,128)S(1)}, f32[8,16,128]{2,1,0:T(8,128)S(1)}, u32[]{:S(2)}, u32[]{:S(2)}) collective-permute-start(f32[8,16,128]{2,1,0:T(8,128)S(1)} %dynamic-slice_bitcast_fusion), channel_id=1, source_target_pairs={{0,1},{1,0},{2,3},{3,2},{4,5},{5,4},{6,7},{7,6},{8,9},{9,8},{10,11... | collective-permute-start | bytes 196616 | tf_op jit(solution)/shard_map/ppermute | solution.py:35
  28.2 3.7 %collective-permute-start.3 = (f32[128,128]{1,0:T(8,128)S(1)}, f32[128,128]{1,0:T(8,128)S(1)}, u32[]{:S(2)}, u32[]{:S(2)}) collective-permute-start(f32[128,128]{1,0:T(8,128)S(1)} %bitcast.33), channel_id=1, source_target_pairs={{0,2},{2,0},{4,6},{6,4},{8,10},{10,8},{12,14},{14,12},{1,3},{3,1},... | collective-permute-start | bytes 196616 | tf_op jit(solution)/shard_map/ppermute | solution.py:39
  29.9 9.8 %collective-permute-start.7 = (f32[4,3,16,128]{3,2,1,0:T(8,128)S(1)}, f32[4,3,16,128]{3,2,1,0:T(8,128)S(1)}, u32[]{:S(2)}, u32[]{:S(2)}) collective-permute-start(f32[4,3,16,128]{3,2,1,0:T(8,128)S(1)} %bitcast_select_fusion.1), channel_id=1, source_target_pairs={{0,2},{2,0},{4,6},{6,4},{8,10},{10,8},{12,14},{14,12},{1,3},{3,1},... | collective-permute-start | bytes 294920 | tf_op jit(solution)/shard_map/ppermute | solution.py:39
  32.0 9.1 %collective-permute-start.6 = (f32[128,128]{1,0:T(8,128)S(1)}, f32[128,128]{1,0:T(8,128)S(1)}, u32[]{:S(2)}, u32[]{:S(2)}) collective-permute-start(f32[128,128]{1,0:T(8,128)S(1)} %add.26), channel_id=1, source_target_pairs={{0,8},{2,10},{4,12},{6,14},{8,0},{10,2},{12,4},{14,6},{1,9},{3,11}... | collective-permute-start | bytes 196616 | tf_op jit(solution)/shard_map/ppermute | solution.py:39
  38.4 5.3 %collective-permute-start.5 = (f32[128,128]{1,0:T(8,128)S(1)}, f32[128,128]{1,0:T(8,128)S(1)}, u32[]{:S(2)}, u32[]{:S(2)}) collective-permute-start(f32[128,128]{1,0:T(8,128)S(1)} %add.26), channel_id=1, source_target_pairs={{0,12},{2,14},{4,8},{6,10},{8,4},{10,6},{12,0},{14,2},{1,13},{3,15... | collective-permute-start | bytes 196616 | tf_op jit(solution)/shard_map/ppermute | solution.py:39
  38.4 5.8 %collective-permute-start.4 = (f32[128,128]{1,0:T(8,128)S(1)}, f32[128,128]{1,0:T(8,128)S(1)}, u32[]{:S(2)}, u32[]{:S(2)}) collective-permute-start(f32[128,128]{1,0:T(8,128)S(1)} %add.26), channel_id=1, source_target_pairs={{0,4},{2,6},{4,0},{6,2},{8,12},{10,14},{12,8},{14,10},{1,5},{3,7},... | collective-permute-start | bytes 196616 | tf_op jit(solution)/shard_map/ppermute | solution.py:39
  70.6 3.6 %collective-permute-start.8 = (bf16[16,8,16,128]{3,2,1,0:T(8,128)(2,1)S(1)}, bf16[16,8,16,128]{3,2,1,0:T(8,128)(2,1)S(1)}, u32[]{:S(2)}, u32[]{:S(2)}) collective-permute-start(bf16[16,8,16,128]{3,2,1,0:T(8,128)(2,1)S(1)} %bitcast.27), channel_id=1, source_target_pairs={{0,1},{1,0},{2,3},{3,2},{4,5},{5,4},{6,7},{7,6},{8,9},{9,8},{10,11... | collective-permute-start | bytes 1572872 | tf_op jit(solution)/shard_map/ppermute | solution.py:35

commit v9 on v8

--- a/solution.py
+++ b/solution.py
@@ -39,16 +39,23 @@
     return lax.ppermute(x, "z", [(z, z ^ flip) for z in range(lax.axis_size("z"))])
 
 
-FLIPS = ((1, 0), (2, 1), (6, 2))
+def placed(pieces, bits):
+    if len(pieces) == 1:
+        return pieces
+    half = len(pieces) // 2
+    low, high = placed(pieces[:half], bits[1:]), placed(pieces[half:], bits[1:])
+    lower = [jnp.where(bits[0] == 1, b, a) for a, b in zip(low, high)]
+    upper = [jnp.where(bits[0] == 1, a, b) for a, b in zip(low, high)]
+    return lower + upper
 
 
-def doubled(x, place, step):
-    flip, level = step
-    other = from_partner(x, flip)
-    mine = jnp.arange(2) == (place[:, None] >> level & 1)
-    place = jnp.where(mine, place[:, None], place[:, None] ^ flip).reshape(-1)
-    x = jnp.where(mine[:, :, None, None, None], x[:, None], other[:, None])
-    return x.reshape(-1, *x.shape[2:]), place
+def gathered(x):
+    z = lax.axis_index("z")
+    bits = [z >> level & 1 for level in (2, 1, 0)]
+    pieces = [x] + [from_partner(x, flip) for flip in (2, 4, 6)]
+    apart = jnp.stack(placed(pieces, bits[:2]))
+    pair = placed([apart, from_partner(apart, 1)], bits[2:])
+    return jnp.stack(pair, axis=1).reshape(-1, *x.shape)
 
 
 def advance(clipped, master, first, second):
@@ -124,20 +131,14 @@
     here = lax.axis_index("c")
 
     arrived = exchange(grads[0].reshape(planes, line * cores * rows, width), ("y", "x"))
-    states = jnp.stack([master, first, second])[None]
-    place = lax.axis_index("z")[None]
-    for step in FLIPS[:0:-1]:
-        states, place = doubled(states, place, step)
+    states = gathered(jnp.stack([master, first, second]))
     arrived, states = lax.optimization_barrier((arrived, states))
     both = arrived.astype(jnp.float32).sum(axis=0).reshape(line, cores, rows, width)
     kept, sent = (lax.dynamic_index_in_dim(both, i, 1, False) for i in (here, 1 - here))
     part = (kept + swapped(sent)).reshape(held, width)
 
-    total, states = lax.optimization_barrier((part, states))
-    whole, _ = doubled(states, place, FLIPS[0])
-    total = total + from_partner(total, 1)
+    total = part + from_partner(part, 1)
     others = [from_partner(total, flip) for flip in (2, 6, 4)]
-    others, states = lax.optimization_barrier((others, whole))
     total = (total + others[0]) + (others[1] + others[2])
     norms = sent_to_all(jnp.sum(total * total, axis=0, keepdims=True), ("y", "x", "c"))
     norms, total, states = lax.optimization_barrier((norms, total, states))

time: 75.3 us -> 78.4 us (1.041)
  blocking collectives: 26.1 us -> 29.7 us
    all_to_all x1, waiting for transfers between devices: 3.97 us -> 0.01 us  [exchange(): return lax.all_to_all(x, axes, split_axis=0, concat_axis=0, tiled=True)]
    ppermute x7 -> x8, waiting for transfers between devices: 10.9 us -> 14.6 us  [from_partner(): lax.ppermute(x, 'z', [(z, z ^ flip) for z in range(lax.axis_size('z'))])]
    all_to_all x2, blocking collectives: 26.1 us -> 29.7 us  [exchange(): return lax.all_to_all(x, axes, split_axis=0, concat_axis=0, tiled=True)]
    ppermute x7 -> x8, starting transfers between devices: 16.5 us -> 16.1 us  [from_partner(): lax.ppermute(x, 'z', [(z, z ^ flip) for z in range(lax.axis_size('z'))])]
  transfers between devices with their start and end apart: 10 -> 11, of which waited for: 9 -> 8; matrix products, arithmetic and copies ran while one was open for 1% -> 0% of each run, Pallas kernels for 1% -> 1%
where the time goes in v9:
time: 78.4 us; the launch traced here: 78.1 us
  blocking collectives  29.7 us (38%)
  starting transfers between devices  29.1 us (37%)
  waiting for transfers between devices  16.2 us (21%)
  Pallas kernels  1.89 us (2%)
  between operations  0.79 us (1%)
    all_to_all x2, blocking collectives, exchange(): return lax.all_to_all(x, axes, split_axis=0, concat_axis=0, tiled=True)  29.7 us
    ppermute x8, starting transfers between devices, from_partner(): lax.ppermute(x, 'z', [(z, z ^ flip) for z in range(lax.axis_size('z'))])  16.1 us
    ppermute x8, waiting for transfers between devices, from_partner(): lax.ppermute(x, 'z', [(z, z ^ flip) for z in range(lax.axis_size('z'))])  14.6 us
    all_to_all x1, starting transfers between devices, exchange(): return lax.all_to_all(x, axes, split_axis=0, concat_axis=0, tiled=True)  7.72 us
    ppermute x2, starting transfers between devices, swapped(): return lax.ppermute(x, 'c', [(0, 1), (1, 0)])  5.36 us
  transfers between devices with their start and end apart: 11, of which 8 were waited for; matrix products, arithmetic and copies ran while one was open for 0% of the time, Pallas kernels for 1%

profile of v9, /device:TPU:1, one launch (start us, length us, event | category | flops | bytes accessed | tf_op | source)
XLA Modules:
  0.0 78.1 jit_solution(11974228613585006114)
XLA Ops:
  0.6 0.0 copy-start.1
  0.6 0.0 copy-start.2
  0.7 0.0 copy-start.3
  0.7 0.0 copy-start.4
  0.7 0.0 copy-start
  0.7 7.7 %all-to-all-start = ((bf16[16,256,128]{2,1,0:T(8,128)(2,1)}), bf16[16,256,128]{2,1,0:T(8,128)(2,1)S(1)}, u32[]{:S(2)}, u32[]{:S(2)}) async-start(bf16[16,256,128]{2,1,0:T(8,128)(2,1)} %bitcast.34), calls=%async_computation | async-start | bytes 2097152 | tf_op jit(solution)/shard_map/all_to_all | solution.py:27
  8.4 0.0 copy-done.1
  8.4 0.0 copy-done.2
  8.4 0.0 copy-done.3
  8.4 0.0 copy-done.4
  8.4 0.1 multiply_bitcast_fusion
  8.5 0.0 copy-done
  8.5 3.1 %collective-permute-start.2 = (f32[3,16,128]{2,1,0:T(8,128)S(1)}, f32[3,16,128]{2,1,0:T(8,128)S(1)}, u32[]{:S(2)}, u32[]{:S(2)}) collective-permute-start(f32[3,16,128]{2,1,0:T(8,128)S(1)} %pad_maximum_fusion.2), channel_id=1, source_target_pairs={{0,4},{2,6},{4,0},{6,2},{8,12},{10,14},{12,8},{14,10},{1,5},{3,7},... | collective-permute-start | bytes 73736 | tf_op jit(solution)/shard_map/ppermute | solution.py:39
  11.6 5.1 %collective-permute-start.1 = (f32[3,16,128]{2,1,0:T(8,128)S(1)}, f32[3,16,128]{2,1,0:T(8,128)S(1)}, u32[]{:S(2)}, u32[]{:S(2)}) collective-permute-start(f32[3,16,128]{2,1,0:T(8,128)S(1)} %pad_maximum_fusion.2), channel_id=1, source_target_pairs={{0,8},{2,10},{4,12},{6,14},{8,0},{10,2},{12,4},{14,6},{1,9},{3,11}... | collective-permute-start | bytes 73736 | tf_op jit(solution)/shard_map/ppermute | solution.py:39
  16.7 0.0 collective-permute-start
  16.7 0.0 collective-permute-done.2
  16.7 1.5 %collective-permute-done.1 = f32[3,16,128]{2,1,0:T(8,128)S(1)} collective-permute-done((f32[3,16,128]{2,1,0:T(8,128)S(1)}, f32[3,16,128]{2,1,0:T(8,128)S(1)}, u32[]{:S(2)}, u32[]{:S(2)}) %collective-permute-start.1) | collective-permute-done | bytes 24608 | tf_op jit(solution)/shard_map/ppermute | solution.py:39
  18.2 3.6 %collective-permute-done = f32[3,16,128]{2,1,0:T(8,128)S(1)} collective-permute-done((f32[3,16,128]{2,1,0:T(8,128)S(1)}, f32[3,16,128]{2,1,0:T(8,128)S(1)}, u32[]{:S(2)}, u32[]{:S(2)}) %collective-permute-start) | collective-permute-done | bytes 24608 | tf_op jit(solution)/shard_map/ppermute | solution.py:39
  21.8 0.8 %collective-permute-start.3 = (f32[4,3,16,128]{3,2,1,0:T(8,128)S(1)}, f32[4,3,16,128]{3,2,1,0:T(8,128)S(1)}, u32[]{:S(2)}, u32[]{:S(2)}) collective-permute-start(f32[4,3,16,128]{3,2,1,0:T(8,128)S(1)} %pad_maximum_fusion.1), channel_id=1, source_target_pairs={{0,2},{2,0},{4,6},{6,4},{8,10},{10,8},{12,14},{14,12},{1,3},{3,1},... | collective-permute-start | bytes 294920 | tf_op jit(solution)/shard_map/ppermute | solution.py:39
  22.6 3.0 %collective-permute-done.3 = f32[4,3,16,128]{3,2,1,0:T(8,128)S(1)} collective-permute-done((f32[4,3,16,128]{3,2,1,0:T(8,128)S(1)}, f32[4,3,16,128]{3,2,1,0:T(8,128)S(1)}, u32[]{:S(2)}, u32[]{:S(2)}) %collective-permute-start.3) | collective-permute-done | bytes 98336 | tf_op jit(solution)/shard_map/ppermute | solution.py:39
  25.7 0.0 all-to-all-done
  25.7 0.1 convert_reduce_fusion
  25.9 3.3 %collective-permute-start.4 = (f32[8,16,128]{2,1,0:T(8,128)S(1)}, f32[8,16,128]{2,1,0:T(8,128)S(1)}, u32[]{:S(2)}, u32[]{:S(2)}) collective-permute-start(f32[8,16,128]{2,1,0:T(8,128)S(1)} %dynamic-slice_bitcast_fusion), channel_id=1, source_target_pairs={{0,1},{1,0},{2,3},{3,2},{4,5},{5,4},{6,7},{7,6},{8,9},{9,8},{10,11... | collective-permute-start | bytes 196616 | tf_op jit(solution)/shard_map/ppermute | solution.py:35
  29.2 0.9 %collective-permute-done.4 = f32[8,16,128]{2,1,0:T(8,128)S(1)} collective-permute-done((f32[8,16,128]{2,1,0:T(8,128)S(1)}, f32[8,16,128]{2,1,0:T(8,128)S(1)}, u32[]{:S(2)}, u32[]{:S(2)}) %collective-permute-start.4) | collective-permute-done | bytes 65568 | tf_op jit(solution)/shard_map/ppermute | solution.py:35
  30.1 0.8 %collective-permute-start.5 = (f32[128,128]{1,0:T(8,128)S(1)}, f32[128,128]{1,0:T(8,128)S(1)}, u32[]{:S(2)}, u32[]{:S(2)}) collective-permute-start(f32[128,128]{1,0:T(8,128)S(1)} %bitcast.38), channel_id=1, source_target_pairs={{0,2},{2,0},{4,6},{6,4},{8,10},{10,8},{12,14},{14,12},{1,3},{3,1},... | collective-permute-start | bytes 196616 | tf_op jit(solution)/shard_map/ppermute | solution.py:39
  31.0 2.4 %collective-permute-done.5 = f32[128,128]{1,0:T(8,128)S(1)} collective-permute-done((f32[128,128]{1,0:T(8,128)S(1)}, f32[128,128]{1,0:T(8,128)S(1)}, u32[]{:S(2)}, u32[]{:S(2)}) %collective-permute-start.5) | collective-permute-done | bytes 65568 | tf_op jit(solution)/shard_map/ppermute | solution.py:39
  33.4 5.1 %collective-permute-start.8 = (f32[128,128]{1,0:T(8,128)S(1)}, f32[128,128]{1,0:T(8,128)S(1)}, u32[]{:S(2)}, u32[]{:S(2)}) collective-permute-start(f32[128,128]{1,0:T(8,128)S(1)} %bitcast_add_fusion.1), channel_id=1, source_target_pairs={{0,8},{2,10},{4,12},{6,14},{8,0},{10,2},{12,4},{14,6},{1,9},{3,11}... | collective-permute-start | bytes 196616 | tf_op jit(solution)/shard_map/ppermute | solution.py:39
  38.4 0.0 collective-permute-start.7
  38.4 1.2 %collective-permute-start.6 = (f32[128,128]{1,0:T(8,128)S(1)}, f32[128,128]{1,0:T(8,128)S(1)}, u32[]{:S(2)}, u32[]{:S(2)}) collective-permute-start(f32[128,128]{1,0:T(8,128)S(1)} %bitcast_add_fusion.1), channel_id=1, source_target_pairs={{0,4},{2,6},{4,0},{6,2},{8,12},{10,14},{12,8},{14,10},{1,5},{3,7},... | collective-permute-start | bytes 196616 | tf_op jit(solution)/shard_map/ppermute | solution.py:39
  39.6 0.9 %collective-permute-done.8 = f32[128,128]{1,0:T(8,128)S(1)} collective-permute-done((f32[128,128]{1,0:T(8,128)S(1)}, f32[128,128]{1,0:T(8,128)S(1)}, u32[]{:S(2)}, u32[]{:S(2)}) %collective-permute-start.8) | collective-permute-done | bytes 65568 | tf_op jit(solution)/shard_map/ppermute | solution.py:39
  40.5 3.3 %collective-permute-done.7 = f32[128,128]{1,0:T(8,128)S(1)} collective-permute-done((f32[128,128]{1,0:T(8,128)S(1)}, f32[128,128]{1,0:T(8,128)S(1)}, u32[]{:S(2)}, u32[]{:S(2)}) %collective-permute-start.7) | collective-permute-done | bytes 65568 | tf_op jit(solution)/shard_map/ppermute | solution.py:39
  43.7 0.0 collective-permute-done.6
  43.8 16.5 %all_to_all.15.norms = f32[32,1,128]{2,1,0:T(1,128)S(1)} all-to-all(f32[32,1,128]{2,1,0:T(1,128)S(1)} %broadcast_in_dim.2), channel_id=1, replica_groups=mesh['y'=4,'x'=4,'z'=8,'c'=2] {'y','x','c'}, dimensions={0} | all-to-all | bytes 32768 | tf_op jit(solution)/shard_map/all_to_all | solution.py:27
  60.3 0.2 shard_map.109
  60.5 13.2 %all_to_all.16 = bf16[16,128,128]{2,1,0:T(8,128)(2,1)S(1)} all-to-all(bf16[16,128,128]{2,1,0:T(8,128)(2,1)S(1)} %get-tuple-element.28), channel_id=1, replica_groups=mesh['y'=4,'x'=4,'z'=8,'c'=2] {'y','x'}, dimensions={0} | all-to-all | bytes 1048576 | tf_op jit(solution)/shard_map/all_to_all | solution.py:27
  73.7 2.0 %collective-permute-start.9 = (bf16[16,8,16,128]{3,2,1,0:T(8,128)(2,1)S(1)}, bf16[16,8,16,128]{3,2,1,0:T(8,128)(2,1)S(1)}, u32[]{:S(2)}, u32[]{:S(2)}) collective-permute-start(bf16[16,8,16,128]{3,2,1,0:T(8,128)(2,1)S(1)} %bitcast.30), channel_id=1, source_target_pairs={{0,1},{1,0},{2,3},{3,2},{4,5},{5,4},{6,7},{7,6},{8,9},{9,8},{10,11... | collective-permute-start | bytes 1572872 | tf_op jit(solution)/shard_map/ppermute | solution.py:35
  75.8 0.9 %shard_map.110 = (bf16[16,8,2,16,128]{4,3,2,1,0:T(8,128)(2,1)}, f32[16,128]{1,0:T(8,128)}, bf16[16,128]{1,0:T(8,128)(2,1)}, f32[1,16]{1,0:T(1,128)}, bf16[16,128]{1,0:T(8,128)(2,1)}, /*index=5*/f32[1,16]{1,0:T(1,128)}) custom-call(bf16[16,8,16,128]{3,2,1,0:T(8,128)(2,1)S(1)} %bitcast.31, f32[8,128]{1,0:T(8,128)S(1)} %get-tuple-element.31.factor, ...), custom_call_target="tpu_custom_call" | custom-call | tf_op jit(solution)/shard_map/pallas_call | solution.py:164
  76.6 0.7 collective-permute-done.9.half
  77.3 0.8 %shard_map.111 = bf16[16,8,2,16,128]{4,3,2,1,0:T(8,128)(2,1)} custom-call(bf16[16,8,16,128]{3,2,1,0:T(8,128)(2,1)S(1)} %collective-permute-done.9.half, bf16[16,8,2,16,128]{4,3,2,1,0:T(8,128)(2,1)} %get-tuple-element.34._), custom_call_target="tpu_custom_call", output_to_operand_aliasing={{}: (1, {})} | custom-call | tf_op jit(solution)/shard_map/pallas_call | solution.py:172
  (11 shorter events, 0.2 us)
Async XLA Ops:
  0.6 7.8 %copy-start.1 = (bf16[16,128]{1,0:T(8,128)(2,1)S(1)}, bf16[16,128]{1,0:T(8,128)(2,1)}, u32[]{:S(2)}) copy-start(bf16[16,128]{1,0:T(8,128)(2,1)} %param.10) | copy-start | bytes 12292
  0.6 7.8 %copy-start.2 = (bf16[16,128]{1,0:T(8,128)(2,1)S(1)}, bf16[16,128]{1,0:T(8,128)(2,1)}, u32[]{:S(2)}) copy-start(bf16[16,128]{1,0:T(8,128)(2,1)} %param.8) | copy-start | bytes 12292
  0.7 7.8 %copy-start.3 = (f32[16]{0:T(128)S(1)}, f32[16]{0:T(128)}, u32[]{:S(2)}) copy-start(f32[16]{0:T(128)} %param.11) | copy-start | bytes 196
  0.7 7.8 %copy-start.4 = (f32[16]{0:T(128)S(1)}, f32[16]{0:T(128)}, u32[]{:S(2)}) copy-start(f32[16]{0:T(128)} %param.9) | copy-start | bytes 196
  0.7 7.9 %copy-start = (f32[16,128]{1,0:T(8,128)S(1)}, f32[16,128]{1,0:T(8,128)}, u32[]{:S(2)}) copy-start(f32[16,128]{1,0:T(8,128)} %param.7) | copy-start | bytes 24580
  0.7 25.1 %all-to-all-start = ((bf16[16,256,128]{2,1,0:T(8,128)(2,1)}), bf16[16,256,128]{2,1,0:T(8,128)(2,1)S(1)}, u32[]{:S(2)}, u32[]{:S(2)}) async-start(bf16[16,256,128]{2,1,0:T(8,128)(2,1)} %bitcast.34), calls=%async_computation | async-start | bytes 2097152 | tf_op jit(solution)/shard_map/all_to_all | solution.py:27
  8.5 8.2 %collective-permute-start.2 = (f32[3,16,128]{2,1,0:T(8,128)S(1)}, f32[3,16,128]{2,1,0:T(8,128)S(1)}, u32[]{:S(2)}, u32[]{:S(2)}) collective-permute-start(f32[3,16,128]{2,1,0:T(8,128)S(1)} %pad_maximum_fusion.2), channel_id=1, source_target_pairs={{0,4},{2,6},{4,0},{6,2},{8,12},{10,14},{12,8},{14,10},{1,5},{3,7},... | collective-permute-start | bytes 73736 | tf_op jit(solution)/shard_map/ppermute | solution.py:39
  11.6 6.6 %collective-permute-start.1 = (f32[3,16,128]{2,1,0:T(8,128)S(1)}, f32[3,16,128]{2,1,0:T(8,128)S(1)}, u32[]{:S(2)}, u32[]{:S(2)}) collective-permute-start(f32[3,16,128]{2,1,0:T(8,128)S(1)} %pad_maximum_fusion.2), channel_id=1, source_target_pairs={{0,8},{2,10},{4,12},{6,14},{8,0},{10,2},{12,4},{14,6},{1,9},{3,11}... | collective-permute-start | bytes 73736 | tf_op jit(solution)/shard_map/ppermute | solution.py:39
  16.7 5.1 %collective-permute-start = (f32[3,16,128]{2,1,0:T(8,128)S(1)}, f32[3,16,128]{2,1,0:T(8,128)S(1)}, u32[]{:S(2)}, u32[]{:S(2)}) collective-permute-start(f32[3,16,128]{2,1,0:T(8,128)S(1)} %pad_maximum_fusion.2), channel_id=1, source_target_pairs={{0,12},{2,14},{4,8},{6,10},{8,4},{10,6},{12,0},{14,2},{1,13},{3,15... | collective-permute-start | bytes 73736 | tf_op jit(solution)/shard_map/ppermute | solution.py:39
  21.8 3.8 %collective-permute-start.3 = (f32[4,3,16,128]{3,2,1,0:T(8,128)S(1)}, f32[4,3,16,128]{3,2,1,0:T(8,128)S(1)}, u32[]{:S(2)}, u32[]{:S(2)}) collective-permute-start(f32[4,3,16,128]{3,2,1,0:T(8,128)S(1)} %pad_maximum_fusion.1), channel_id=1, source_target_pairs={{0,2},{2,0},{4,6},{6,4},{8,10},{10,8},{12,14},{14,12},{1,3},{3,1},... | collective-permute-start | bytes 294920 | tf_op jit(solution)/shard_map/ppermute | solution.py:39
  25.9 4.2 %collective-permute-start.4 = (f32[8,16,128]{2,1,0:T(8,128)S(1)}, f32[8,16,128]{2,1,0:T(8,128)S(1)}, u32[]{:S(2)}, u32[]{:S(2)}) collective-permute-start(f32[8,16,128]{2,1,0:T(8,128)S(1)} %dynamic-slice_bitcast_fusion), channel_id=1, source_target_pairs={{0,1},{1,0},{2,3},{3,2},{4,5},{5,4},{6,7},{7,6},{8,9},{9,8},{10,11... | collective-permute-start | bytes 196616 | tf_op jit(solution)/shard_map/ppermute | solution.py:35
  30.1 3.2 %collective-permute-start.5 = (f32[128,128]{1,0:T(8,128)S(1)}, f32[128,128]{1,0:T(8,128)S(1)}, u32[]{:S(2)}, u32[]{:S(2)}) collective-permute-start(f32[128,128]{1,0:T(8,128)S(1)} %bitcast.38), channel_id=1, source_target_pairs={{0,2},{2,0},{4,6},{6,4},{8,10},{10,8},{12,14},{14,12},{1,3},{3,1},... | collective-permute-start | bytes 196616 | tf_op jit(solution)/shard_map/ppermute | solution.py:39
  33.4 7.1 %collective-permute-start.8 = (f32[128,128]{1,0:T(8,128)S(1)}, f32[128,128]{1,0:T(8,128)S(1)}, u32[]{:S(2)}, u32[]{:S(2)}) collective-permute-start(f32[128,128]{1,0:T(8,128)S(1)} %bitcast_add_fusion.1), channel_id=1, source_target_pairs={{0,8},{2,10},{4,12},{6,14},{8,0},{10,2},{12,4},{14,6},{1,9},{3,11}... | collective-permute-start | bytes 196616 | tf_op jit(solution)/shard_map/ppermute | solution.py:39
  38.4 5.3 %collective-permute-start.7 = (f32[128,128]{1,0:T(8,128)S(1)}, f32[128,128]{1,0:T(8,128)S(1)}, u32[]{:S(2)}, u32[]{:S(2)}) collective-permute-start(f32[128,128]{1,0:T(8,128)S(1)} %bitcast_add_fusion.1), channel_id=1, source_target_pairs={{0,12},{2,14},{4,8},{6,10},{8,4},{10,6},{12,0},{14,2},{1,13},{3,15... | collective-permute-start | bytes 196616 | tf_op jit(solution)/shard_map/ppermute | solution.py:39
  38.4 5.3 %collective-permute-start.6 = (f32[128,128]{1,0:T(8,128)S(1)}, f32[128,128]{1,0:T(8,128)S(1)}, u32[]{:S(2)}, u32[]{:S(2)}) collective-permute-start(f32[128,128]{1,0:T(8,128)S(1)} %bitcast_add_fusion.1), channel_id=1, source_target_pairs={{0,4},{2,6},{4,0},{6,2},{8,12},{10,14},{12,8},{14,10},{1,5},{3,7},... | collective-permute-start | bytes 196616 | tf_op jit(solution)/shard_map/ppermute | solution.py:39
  73.7 3.6 %collective-permute-start.9 = (bf16[16,8,16,128]{3,2,1,0:T(8,128)(2,1)S(1)}, bf16[16,8,16,128]{3,2,1,0:T(8,128)(2,1)S(1)}, u32[]{:S(2)}, u32[]{:S(2)}) collective-permute-start(bf16[16,8,16,128]{3,2,1,0:T(8,128)(2,1)S(1)} %bitcast.30), channel_id=1, source_target_pairs={{0,1},{1,0},{2,3},{3,2},{4,5},{5,4},{6,7},{7,6},{8,9},{9,8},{10,11... | collective-permute-start | bytes 1572872 | tf_op jit(solution)/shard_map/ppermute | solution.py:35

commit v10 on v8

--- a/solution.py
+++ b/solution.py
@@ -39,15 +39,12 @@
     return lax.ppermute(x, "z", [(z, z ^ flip) for z in range(lax.axis_size("z"))])
 
 
-FLIPS = ((1, 0), (2, 1), (6, 2))
-
-
 def doubled(x, place, step):
     flip, level = step
     other = from_partner(x, flip)
     mine = jnp.arange(2) == (place[:, None] >> level & 1)
     place = jnp.where(mine, place[:, None], place[:, None] ^ flip).reshape(-1)
-    x = jnp.where(mine[:, :, None, None, None], x[:, None], other[:, None])
+    x = jnp.where(mine.reshape(mine.shape + (1,) * (x.ndim - 1)), x[:, None], other[:, None])
     return x.reshape(-1, *x.shape[2:]), place
 
 
@@ -77,21 +74,19 @@
     planes = half.shape[0] // PARTS
     spans = [pl.ds(part * planes, planes) for part in range(PARTS)]
     return [
-        pltpu.make_async_copy(half.at[span], out.at[span, :, side], sent.at[part])
+        pltpu.make_async_copy(half.at[span], out.at[span, side], sent.at[part])
         for part, span in enumerate(spans)
     ]
 
 
-def lay_and_advance(half, factor, total, states, out, *refs):
+def lay_and_advance(half, factor, own, states, out, *refs):
     results, held, sent = refs[:5], refs[5:10], refs[10]
     copies = copies_of_half(half, out, 0, sent)
     for copy in copies:
         copy.start()
 
-    rows = states.shape[2]
-    z = lax.axis_index("z")
-    own = total[pl.ds(pl.multiple_of(z * rows, rows), rows)]
-    held[0][...], *new = advance(factor[:1] * own, states[z, 0], states[z, 1], states[z, 2])
+    rows = own.shape[0]
+    held[0][...], *new = advance(factor[:1] * own[...], states[0], states[1], states[2])
     square = (rows, rows)
     diagonal = lax.broadcasted_iota(jnp.int32, square, 0) == lax.broadcasted_iota(jnp.int32, square, 1)
     for moment, quotient, scale in zip(new, held[1::2], held[2::2]):
@@ -121,24 +116,26 @@
     first = first_q.astype(jnp.float32) * first_scale[:, None]
     second = second_q.astype(jnp.float32) * second_scale[:, None]
 
-    here = lax.axis_index("c")
+    z, core = lax.axis_index("z"), lax.axis_index("c")
+    near = z // (line // cores) == core
+    chunks = line // cores * cores
 
-    arrived = exchange(grads[0].reshape(planes, line * cores * rows, width), ("y", "x"))
-    states = jnp.stack([master, first, second])[None]
-    place = lax.axis_index("z")[None]
-    for step in FLIPS[:0:-1]:
-        states, place = doubled(states, place, step)
+    arrived = exchange(grads[0].reshape(planes * cores, held, width), ("y", "x", "c"))
+    kept = jnp.stack([master, first, second])
+    chip = jnp.where((jnp.arange(cores) == core)[:, None, None, None], kept, swapped(kept))
+    states = jnp.where(near, chip, from_partner(chip, 6))[None]
+    place = jnp.where(near, z, z ^ 6)[None]
+    states, place = doubled(states, place, (2, 1))
     arrived, states = lax.optimization_barrier((arrived, states))
-    both = arrived.astype(jnp.float32).sum(axis=0).reshape(line, cores, rows, width)
-    kept, sent = (lax.dynamic_index_in_dim(both, i, 1, False) for i in (here, 1 - here))
-    part = (kept + swapped(sent)).reshape(held, width)
+    part = arrived.astype(jnp.float32).sum(axis=0)
 
     total, states = lax.optimization_barrier((part, states))
-    whole, _ = doubled(states, place, FLIPS[0])
+    whole, _ = doubled(states, place, (1, 0))
     total = total + from_partner(total, 1)
     others = [from_partner(total, flip) for flip in (2, 6, 4)]
     others, states = lax.optimization_barrier((others, whole))
     total = (total + others[0]) + (others[1] + others[2])
+    states = states.reshape(chunks, 3, rows, width)
     norms = sent_to_all(jnp.sum(total * total, axis=0, keepdims=True), ("y", "x", "c"))
     norms, total, states = lax.optimization_barrier((norms, total, states))
     small = pltpu.CompilerParams(vmem_limit_bytes=4 << 20)
@@ -151,12 +148,14 @@
         compiler_params=small,
     )(norms, total, states)
 
-    weights, factor, total, states = lax.optimization_barrier(
-        (exchange(weights, ("y", "x")), factor, total, states)
+    weights, factor, total, kept, z = lax.optimization_barrier(
+        (exchange(weights, ("y", "x")), factor, total, kept, z)
     )
-    weights = weights.reshape(planes, line, rows, width)
     partner = swapped(weights)
-    whole = jax.ShapeDtypeStruct((planes, line, cores, rows, width), jnp.bfloat16)
+    pieces = total.reshape(line // cores, cores, rows, width)[z % (line // cores)]
+    mine, other = (lax.dynamic_index_in_dim(pieces, i, 0, False) for i in (core, 1 - core))
+    own_total = jnp.where(near, mine, swapped(other))
+    whole = jax.ShapeDtypeStruct((planes, cores, held, width), jnp.bfloat16)
     own, scale = (rows, width), (1, rows)
     results = [(own, jnp.float32)] + [(own, jnp.bfloat16), (scale, jnp.float32)] * 2
     vmem, anywhere = (pl.BlockSpec(memory_space=space) for space in (pltpu.VMEM, pl.ANY))
@@ -167,7 +166,7 @@
         out_specs=[anywhere] * 6,
         scratch_shapes=[pltpu.VMEM(*result) for result in results] + [pltpu.SemaphoreType.DMA((PARTS + 5,))],
         compiler_params=small,
-    )(weights, factor, total, states)
+    )(weights, factor, own_total, kept)
     weights = pl.pallas_call(
         lay_other,
         out_shape=whole,

time: 75.3 us -> 75.6 us (level)
  starting transfers between devices: 28.9 us -> 27.8 us
  blocking collectives: 26.1 us -> 27.1 us
    ppermute x2 -> x3, starting transfers between devices: 4.72 us -> 2.35 us  [swapped(): return lax.ppermute(x, 'c', [(0, 1), (1, 0)])]
    ppermute x2 -> x3, waiting for transfers between devices: 1.25 us -> 2.5 us  [swapped(): return lax.ppermute(x, 'c', [(0, 1), (1, 0)])]
    all_to_all x1, starting transfers between devices: 7.72 us -> 8.72 us  [exchange(): return lax.all_to_all(x, axes, split_axis=0, concat_axis=0, tiled=True)]
    all_to_all x2, blocking collectives: 26.1 us -> 27.1 us  [exchange(): return lax.all_to_all(x, axes, split_axis=0, concat_axis=0, tiled=True)]
  transfers between devices with their start and end apart: 10 -> 11, of which waited for: 9 -> 9; matrix products, arithmetic and copies ran while one was open for 1% -> 1% of each run, Pallas kernels for 1% -> 1%
where the time goes in v10:
time: 75.6 us; the launch traced here: 75.3 us
  starting transfers between devices  27.8 us (37%)
  blocking collectives  27.1 us (36%)
  waiting for transfers between devices  16.8 us (22%)
  Pallas kernels  1.91 us (3%)
  between operations  0.76 us (1%)
    all_to_all x2, blocking collectives, exchange(): return lax.all_to_all(x, axes, split_axis=0, concat_axis=0, tiled=True)  27.1 us
    ppermute x7, starting transfers between devices, from_partner(): lax.ppermute(x, 'z', [(z, z ^ flip) for z in range(lax.axis_size('z'))])  16.8 us
    ppermute x7, waiting for transfers between devices, from_partner(): lax.ppermute(x, 'z', [(z, z ^ flip) for z in range(lax.axis_size('z'))])  11 us
    all_to_all x1, starting transfers between devices, exchange(): return lax.all_to_all(x, axes, split_axis=0, concat_axis=0, tiled=True)  8.72 us
    all_to_all x1, waiting for transfers between devices, exchange(): return lax.all_to_all(x, axes, split_axis=0, concat_axis=0, tiled=True)  3.34 us
    ppermute x3, waiting for transfers between devices, swapped(): return lax.ppermute(x, 'c', [(0, 1), (1, 0)])  2.5 us
    ppermute x3, starting transfers between devices, swapped(): return lax.ppermute(x, 'c', [(0, 1), (1, 0)])  2.35 us
  transfers between devices with their start and end apart: 11, of which 9 were waited for; matrix products, arithmetic and copies ran while one was open for 1% of the time, Pallas kernels for 1%

profile of v10, /device:TPU:1, one launch (start us, length us, event | category | flops | bytes accessed | tf_op | source)
XLA Modules:
  0.0 75.3 jit_solution(11908085043787387264)
XLA Ops:
  0.6 0.0 copy-start.1
  0.6 0.0 copy-start.2
  0.7 0.0 copy-start.3
  0.7 0.0 copy-start.4
  0.7 0.0 copy-start
  0.7 8.7 %all-to-all-start = ((bf16[32,128,128]{2,1,0:T(8,128)(2,1)}), bf16[32,128,128]{2,1,0:T(8,128)(2,1)S(1)}, u32[]{:S(2)}, u32[]{:S(2)}) async-start(bf16[32,128,128]{2,1,0:T(8,128)(2,1)} %bitcast.25), calls=%async_computation | async-start | bytes 2097152 | tf_op jit(solution)/shard_map/all_to_all | solution.py:27
  9.4 0.0 copy-done.1
  9.4 0.0 copy-done.2
  9.4 0.0 copy-done.3
  9.4 0.0 copy-done.4
  9.5 0.1 multiply_bitcast_fusion
  9.5 0.0 copy-done
  9.5 0.3 collective-permute-start
  9.8 1.0 %collective-permute-done = f32[3,16,128]{2,1,0:T(8,128)S(1)} collective-permute-done((f32[3,16,128]{2,1,0:T(8,128)S(1)}, f32[3,16,128]{2,1,0:T(8,128)S(1)}, u32[]{:S(2)}, u32[]{:S(2)}) %collective-permute-start) | collective-permute-done | bytes 24608 | tf_op jit(solution)/shard_map/ppermute | solution.py:35
  10.8 0.1 broadcast_select_fusion.1
  10.9 6.0 %collective-permute-start.1 = (f32[2,3,16,128]{3,2,1,0:T(8,128)S(1)}, f32[2,3,16,128]{3,2,1,0:T(8,128)S(1)}, u32[]{:S(2)}, u32[]{:S(2)}) collective-permute-start(f32[2,3,16,128]{3,2,1,0:T(8,128)S(1)} %broadcast_select_fusion.1), channel_id=1, source_target_pairs={{0,12},{2,14},{4,8},{6,10},{8,4},{10,6},{12,0},{14,2},{1,13},{3,15... | collective-permute-start | bytes 147464 | tf_op jit(solution)/shard_map/ppermute | solution.py:39
  16.9 1.9 %collective-permute-done.1 = f32[2,3,16,128]{3,2,1,0:T(8,128)S(1)} collective-permute-done((f32[2,3,16,128]{3,2,1,0:T(8,128)S(1)}, f32[2,3,16,128]{3,2,1,0:T(8,128)S(1)}, u32[]{:S(2)}, u32[]{:S(2)}) %collective-permute-start.1) | collective-permute-done | bytes 49184 | tf_op jit(solution)/shard_map/ppermute | solution.py:39
  18.8 0.1 fusion
  18.9 1.2 %collective-permute-start.2 = (f32[1,2,3,16,128]{4,3,2,1,0:T(8,128)S(1)}, f32[1,2,3,16,128]{4,3,2,1,0:T(8,128)S(1)}, u32[]{:S(2)}, u32[]{:S(2)}) collective-permute-start(f32[1,2,3,16,128]{4,3,2,1,0:T(8,128)S(1)} %fusion), channel_id=1, source_target_pairs={{0,4},{2,6},{4,0},{6,2},{8,12},{10,14},{12,8},{14,10},{1,5},{3,7},... | collective-permute-start | bytes 147464 | tf_op jit(solution)/shard_map/ppermute | solution.py:39
  20.1 0.1 broadcast_select_fusion.2
  20.2 2.9 %collective-permute-done.2 = f32[1,2,3,16,128]{4,3,2,1,0:T(8,128)S(1)} collective-permute-done((f32[1,2,3,16,128]{4,3,2,1,0:T(8,128)S(1)}, f32[1,2,3,16,128]{4,3,2,1,0:T(8,128)S(1)}, u32[]{:S(2)}, u32[]{:S(2)}) %collective-permute-start.2) | collective-permute-done | bytes 49184 | tf_op jit(solution)/shard_map/ppermute | solution.py:39
  23.0 0.1 broadcast_select_fusion
  23.1 3.3 %all-to-all-done = bf16[32,128,128]{2,1,0:T(8,128)(2,1)S(1)} async-done(((bf16[32,128,128]{2,1,0:T(8,128)(2,1)}), bf16[32,128,128]{2,1,0:T(8,128)(2,1)S(1)}, u32[]{:S(2)}, u32[]{:S(2)}) %all-to-all-start) | async-done | bytes 1048608 | tf_op jit(solution)/shard_map/all_to_all | solution.py:27
  26.5 0.2 convert_reduce_fusion
  26.6 1.7 %collective-permute-start.3 = (f32[128,128]{1,0:T(8,128)S(1)}, f32[128,128]{1,0:T(8,128)S(1)}, u32[]{:S(2)}, u32[]{:S(2)}) collective-permute-start(f32[128,128]{1,0:T(8,128)S(1)} %convert_reduce_fusion), channel_id=1, source_target_pairs={{0,2},{2,0},{4,6},{6,4},{8,10},{10,8},{12,14},{14,12},{1,3},{3,1},... | collective-permute-start | bytes 196616 | tf_op jit(solution)/shard_map/ppermute | solution.py:39
  28.3 0.1 collective-permute-start.7
  28.4 1.9 %collective-permute-done.3 = f32[128,128]{1,0:T(8,128)S(1)} collective-permute-done((f32[128,128]{1,0:T(8,128)S(1)}, f32[128,128]{1,0:T(8,128)S(1)}, u32[]{:S(2)}, u32[]{:S(2)}) %collective-permute-start.3) | collective-permute-done | bytes 65568 | tf_op jit(solution)/shard_map/ppermute | solution.py:39
  30.3 6.5 %collective-permute-start.6 = (f32[128,128]{1,0:T(8,128)S(1)}, f32[128,128]{1,0:T(8,128)S(1)}, u32[]{:S(2)}, u32[]{:S(2)}) collective-permute-start(f32[128,128]{1,0:T(8,128)S(1)} %add.36), channel_id=1, source_target_pairs={{0,8},{2,10},{4,12},{6,14},{8,0},{10,2},{12,4},{14,6},{1,9},{3,11}... | collective-permute-start | bytes 196616 | tf_op jit(solution)/shard_map/ppermute | solution.py:39
  36.8 0.0 collective-permute-start.5
  36.8 1.2 %collective-permute-start.4 = (f32[128,128]{1,0:T(8,128)S(1)}, f32[128,128]{1,0:T(8,128)S(1)}, u32[]{:S(2)}, u32[]{:S(2)}) collective-permute-start(f32[128,128]{1,0:T(8,128)S(1)} %add.36), channel_id=1, source_target_pairs={{0,4},{2,6},{4,0},{6,2},{8,12},{10,14},{12,8},{14,10},{1,5},{3,7},... | collective-permute-start | bytes 196616 | tf_op jit(solution)/shard_map/ppermute | solution.py:39
  38.0 0.1 iota_compare_fusion
  38.1 0.1 eq.63
  38.2 0.0 collective-permute-done.7
  38.2 0.1 bitcast_select_fusion
  38.3 1.1 %collective-permute-done.6 = f32[128,128]{1,0:T(8,128)S(1)} collective-permute-done((f32[128,128]{1,0:T(8,128)S(1)}, f32[128,128]{1,0:T(8,128)S(1)}, u32[]{:S(2)}, u32[]{:S(2)}) %collective-permute-start.6) | collective-permute-done | bytes 65568 | tf_op jit(solution)/shard_map/ppermute | solution.py:39
  39.4 2.7 %collective-permute-done.5 = f32[128,128]{1,0:T(8,128)S(1)} collective-permute-done((f32[128,128]{1,0:T(8,128)S(1)}, f32[128,128]{1,0:T(8,128)S(1)}, u32[]{:S(2)}, u32[]{:S(2)}) %collective-permute-start.5) | collective-permute-done | bytes 65568 | tf_op jit(solution)/shard_map/ppermute | solution.py:39
  42.1 0.5 collective-permute-done.4
  42.7 13.9 %all_to_all.15.norms = f32[32,1,128]{2,1,0:T(1,128)S(1)} all-to-all(f32[32,1,128]{2,1,0:T(1,128)S(1)} %broadcast_in_dim.116), channel_id=1, replica_groups=mesh['y'=4,'x'=4,'z'=8,'c'=2] {'y','x','c'}, dimensions={0} | all-to-all | bytes 32768 | tf_op jit(solution)/shard_map/all_to_all | solution.py:27
  56.6 0.2 shard_map.109
  56.8 13.2 %all_to_all.16.half = bf16[16,128,128]{2,1,0:T(8,128)(2,1)S(1)} all-to-all(bf16[16,128,128]{2,1,0:T(8,128)(2,1)S(1)} %get-tuple-element.41), channel_id=1, replica_groups=mesh['y'=4,'x'=4,'z'=8,'c'=2] {'y','x'}, dimensions={0} | all-to-all | bytes 1048576 | tf_op jit(solution)/shard_map/all_to_all | solution.py:27
  70.0 2.0 %collective-permute-start.8 = (bf16[16,128,128]{2,1,0:T(8,128)(2,1)S(1)}, bf16[16,128,128]{2,1,0:T(8,128)(2,1)S(1)}, u32[]{:S(2)}, u32[]{:S(2)}) collective-permute-start(bf16[16,128,128]{2,1,0:T(8,128)(2,1)S(1)} %all_to_all.16.half), channel_id=1, source_target_pairs={{0,1},{1,0},{2,3},{3,2},{4,5},{5,4},{6,7},{7,6},{8,9},{9,8},{10,11... | collective-permute-start | bytes 1572872 | tf_op jit(solution)/shard_map/ppermute | solution.py:35
  72.0 0.0 collective-permute-start.9
  72.0 1.5 %collective-permute-done.9 = f32[16,128]{1,0:T(8,128)S(1)} collective-permute-done((f32[16,128]{1,0:T(8,128)S(1)}, f32[16,128]{1,0:T(8,128)S(1)}, u32[]{:S(2)}, u32[]{:S(2)}) %collective-permute-start.9) | collective-permute-done | bytes 8224 | tf_op jit(solution)/shard_map/ppermute | solution.py:35
  73.6 0.9 %shard_map.110 = (bf16[16,2,128,128]{3,2,1,0:T(8,128)(2,1)}, f32[16,128]{1,0:T(8,128)}, bf16[16,128]{1,0:T(8,128)(2,1)}, f32[1,16]{1,0:T(1,128)}, bf16[16,128]{1,0:T(8,128)(2,1)}, /*index=5*/f32[1,16]{1,0:T(1,128)}) custom-call(bf16[16,128,128]{2,1,0:T(8,128)(2,1)S(1)} %all_to_all.16.half, f32[8,128]{1,0:T(8,128)S(1)} %get-tuple-element.44.factor, ...), custom_call_target="tpu_custom_call" | custom-call | tf_op jit(solution)/shard_map/pallas_call | solution.py:162
  74.4 0.0 collective-permute-done.8.half
  74.5 0.8 %shard_map.111 = bf16[16,2,128,128]{3,2,1,0:T(8,128)(2,1)} custom-call(bf16[16,128,128]{2,1,0:T(8,128)(2,1)S(1)} %collective-permute-done.8.half, bf16[16,2,128,128]{3,2,1,0:T(8,128)(2,1)} %get-tuple-element.48._), custom_call_target="tpu_custom_call", output_to_operand_aliasing={{}: (1, {})} | custom-call | tf_op jit(solution)/shard_map/pallas_call | solution.py:170
  (9 shorter events, 0.1 us)
Async XLA Ops:
  0.6 8.8 %copy-start.1 = (bf16[16,128]{1,0:T(8,128)(2,1)S(1)}, bf16[16,128]{1,0:T(8,128)(2,1)}, u32[]{:S(2)}) copy-start(bf16[16,128]{1,0:T(8,128)(2,1)} %param.10) | copy-start | bytes 12292
  0.6 8.8 %copy-start.2 = (bf16[16,128]{1,0:T(8,128)(2,1)S(1)}, bf16[16,128]{1,0:T(8,128)(2,1)}, u32[]{:S(2)}) copy-start(bf16[16,128]{1,0:T(8,128)(2,1)} %param.8) | copy-start | bytes 12292
  0.7 8.8 %copy-start.3 = (f32[16]{0:T(128)S(1)}, f32[16]{0:T(128)}, u32[]{:S(2)}) copy-start(f32[16]{0:T(128)} %param.11) | copy-start | bytes 196
  0.7 8.8 %copy-start.4 = (f32[16]{0:T(128)S(1)}, f32[16]{0:T(128)}, u32[]{:S(2)}) copy-start(f32[16]{0:T(128)} %param.9) | copy-start | bytes 196
  0.7 8.9 %copy-start = (f32[16,128]{1,0:T(8,128)S(1)}, f32[16,128]{1,0:T(8,128)}, u32[]{:S(2)}) copy-start(f32[16,128]{1,0:T(8,128)} %param.7) | copy-start | bytes 24580
  0.7 25.8 %all-to-all-start = ((bf16[32,128,128]{2,1,0:T(8,128)(2,1)}), bf16[32,128,128]{2,1,0:T(8,128)(2,1)S(1)}, u32[]{:S(2)}, u32[]{:S(2)}) async-start(bf16[32,128,128]{2,1,0:T(8,128)(2,1)} %bitcast.25), calls=%async_computation | async-start | bytes 2097152 | tf_op jit(solution)/shard_map/all_to_all | solution.py:27
  9.5 1.3 %collective-permute-start = (f32[3,16,128]{2,1,0:T(8,128)S(1)}, f32[3,16,128]{2,1,0:T(8,128)S(1)}, u32[]{:S(2)}, u32[]{:S(2)}) collective-permute-start(f32[3,16,128]{2,1,0:T(8,128)S(1)} %pad_maximum_fusion.states), channel_id=1, source_target_pairs={{0,1},{1,0},{2,3},{3,2},{4,5},{5,4},{6,7},{7,6},{8,9},{9,8},{10,11... | collective-permute-start | bytes 73736 | tf_op jit(solution)/shard_map/ppermute | solution.py:35
  10.9 7.9 %collective-permute-start.1 = (f32[2,3,16,128]{3,2,1,0:T(8,128)S(1)}, f32[2,3,16,128]{3,2,1,0:T(8,128)S(1)}, u32[]{:S(2)}, u32[]{:S(2)}) collective-permute-start(f32[2,3,16,128]{3,2,1,0:T(8,128)S(1)} %broadcast_select_fusion.1), channel_id=1, source_target_pairs={{0,12},{2,14},{4,8},{6,10},{8,4},{10,6},{12,0},{14,2},{1,13},{3,15... | collective-permute-start | bytes 147464 | tf_op jit(solution)/shard_map/ppermute | solution.py:39
  18.9 4.2 %collective-permute-start.2 = (f32[1,2,3,16,128]{4,3,2,1,0:T(8,128)S(1)}, f32[1,2,3,16,128]{4,3,2,1,0:T(8,128)S(1)}, u32[]{:S(2)}, u32[]{:S(2)}) collective-permute-start(f32[1,2,3,16,128]{4,3,2,1,0:T(8,128)S(1)} %fusion), channel_id=1, source_target_pairs={{0,4},{2,6},{4,0},{6,2},{8,12},{10,14},{12,8},{14,10},{1,5},{3,7},... | collective-permute-start | bytes 147464 | tf_op jit(solution)/shard_map/ppermute | solution.py:39
  26.6 3.7 %collective-permute-start.3 = (f32[128,128]{1,0:T(8,128)S(1)}, f32[128,128]{1,0:T(8,128)S(1)}, u32[]{:S(2)}, u32[]{:S(2)}) collective-permute-start(f32[128,128]{1,0:T(8,128)S(1)} %convert_reduce_fusion), channel_id=1, source_target_pairs={{0,2},{2,0},{4,6},{6,4},{8,10},{10,8},{12,14},{14,12},{1,3},{3,1},... | collective-permute-start | bytes 196616 | tf_op jit(solution)/shard_map/ppermute | solution.py:39
  28.3 9.8 %collective-permute-start.7 = (f32[2,2,3,16,128]{4,3,2,1,0:T(8,128)S(1)}, f32[2,2,3,16,128]{4,3,2,1,0:T(8,128)S(1)}, u32[]{:S(2)}, u32[]{:S(2)}) collective-permute-start(f32[2,2,3,16,128]{4,3,2,1,0:T(8,128)S(1)} %broadcast_select_fusion), channel_id=1, source_target_pairs={{0,2},{2,0},{4,6},{6,4},{8,10},{10,8},{12,14},{14,12},{1,3},{3,1},... | collective-permute-start | bytes 294920 | tf_op jit(solution)/shard_map/ppermute | solution.py:39
  30.3 9.1 %collective-permute-start.6 = (f32[128,128]{1,0:T(8,128)S(1)}, f32[128,128]{1,0:T(8,128)S(1)}, u32[]{:S(2)}, u32[]{:S(2)}) collective-permute-start(f32[128,128]{1,0:T(8,128)S(1)} %add.36), channel_id=1, source_target_pairs={{0,8},{2,10},{4,12},{6,14},{8,0},{10,2},{12,4},{14,6},{1,9},{3,11}... | collective-permute-start | bytes 196616 | tf_op jit(solution)/shard_map/ppermute | solution.py:39
  36.8 5.3 %collective-permute-start.5 = (f32[128,128]{1,0:T(8,128)S(1)}, f32[128,128]{1,0:T(8,128)S(1)}, u32[]{:S(2)}, u32[]{:S(2)}) collective-permute-start(f32[128,128]{1,0:T(8,128)S(1)} %add.36), channel_id=1, source_target_pairs={{0,12},{2,14},{4,8},{6,10},{8,4},{10,6},{12,0},{14,2},{1,13},{3,15... | collective-permute-start | bytes 196616 | tf_op jit(solution)/shard_map/ppermute | solution.py:39
  36.8 5.8 %collective-permute-start.4 = (f32[128,128]{1,0:T(8,128)S(1)}, f32[128,128]{1,0:T(8,128)S(1)}, u32[]{:S(2)}, u32[]{:S(2)}) collective-permute-start(f32[128,128]{1,0:T(8,128)S(1)} %add.36), channel_id=1, source_target_pairs={{0,4},{2,6},{4,0},{6,2},{8,12},{10,14},{12,8},{14,10},{1,5},{3,7},... | collective-permute-start | bytes 196616 | tf_op jit(solution)/shard_map/ppermute | solution.py:39
  70.0 4.5 %collective-permute-start.8 = (bf16[16,128,128]{2,1,0:T(8,128)(2,1)S(1)}, bf16[16,128,128]{2,1,0:T(8,128)(2,1)S(1)}, u32[]{:S(2)}, u32[]{:S(2)}) collective-permute-start(bf16[16,128,128]{2,1,0:T(8,128)(2,1)S(1)} %all_to_all.16.half), channel_id=1, source_target_pairs={{0,1},{1,0},{2,3},{3,2},{4,5},{5,4},{6,7},{7,6},{8,9},{9,8},{10,11... | collective-permute-start | bytes 1572872 | tf_op jit(solution)/shard_map/ppermute | solution.py:35
  72.0 1.5 %collective-permute-start.9 = (f32[16,128]{1,0:T(8,128)S(1)}, f32[16,128]{1,0:T(8,128)S(1)}, u32[]{:S(2)}, u32[]{:S(2)}) collective-permute-start(f32[16,128]{1,0:T(8,128)S(1)} %dynamic-slice_bitcast_fusion), channel_id=1, source_target_pairs={{0,1},{1,0},{2,3},{3,2},{4,5},{5,4},{6,7},{7,6},{8,9},{9,8},{10,11... | collective-permute-start | bytes 24584 | tf_op jit(solution)/shard_map/ppermute | solution.py:35

commit v11 on v10

--- a/solution.py
+++ b/solution.py
@@ -79,9 +79,17 @@
     ]
 
 
-def lay_and_advance(half, factor, own, states, out, *refs):
+def lay(half, out, sent):
+    copies = copies_of_half(half, out, 0, sent)
+    for copy in copies:
+        copy.start()
+    for copy in copies:
+        copy.wait()
+
+
+def lay_and_advance(half, factor, own, states, _, out, *refs):
     results, held, sent = refs[:5], refs[5:10], refs[10]
-    copies = copies_of_half(half, out, 0, sent)
+    copies = copies_of_half(half, out, 1, sent)
     for copy in copies:
         copy.start()
 
@@ -96,14 +104,6 @@
     for i, (result, kept) in enumerate(zip(results, held)):
         copies.append(pltpu.make_async_copy(kept, result, sent.at[PARTS + i]))
         copies[-1].start()
-    for copy in copies:
-        copy.wait()
-
-
-def lay_other(half, _, out, sent):
-    copies = copies_of_half(half, out, 1, sent)
-    for copy in copies:
-        copy.start()
     for copy in copies:
         copy.wait()
 
@@ -159,23 +159,23 @@
     own, scale = (rows, width), (1, rows)
     results = [(own, jnp.float32)] + [(own, jnp.bfloat16), (scale, jnp.float32)] * 2
     vmem, anywhere = (pl.BlockSpec(memory_space=space) for space in (pltpu.VMEM, pl.ANY))
+    weights = pl.pallas_call(
+        lay,
+        out_shape=whole,
+        in_specs=[vmem],
+        out_specs=anywhere,
+        scratch_shapes=[pltpu.SemaphoreType.DMA((PARTS,))],
+        compiler_params=small,
+    )(weights)
     weights, *results = pl.pallas_call(
         lay_and_advance,
         out_shape=[whole] + [jax.ShapeDtypeStruct(*result) for result in results],
-        in_specs=[vmem] * 4,
+        in_specs=[vmem] * 4 + [anywhere],
         out_specs=[anywhere] * 6,
         scratch_shapes=[pltpu.VMEM(*result) for result in results] + [pltpu.SemaphoreType.DMA((PARTS + 5,))],
+        input_output_aliases={4: 0},
         compiler_params=small,
-    )(weights, factor, own_total, kept)
-    weights = pl.pallas_call(
-        lay_other,
-        out_shape=whole,
-        in_specs=[vmem, anywhere],
-        out_specs=anywhere,
-        scratch_shapes=[pltpu.SemaphoreType.DMA((PARTS,))],
-        input_output_aliases={1: 0},
-        compiler_params=small,
-    )(partner, weights)
+    )(partner, factor, own_total, kept, weights)
     master_new, first_q_new, first_scale_new, second_q_new, second_scale_new = results
     weights = weights.reshape(blocks, width)
     return (weights, master_new, first_q_new, first_scale_new[0], second_q_new, second_scale_new[0])

time: 75.6 us -> 74.7 us (0.988)
  waiting for transfers between devices: 16.8 us -> 16 us
    ppermute x3, waiting for transfers between devices: 2.5 us -> 1.67 us  [swapped(): return lax.ppermute(x, 'c', [(0, 1), (1, 0)])]
where the time goes in v11:
time: 74.7 us; the launch traced here: 74.4 us
  starting transfers between devices  27.8 us (37%)
  blocking collectives  27.1 us (36%)
  waiting for transfers between devices  16 us (21%)
  Pallas kernels  1.9 us (3%)
  between operations  0.76 us (1%)
  other arithmetic  0.75 us (1%)
    all_to_all x2, blocking collectives, exchange(): return lax.all_to_all(x, axes, split_axis=0, concat_axis=0, tiled=True)  27.1 us
    ppermute x7, starting transfers between devices, from_partner(): lax.ppermute(x, 'z', [(z, z ^ flip) for z in range(lax.axis_size('z'))])  16.8 us
    ppermute x7, waiting for transfers between devices, from_partner(): lax.ppermute(x, 'z', [(z, z ^ flip) for z in range(lax.axis_size('z'))])  11 us
    all_to_all x1, starting transfers between devices, exchange(): return lax.all_to_all(x, axes, split_axis=0, concat_axis=0, tiled=True)  8.72 us
    all_to_all x1, waiting for transfers between devices, exchange(): return lax.all_to_all(x, axes, split_axis=0, concat_axis=0, tiled=True)  3.34 us
    ppermute x3, starting transfers between devices, swapped(): return lax.ppermute(x, 'c', [(0, 1), (1, 0)])  2.35 us
    ppermute x3, waiting for transfers between devices, swapped(): return lax.ppermute(x, 'c', [(0, 1), (1, 0)])  1.67 us
  transfers between devices with their start and end apart: 11, of which 9 were waited for; matrix products, arithmetic and copies ran while one was open for 1% of the time, Pallas kernels for 1%

profile of v11, /device:TPU:1, one launch (start us, length us, event | category | flops | bytes accessed | tf_op | source)
XLA Modules:
  0.0 74.4 jit_solution(7448349535437085616)
XLA Ops:
  0.6 0.0 copy-start.1
  0.6 0.0 copy-start.2
  0.7 0.0 copy-start.3
  0.7 0.0 copy-start.4
  0.7 0.0 copy-start
  0.7 8.7 %all-to-all-start = ((bf16[32,128,128]{2,1,0:T(8,128)(2,1)}), bf16[32,128,128]{2,1,0:T(8,128)(2,1)S(1)}, u32[]{:S(2)}, u32[]{:S(2)}) async-start(bf16[32,128,128]{2,1,0:T(8,128)(2,1)} %bitcast.26), calls=%async_computation | async-start | bytes 2097152 | tf_op jit(solution)/shard_map/all_to_all | solution.py:27
  9.4 0.0 copy-done.1
  9.4 0.0 copy-done.2
  9.4 0.0 copy-done.3
  9.4 0.0 copy-done.4
  9.5 0.1 multiply_bitcast_fusion
  9.5 0.0 copy-done
  9.5 0.3 collective-permute-start
  9.8 1.0 %collective-permute-done = f32[3,16,128]{2,1,0:T(8,128)S(1)} collective-permute-done((f32[3,16,128]{2,1,0:T(8,128)S(1)}, f32[3,16,128]{2,1,0:T(8,128)S(1)}, u32[]{:S(2)}, u32[]{:S(2)}) %collective-permute-start) | collective-permute-done | bytes 24608 | tf_op jit(solution)/shard_map/ppermute | solution.py:35
  10.8 0.1 broadcast_select_fusion.1
  10.9 6.0 %collective-permute-start.1 = (f32[2,3,16,128]{3,2,1,0:T(8,128)S(1)}, f32[2,3,16,128]{3,2,1,0:T(8,128)S(1)}, u32[]{:S(2)}, u32[]{:S(2)}) collective-permute-start(f32[2,3,16,128]{3,2,1,0:T(8,128)S(1)} %broadcast_select_fusion.1), channel_id=1, source_target_pairs={{0,12},{2,14},{4,8},{6,10},{8,4},{10,6},{12,0},{14,2},{1,13},{3,15... | collective-permute-start | bytes 147464 | tf_op jit(solution)/shard_map/ppermute | solution.py:39
  16.9 1.9 %collective-permute-done.1 = f32[2,3,16,128]{3,2,1,0:T(8,128)S(1)} collective-permute-done((f32[2,3,16,128]{3,2,1,0:T(8,128)S(1)}, f32[2,3,16,128]{3,2,1,0:T(8,128)S(1)}, u32[]{:S(2)}, u32[]{:S(2)}) %collective-permute-start.1) | collective-permute-done | bytes 49184 | tf_op jit(solution)/shard_map/ppermute | solution.py:39
  18.8 0.1 fusion
  18.9 1.2 %collective-permute-start.2 = (f32[1,2,3,16,128]{4,3,2,1,0:T(8,128)S(1)}, f32[1,2,3,16,128]{4,3,2,1,0:T(8,128)S(1)}, u32[]{:S(2)}, u32[]{:S(2)}) collective-permute-start(f32[1,2,3,16,128]{4,3,2,1,0:T(8,128)S(1)} %fusion), channel_id=1, source_target_pairs={{0,4},{2,6},{4,0},{6,2},{8,12},{10,14},{12,8},{14,10},{1,5},{3,7},... | collective-permute-start | bytes 147464 | tf_op jit(solution)/shard_map/ppermute | solution.py:39
  20.1 0.1 broadcast_select_fusion.2
  20.2 2.9 %collective-permute-done.2 = f32[1,2,3,16,128]{4,3,2,1,0:T(8,128)S(1)} collective-permute-done((f32[1,2,3,16,128]{4,3,2,1,0:T(8,128)S(1)}, f32[1,2,3,16,128]{4,3,2,1,0:T(8,128)S(1)}, u32[]{:S(2)}, u32[]{:S(2)}) %collective-permute-start.2) | collective-permute-done | bytes 49184 | tf_op jit(solution)/shard_map/ppermute | solution.py:39
  23.0 0.1 broadcast_select_fusion
  23.1 3.3 %all-to-all-done = bf16[32,128,128]{2,1,0:T(8,128)(2,1)S(1)} async-done(((bf16[32,128,128]{2,1,0:T(8,128)(2,1)}), bf16[32,128,128]{2,1,0:T(8,128)(2,1)S(1)}, u32[]{:S(2)}, u32[]{:S(2)}) %all-to-all-start) | async-done | bytes 1048608 | tf_op jit(solution)/shard_map/all_to_all | solution.py:27
  26.5 0.2 convert_reduce_fusion
  26.6 1.7 %collective-permute-start.3 = (f32[128,128]{1,0:T(8,128)S(1)}, f32[128,128]{1,0:T(8,128)S(1)}, u32[]{:S(2)}, u32[]{:S(2)}) collective-permute-start(f32[128,128]{1,0:T(8,128)S(1)} %convert_reduce_fusion), channel_id=1, source_target_pairs={{0,2},{2,0},{4,6},{6,4},{8,10},{10,8},{12,14},{14,12},{1,3},{3,1},... | collective-permute-start | bytes 196616 | tf_op jit(solution)/shard_map/ppermute | solution.py:39
  28.3 0.1 collective-permute-start.7
  28.4 1.9 %collective-permute-done.3 = f32[128,128]{1,0:T(8,128)S(1)} collective-permute-done((f32[128,128]{1,0:T(8,128)S(1)}, f32[128,128]{1,0:T(8,128)S(1)}, u32[]{:S(2)}, u32[]{:S(2)}) %collective-permute-start.3) | collective-permute-done | bytes 65568 | tf_op jit(solution)/shard_map/ppermute | solution.py:39
  30.3 6.5 %collective-permute-start.6 = (f32[128,128]{1,0:T(8,128)S(1)}, f32[128,128]{1,0:T(8,128)S(1)}, u32[]{:S(2)}, u32[]{:S(2)}) collective-permute-start(f32[128,128]{1,0:T(8,128)S(1)} %add.36), channel_id=1, source_target_pairs={{0,8},{2,10},{4,12},{6,14},{8,0},{10,2},{12,4},{14,6},{1,9},{3,11}... | collective-permute-start | bytes 196616 | tf_op jit(solution)/shard_map/ppermute | solution.py:39
  36.8 0.0 collective-permute-start.5
  36.8 1.2 %collective-permute-start.4 = (f32[128,128]{1,0:T(8,128)S(1)}, f32[128,128]{1,0:T(8,128)S(1)}, u32[]{:S(2)}, u32[]{:S(2)}) collective-permute-start(f32[128,128]{1,0:T(8,128)S(1)} %add.36), channel_id=1, source_target_pairs={{0,4},{2,6},{4,0},{6,2},{8,12},{10,14},{12,8},{14,10},{1,5},{3,7},... | collective-permute-start | bytes 196616 | tf_op jit(solution)/shard_map/ppermute | solution.py:39
  38.0 0.1 iota_compare_fusion
  38.1 0.1 eq.63
  38.2 0.0 collective-permute-done.7
  38.2 0.1 bitcast_select_fusion
  38.3 1.1 %collective-permute-done.6 = f32[128,128]{1,0:T(8,128)S(1)} collective-permute-done((f32[128,128]{1,0:T(8,128)S(1)}, f32[128,128]{1,0:T(8,128)S(1)}, u32[]{:S(2)}, u32[]{:S(2)}) %collective-permute-start.6) | collective-permute-done | bytes 65568 | tf_op jit(solution)/shard_map/ppermute | solution.py:39
  39.4 2.7 %collective-permute-done.5 = f32[128,128]{1,0:T(8,128)S(1)} collective-permute-done((f32[128,128]{1,0:T(8,128)S(1)}, f32[128,128]{1,0:T(8,128)S(1)}, u32[]{:S(2)}, u32[]{:S(2)}) %collective-permute-start.5) | collective-permute-done | bytes 65568 | tf_op jit(solution)/shard_map/ppermute | solution.py:39
  42.1 0.5 collective-permute-done.4
  42.7 13.9 %all_to_all.15.norms = f32[32,1,128]{2,1,0:T(1,128)S(1)} all-to-all(f32[32,1,128]{2,1,0:T(1,128)S(1)} %broadcast_in_dim.116), channel_id=1, replica_groups=mesh['y'=4,'x'=4,'z'=8,'c'=2] {'y','x','c'}, dimensions={0} | all-to-all | bytes 32768 | tf_op jit(solution)/shard_map/all_to_all | solution.py:27
  56.6 0.2 shard_map.109
  56.8 13.2 %all_to_all.16.half = bf16[16,128,128]{2,1,0:T(8,128)(2,1)S(1)} all-to-all(bf16[16,128,128]{2,1,0:T(8,128)(2,1)S(1)} %get-tuple-element.41), channel_id=1, replica_groups=mesh['y'=4,'x'=4,'z'=8,'c'=2] {'y','x'}, dimensions={0} | all-to-all | bytes 1048576 | tf_op jit(solution)/shard_map/all_to_all | solution.py:27
  70.0 2.0 %collective-permute-start.8 = (bf16[16,128,128]{2,1,0:T(8,128)(2,1)S(1)}, bf16[16,128,128]{2,1,0:T(8,128)(2,1)S(1)}, u32[]{:S(2)}, u32[]{:S(2)}) collective-permute-start(bf16[16,128,128]{2,1,0:T(8,128)(2,1)S(1)} %all_to_all.16.half), channel_id=1, source_target_pairs={{0,1},{1,0},{2,3},{3,2},{4,5},{5,4},{6,7},{7,6},{8,9},{9,8},{10,11... | collective-permute-start | bytes 1572872 | tf_op jit(solution)/shard_map/ppermute | solution.py:35
  72.0 0.0 collective-permute-start.9
  72.0 0.8 %shard_map.110._ = bf16[16,2,128,128]{3,2,1,0:T(8,128)(2,1)} custom-call(bf16[16,128,128]{2,1,0:T(8,128)(2,1)S(1)} %all_to_all.16.half), custom_call_target="tpu_custom_call" | custom-call | tf_op jit(solution)/shard_map/pallas_call | solution.py:162
  72.8 0.7 collective-permute-done.9
  73.6 0.0 collective-permute-done.8.half
  73.6 0.9 %shard_map.111 = (bf16[16,2,128,128]{3,2,1,0:T(8,128)(2,1)}, f32[16,128]{1,0:T(8,128)}, bf16[16,128]{1,0:T(8,128)(2,1)}, f32[1,16]{1,0:T(1,128)}, bf16[16,128]{1,0:T(8,128)(2,1)}, /*index=5*/f32[1,16]{1,0:T(1,128)}) custom-call(bf16[16,128,128]{2,1,0:T(8,128)(2,1)S(1)} %collective-permute-done.8.half, ...), custom_call_target="tpu_custom_call", output_to_operand_aliasing={{0}: (4, {})} | custom-call | tf_op jit(solution)/shard_map/pallas_call | solution.py:170
  (9 shorter events, 0.1 us)
Async XLA Ops:
  0.6 8.8 %copy-start.1 = (bf16[16,128]{1,0:T(8,128)(2,1)S(1)}, bf16[16,128]{1,0:T(8,128)(2,1)}, u32[]{:S(2)}) copy-start(bf16[16,128]{1,0:T(8,128)(2,1)} %param.10) | copy-start | bytes 12292
  0.6 8.8 %copy-start.2 = (bf16[16,128]{1,0:T(8,128)(2,1)S(1)}, bf16[16,128]{1,0:T(8,128)(2,1)}, u32[]{:S(2)}) copy-start(bf16[16,128]{1,0:T(8,128)(2,1)} %param.8) | copy-start | bytes 12292
  0.7 8.8 %copy-start.3 = (f32[16]{0:T(128)S(1)}, f32[16]{0:T(128)}, u32[]{:S(2)}) copy-start(f32[16]{0:T(128)} %param.11) | copy-start | bytes 196
  0.7 8.8 %copy-start.4 = (f32[16]{0:T(128)S(1)}, f32[16]{0:T(128)}, u32[]{:S(2)}) copy-start(f32[16]{0:T(128)} %param.9) | copy-start | bytes 196
  0.7 8.9 %copy-start = (f32[16,128]{1,0:T(8,128)S(1)}, f32[16,128]{1,0:T(8,128)}, u32[]{:S(2)}) copy-start(f32[16,128]{1,0:T(8,128)} %param.7) | copy-start | bytes 24580
  0.7 25.8 %all-to-all-start = ((bf16[32,128,128]{2,1,0:T(8,128)(2,1)}), bf16[32,128,128]{2,1,0:T(8,128)(2,1)S(1)}, u32[]{:S(2)}, u32[]{:S(2)}) async-start(bf16[32,128,128]{2,1,0:T(8,128)(2,1)} %bitcast.26), calls=%async_computation | async-start | bytes 2097152 | tf_op jit(solution)/shard_map/all_to_all | solution.py:27
  9.5 1.3 %collective-permute-start = (f32[3,16,128]{2,1,0:T(8,128)S(1)}, f32[3,16,128]{2,1,0:T(8,128)S(1)}, u32[]{:S(2)}, u32[]{:S(2)}) collective-permute-start(f32[3,16,128]{2,1,0:T(8,128)S(1)} %pad_maximum_fusion.states), channel_id=1, source_target_pairs={{0,1},{1,0},{2,3},{3,2},{4,5},{5,4},{6,7},{7,6},{8,9},{9,8},{10,11... | collective-permute-start | bytes 73736 | tf_op jit(solution)/shard_map/ppermute | solution.py:35
  10.9 7.9 %collective-permute-start.1 = (f32[2,3,16,128]{3,2,1,0:T(8,128)S(1)}, f32[2,3,16,128]{3,2,1,0:T(8,128)S(1)}, u32[]{:S(2)}, u32[]{:S(2)}) collective-permute-start(f32[2,3,16,128]{3,2,1,0:T(8,128)S(1)} %broadcast_select_fusion.1), channel_id=1, source_target_pairs={{0,12},{2,14},{4,8},{6,10},{8,4},{10,6},{12,0},{14,2},{1,13},{3,15... | collective-permute-start | bytes 147464 | tf_op jit(solution)/shard_map/ppermute | solution.py:39
  18.9 4.2 %collective-permute-start.2 = (f32[1,2,3,16,128]{4,3,2,1,0:T(8,128)S(1)}, f32[1,2,3,16,128]{4,3,2,1,0:T(8,128)S(1)}, u32[]{:S(2)}, u32[]{:S(2)}) collective-permute-start(f32[1,2,3,16,128]{4,3,2,1,0:T(8,128)S(1)} %fusion), channel_id=1, source_target_pairs={{0,4},{2,6},{4,0},{6,2},{8,12},{10,14},{12,8},{14,10},{1,5},{3,7},... | collective-permute-start | bytes 147464 | tf_op jit(solution)/shard_map/ppermute | solution.py:39
  26.6 3.7 %collective-permute-start.3 = (f32[128,128]{1,0:T(8,128)S(1)}, f32[128,128]{1,0:T(8,128)S(1)}, u32[]{:S(2)}, u32[]{:S(2)}) collective-permute-start(f32[128,128]{1,0:T(8,128)S(1)} %convert_reduce_fusion), channel_id=1, source_target_pairs={{0,2},{2,0},{4,6},{6,4},{8,10},{10,8},{12,14},{14,12},{1,3},{3,1},... | collective-permute-start | bytes 196616 | tf_op jit(solution)/shard_map/ppermute | solution.py:39
  28.3 9.8 %collective-permute-start.7 = (f32[2,2,3,16,128]{4,3,2,1,0:T(8,128)S(1)}, f32[2,2,3,16,128]{4,3,2,1,0:T(8,128)S(1)}, u32[]{:S(2)}, u32[]{:S(2)}) collective-permute-start(f32[2,2,3,16,128]{4,3,2,1,0:T(8,128)S(1)} %broadcast_select_fusion), channel_id=1, source_target_pairs={{0,2},{2,0},{4,6},{6,4},{8,10},{10,8},{12,14},{14,12},{1,3},{3,1},... | collective-permute-start | bytes 294920 | tf_op jit(solution)/shard_map/ppermute | solution.py:39
  30.3 9.1 %collective-permute-start.6 = (f32[128,128]{1,0:T(8,128)S(1)}, f32[128,128]{1,0:T(8,128)S(1)}, u32[]{:S(2)}, u32[]{:S(2)}) collective-permute-start(f32[128,128]{1,0:T(8,128)S(1)} %add.36), channel_id=1, source_target_pairs={{0,8},{2,10},{4,12},{6,14},{8,0},{10,2},{12,4},{14,6},{1,9},{3,11}... | collective-permute-start | bytes 196616 | tf_op jit(solution)/shard_map/ppermute | solution.py:39
  36.8 5.3 %collective-permute-start.5 = (f32[128,128]{1,0:T(8,128)S(1)}, f32[128,128]{1,0:T(8,128)S(1)}, u32[]{:S(2)}, u32[]{:S(2)}) collective-permute-start(f32[128,128]{1,0:T(8,128)S(1)} %add.36), channel_id=1, source_target_pairs={{0,12},{2,14},{4,8},{6,10},{8,4},{10,6},{12,0},{14,2},{1,13},{3,15... | collective-permute-start | bytes 196616 | tf_op jit(solution)/shard_map/ppermute | solution.py:39
  36.8 5.8 %collective-permute-start.4 = (f32[128,128]{1,0:T(8,128)S(1)}, f32[128,128]{1,0:T(8,128)S(1)}, u32[]{:S(2)}, u32[]{:S(2)}) collective-permute-start(f32[128,128]{1,0:T(8,128)S(1)} %add.36), channel_id=1, source_target_pairs={{0,4},{2,6},{4,0},{6,2},{8,12},{10,14},{12,8},{14,10},{1,5},{3,7},... | collective-permute-start | bytes 196616 | tf_op jit(solution)/shard_map/ppermute | solution.py:39
  70.0 3.6 %collective-permute-start.8 = (bf16[16,128,128]{2,1,0:T(8,128)(2,1)S(1)}, bf16[16,128,128]{2,1,0:T(8,128)(2,1)S(1)}, u32[]{:S(2)}, u32[]{:S(2)}) collective-permute-start(bf16[16,128,128]{2,1,0:T(8,128)(2,1)S(1)} %all_to_all.16.half), channel_id=1, source_target_pairs={{0,1},{1,0},{2,3},{3,2},{4,5},{5,4},{6,7},{7,6},{8,9},{9,8},{10,11... | collective-permute-start | bytes 1572872 | tf_op jit(solution)/shard_map/ppermute | solution.py:35
  72.0 1.5 %collective-permute-start.9 = (f32[16,128]{1,0:T(8,128)S(1)}, f32[16,128]{1,0:T(8,128)S(1)}, u32[]{:S(2)}, u32[]{:S(2)}) collective-permute-start(f32[16,128]{1,0:T(8,128)S(1)} %dynamic-slice_bitcast_fusion), channel_id=1, source_target_pairs={{0,1},{1,0},{2,3},{3,2},{4,5},{5,4},{6,7},{7,6},{8,9},{9,8},{10,11... | collective-permute-start | bytes 24584 | tf_op jit(solution)/shard_map/ppermute | solution.py:35

commit v12 on v11

--- a/solution.py
+++ b/solution.py
@@ -27,6 +27,19 @@
     return lax.all_to_all(x, axes, split_axis=0, concat_axis=0, tiled=True)
 
 
+def odd(z):
+    return (z ^ z >> 1) & 1
+
+
+def exchange_halves(x):
+    y, x_, line, cores = (lax.axis_size(axis) for axis in DP)
+    groups = [
+        [(plane * line + z) * cores + (half ^ odd(z)) for plane in range(y * x_) for half in range(cores)]
+        for z in range(line)
+    ]
+    return lax.all_to_all(x, DP, split_axis=0, concat_axis=0, tiled=True, axis_index_groups=groups)
+
+
 def sent_to_all(x, axes):
     return exchange(jnp.broadcast_to(x, (lax.axis_size(axes), *x.shape)), axes)
 
@@ -36,7 +49,9 @@
 
 
 def from_partner(x, flip):
-    return lax.ppermute(x, "z", [(z, z ^ flip) for z in range(lax.axis_size("z"))])
+    line = lax.axis_size("z")
+    route = [(2 * z + c, 2 * (z ^ flip) + (c ^ odd(flip))) for z in range(line) for c in range(2)]
+    return lax.ppermute(x, ("z", "c"), route)
 
 
 def doubled(x, place, step):
@@ -57,8 +72,9 @@
 
 
 def clip_and_advance(limit, norms, total, states, weights, factors):
-    squares = jnp.sum(norms[...], axis=0)
-    factor = jnp.minimum(1.0, limit / (jnp.sqrt(jnp.sum(squares, axis=1, keepdims=True)) + 1e-06))
+    pairs = norms[...]
+    squares = jnp.sum(pairs[:, 0] + pairs[:, 1], keepdims=True)
+    factor = jnp.minimum(1.0, limit / (jnp.sqrt(squares) + 1e-06))
     factors[...] = jnp.broadcast_to(factor, factors.shape)
     line, _, rows, width = states.shape
     for z in range(line):
@@ -70,7 +86,7 @@
 
 
 def copies_of_half(half, out, other, sent):
-    side = lax.axis_index("c") ^ other
+    side = lax.axis_index("c") ^ odd(lax.axis_index("z")) ^ other
     planes = half.shape[0] // PARTS
     spans = [pl.ds(part * planes, planes) for part in range(PARTS)]
     return [
@@ -117,10 +133,10 @@
     second = second_q.astype(jnp.float32) * second_scale[:, None]
 
     z, core = lax.axis_index("z"), lax.axis_index("c")
-    near = z // (line // cores) == core
+    near = z // (line // cores) == core ^ odd(z)
     chunks = line // cores * cores
 
-    arrived = exchange(grads[0].reshape(planes * cores, held, width), ("y", "x", "c"))
+    arrived = exchange_halves(grads[0].reshape(planes * cores, held, width))
     kept = jnp.stack([master, first, second])
     chip = jnp.where((jnp.arange(cores) == core)[:, None, None, None], kept, swapped(kept))
     states = jnp.where(near, chip, from_partner(chip, 6))[None]
@@ -146,7 +162,7 @@
             jax.ShapeDtypeStruct((8, width), jnp.float32),
         ),
         compiler_params=small,
-    )(norms, total, states)
+    )(norms.reshape(planes, cores, width), total, states)
 
     weights, factor, total, kept, z = lax.optimization_barrier(
         (exchange(weights, ("y", "x")), factor, total, kept, z)

time: 74.7 us -> 75 us (level)
  blocking collectives: 27.1 us -> 24.4 us
  waiting for transfers between devices: 16 us -> 18.4 us
    ppermute x7, waiting for transfers between devices: 11 us -> 14.6 us  [from_partner(): return lax.ppermute(x, ('z', 'c'), route)]
    all_to_all x2, blocking collectives: 27.1 us -> 24.4 us  [exchange(): return lax.all_to_all(x, axes, split_axis=0, concat_axis=0, tiled=True)]
    all_to_all x1, waiting for transfers between devices: 3.34 us -> 2.1 us  [exchange_halves(): lax.all_to_all(x, DP, split_axis=0, concat_axis=0, tiled=True, axis_index...]
where the time goes in v12:
time: 75 us; the launch traced here: 74.7 us
  starting transfers between devices  28.4 us (38%)
  blocking collectives  24.4 us (33%)
  waiting for transfers between devices  18.4 us (25%)
  Pallas kernels  1.92 us (3%)
  between operations  0.76 us (1%)
  other arithmetic  0.75 us (1%)
    all_to_all x2, blocking collectives, exchange(): return lax.all_to_all(x, axes, split_axis=0, concat_axis=0, tiled=True)  24.4 us
    ppermute x7, starting transfers between devices, from_partner(): return lax.ppermute(x, ('z', 'c'), route)  17.3 us
    ppermute x7, waiting for transfers between devices, from_partner(): return lax.ppermute(x, ('z', 'c'), route)  14.6 us
    all_to_all x1, starting transfers between devices, exchange_halves(): lax.all_to_all(x, DP, split_axis=0, concat_axis=0, tiled=True, axis_index...  8.72 us
    ppermute x3, starting transfers between devices, swapped(): return lax.ppermute(x, 'c', [(0, 1), (1, 0)])  2.35 us
    all_to_all x1, waiting for transfers between devices, exchange_halves(): lax.all_to_all(x, DP, split_axis=0, concat_axis=0, tiled=True, axis_index...  2.1 us
    ppermute x3, waiting for transfers between devices, swapped(): return lax.ppermute(x, 'c', [(0, 1), (1, 0)])  1.67 us
  transfers between devices with their start and end apart: 11, of which 9 were waited for; matrix products, arithmetic and copies ran while one was open for 1% of the time, Pallas kernels for 1%

profile of v12, /device:TPU:1, one launch (start us, length us, event | category | flops | bytes accessed | tf_op | source)
XLA Modules:
  0.0 74.7 jit_solution(10142476954150955802)
XLA Ops:
  0.6 0.0 copy-start.1
  0.6 0.0 copy-start.2
  0.7 0.0 copy-start.3
  0.7 0.0 copy-start.4
  0.7 0.0 copy-start
  0.7 8.7 %all-to-all-start = ((bf16[32,128,128]{2,1,0:T(8,128)(2,1)}), bf16[32,128,128]{2,1,0:T(8,128)(2,1)S(1)}, u32[]{:S(2)}, u32[]{:S(2)}) async-start(bf16[32,128,128]{2,1,0:T(8,128)(2,1)} %bitcast.28), calls=%async_computation | async-start | bytes 2097152 | tf_op jit(solution)/shard_map/all_to_all | solution.py:40
  9.4 0.0 copy-done.1
  9.4 0.0 copy-done.2
  9.4 0.0 copy-done.3
  9.4 0.0 copy-done.4
  9.5 0.1 multiply_bitcast_fusion
  9.5 0.0 copy-done
  9.5 0.3 collective-permute-start
  9.8 1.0 %collective-permute-done = f32[3,16,128]{2,1,0:T(8,128)S(1)} collective-permute-done((f32[3,16,128]{2,1,0:T(8,128)S(1)}, f32[3,16,128]{2,1,0:T(8,128)S(1)}, u32[]{:S(2)}, u32[]{:S(2)}) %collective-permute-start) | collective-permute-done | bytes 24608 | tf_op jit(solution)/shard_map/ppermute | solution.py:48
  10.8 0.1 broadcast_select_fusion.1
  10.9 6.0 %collective-permute-start.1 = (f32[2,3,16,128]{3,2,1,0:T(8,128)S(1)}, f32[2,3,16,128]{3,2,1,0:T(8,128)S(1)}, u32[]{:S(2)}, u32[]{:S(2)}) collective-permute-start(f32[2,3,16,128]{3,2,1,0:T(8,128)S(1)} %broadcast_select_fusion.1), channel_id=1, source_target_pairs={{0,13},{1,12},{2,15},{3,14},{4,9},{5,8},{6,11},{7,10},{8,5},{9,4},... | collective-permute-start | bytes 147464 | tf_op jit(solution)/shard_map/ppermute | solution.py:54
  16.9 2.2 %collective-permute-done.1 = f32[2,3,16,128]{3,2,1,0:T(8,128)S(1)} collective-permute-done((f32[2,3,16,128]{3,2,1,0:T(8,128)S(1)}, f32[2,3,16,128]{3,2,1,0:T(8,128)S(1)}, u32[]{:S(2)}, u32[]{:S(2)}) %collective-permute-start.1) | collective-permute-done | bytes 49184 | tf_op jit(solution)/shard_map/ppermute | solution.py:54
  19.1 0.1 fusion
  19.2 1.2 %collective-permute-start.2 = (f32[1,2,3,16,128]{4,3,2,1,0:T(8,128)S(1)}, f32[1,2,3,16,128]{4,3,2,1,0:T(8,128)S(1)}, u32[]{:S(2)}, u32[]{:S(2)}) collective-permute-start(f32[1,2,3,16,128]{4,3,2,1,0:T(8,128)S(1)} %fusion), channel_id=1, source_target_pairs={{0,5},{1,4},{2,7},{3,6},{4,1},{5,0},{6,3},{7,2},{8,13},{9,12},{10,... | collective-permute-start | bytes 147464 | tf_op jit(solution)/shard_map/ppermute | solution.py:54
  20.4 0.1 broadcast_select_fusion.2
  20.4 3.8 %collective-permute-done.2 = f32[1,2,3,16,128]{4,3,2,1,0:T(8,128)S(1)} collective-permute-done((f32[1,2,3,16,128]{4,3,2,1,0:T(8,128)S(1)}, f32[1,2,3,16,128]{4,3,2,1,0:T(8,128)S(1)}, u32[]{:S(2)}, u32[]{:S(2)}) %collective-permute-start.2) | collective-permute-done | bytes 49184 | tf_op jit(solution)/shard_map/ppermute | solution.py:54
  24.3 0.1 broadcast_select_fusion
  24.4 2.1 %all-to-all-done = bf16[32,128,128]{2,1,0:T(8,128)(2,1)S(1)} async-done(((bf16[32,128,128]{2,1,0:T(8,128)(2,1)}), bf16[32,128,128]{2,1,0:T(8,128)(2,1)S(1)}, u32[]{:S(2)}, u32[]{:S(2)}) %all-to-all-start) | async-done | bytes 1048608 | tf_op jit(solution)/shard_map/all_to_all | solution.py:40
  26.5 0.2 convert_reduce_fusion
  26.6 1.3 %collective-permute-start.3 = (f32[128,128]{1,0:T(8,128)S(1)}, f32[128,128]{1,0:T(8,128)S(1)}, u32[]{:S(2)}, u32[]{:S(2)}) collective-permute-start(f32[128,128]{1,0:T(8,128)S(1)} %convert_reduce_fusion), channel_id=1, source_target_pairs={{0,3},{1,2},{2,1},{3,0},{4,7},{5,6},{6,5},{7,4},{8,11},{9,10},{10,... | collective-permute-start | bytes 196616 | tf_op jit(solution)/shard_map/ppermute | solution.py:54
  27.9 0.6 collective-permute-start.7
  28.4 2.3 %collective-permute-done.3 = f32[128,128]{1,0:T(8,128)S(1)} collective-permute-done((f32[128,128]{1,0:T(8,128)S(1)}, f32[128,128]{1,0:T(8,128)S(1)}, u32[]{:S(2)}, u32[]{:S(2)}) %collective-permute-start.3) | collective-permute-done | bytes 65568 | tf_op jit(solution)/shard_map/ppermute | solution.py:54
  30.8 7.6 %collective-permute-start.6 = (f32[128,128]{1,0:T(8,128)S(1)}, f32[128,128]{1,0:T(8,128)S(1)}, u32[]{:S(2)}, u32[]{:S(2)}) collective-permute-start(f32[128,128]{1,0:T(8,128)S(1)} %add.36), channel_id=1, source_target_pairs={{0,8},{1,9},{2,10},{3,11},{4,12},{5,13},{6,14},{7,15},{8,0},{9,1},... | collective-permute-start | bytes 196616 | tf_op jit(solution)/shard_map/ppermute | solution.py:54
  38.4 0.0 collective-permute-start.5
  38.4 0.7 collective-permute-start.4
  39.1 0.1 iota_compare_fusion
  39.1 0.1 eq.63
  39.2 0.0 collective-permute-done.7
  39.2 0.1 bitcast_select_fusion
  39.3 1.7 %collective-permute-done.6 = f32[128,128]{1,0:T(8,128)S(1)} collective-permute-done((f32[128,128]{1,0:T(8,128)S(1)}, f32[128,128]{1,0:T(8,128)S(1)}, u32[]{:S(2)}, u32[]{:S(2)}) %collective-permute-start.6) | collective-permute-done | bytes 65568 | tf_op jit(solution)/shard_map/ppermute | solution.py:54
  41.0 3.4 %collective-permute-done.5 = f32[128,128]{1,0:T(8,128)S(1)} collective-permute-done((f32[128,128]{1,0:T(8,128)S(1)}, f32[128,128]{1,0:T(8,128)S(1)}, u32[]{:S(2)}, u32[]{:S(2)}) %collective-permute-start.5) | collective-permute-done | bytes 65568 | tf_op jit(solution)/shard_map/ppermute | solution.py:54
  44.4 1.1 %collective-permute-done.4 = f32[128,128]{1,0:T(8,128)S(1)} collective-permute-done((f32[128,128]{1,0:T(8,128)S(1)}, f32[128,128]{1,0:T(8,128)S(1)}, u32[]{:S(2)}, u32[]{:S(2)}) %collective-permute-start.4) | collective-permute-done | bytes 65568 | tf_op jit(solution)/shard_map/ppermute | solution.py:54
  45.6 11.2 %all_to_all.15 = f32[32,1,128]{2,1,0:T(1,128)S(1)} all-to-all(f32[32,1,128]{2,1,0:T(1,128)S(1)} %broadcast_in_dim.116), channel_id=1, replica_groups=mesh['y'=4,'x'=4,'z'=8,'c'=2] {'y','x','c'}, dimensions={0} | all-to-all | bytes 32768 | tf_op jit(solution)/shard_map/all_to_all | solution.py:27
  56.8 0.2 shard_map.109
  57.0 13.2 %all_to_all.16.half = bf16[16,128,128]{2,1,0:T(8,128)(2,1)S(1)} all-to-all(bf16[16,128,128]{2,1,0:T(8,128)(2,1)S(1)} %get-tuple-element.41), channel_id=1, replica_groups=mesh['y'=4,'x'=4,'z'=8,'c'=2] {'y','x'}, dimensions={0} | all-to-all | bytes 1048576 | tf_op jit(solution)/shard_map/all_to_all | solution.py:27
  70.2 2.0 %collective-permute-start.8 = (bf16[16,128,128]{2,1,0:T(8,128)(2,1)S(1)}, bf16[16,128,128]{2,1,0:T(8,128)(2,1)S(1)}, u32[]{:S(2)}, u32[]{:S(2)}) collective-permute-start(bf16[16,128,128]{2,1,0:T(8,128)(2,1)S(1)} %all_to_all.16.half), channel_id=1, source_target_pairs={{0,1},{1,0},{2,3},{3,2},{4,5},{5,4},{6,7},{7,6},{8,9},{9,8},{10,11... | collective-permute-start | bytes 1572872 | tf_op jit(solution)/shard_map/ppermute | solution.py:48
  72.2 0.0 collective-permute-start.9
  72.2 0.8 %shard_map.110._ = bf16[16,2,128,128]{3,2,1,0:T(8,128)(2,1)} custom-call(bf16[16,128,128]{2,1,0:T(8,128)(2,1)S(1)} %all_to_all.16.half), custom_call_target="tpu_custom_call" | custom-call | tf_op jit(solution)/shard_map/pallas_call | solution.py:178
  73.0 0.7 collective-permute-done.9
  73.8 0.0 collective-permute-done.8.half
  73.8 0.9 %shard_map.111 = (bf16[16,2,128,128]{3,2,1,0:T(8,128)(2,1)}, f32[16,128]{1,0:T(8,128)}, bf16[16,128]{1,0:T(8,128)(2,1)}, f32[1,16]{1,0:T(1,128)}, bf16[16,128]{1,0:T(8,128)(2,1)}, /*index=5*/f32[1,16]{1,0:T(1,128)}) custom-call(bf16[16,128,128]{2,1,0:T(8,128)(2,1)S(1)} %collective-permute-done.8.half, ...), custom_call_target="tpu_custom_call", output_to_operand_aliasing={{0}: (4, {})} | custom-call | tf_op jit(solution)/shard_map/pallas_call | solution.py:186
  (9 shorter events, 0.1 us)
Async XLA Ops:
  0.6 8.8 %copy-start.1 = (bf16[16,128]{1,0:T(8,128)(2,1)S(1)}, bf16[16,128]{1,0:T(8,128)(2,1)}, u32[]{:S(2)}) copy-start(bf16[16,128]{1,0:T(8,128)(2,1)} %param.10) | copy-start | bytes 12292
  0.6 8.8 %copy-start.2 = (bf16[16,128]{1,0:T(8,128)(2,1)S(1)}, bf16[16,128]{1,0:T(8,128)(2,1)}, u32[]{:S(2)}) copy-start(bf16[16,128]{1,0:T(8,128)(2,1)} %param.8) | copy-start | bytes 12292
  0.7 8.8 %copy-start.3 = (f32[16]{0:T(128)S(1)}, f32[16]{0:T(128)}, u32[]{:S(2)}) copy-start(f32[16]{0:T(128)} %param.11) | copy-start | bytes 196
  0.7 8.8 %copy-start.4 = (f32[16]{0:T(128)S(1)}, f32[16]{0:T(128)}, u32[]{:S(2)}) copy-start(f32[16]{0:T(128)} %param.9) | copy-start | bytes 196
  0.7 8.9 %copy-start = (f32[16,128]{1,0:T(8,128)S(1)}, f32[16,128]{1,0:T(8,128)}, u32[]{:S(2)}) copy-start(f32[16,128]{1,0:T(8,128)} %param.7) | copy-start | bytes 24580
  0.7 25.8 %all-to-all-start = ((bf16[32,128,128]{2,1,0:T(8,128)(2,1)}), bf16[32,128,128]{2,1,0:T(8,128)(2,1)S(1)}, u32[]{:S(2)}, u32[]{:S(2)}) async-start(bf16[32,128,128]{2,1,0:T(8,128)(2,1)} %bitcast.28), calls=%async_computation | async-start | bytes 2097152 | tf_op jit(solution)/shard_map/all_to_all | solution.py:40
  9.5 1.3 %collective-permute-start = (f32[3,16,128]{2,1,0:T(8,128)S(1)}, f32[3,16,128]{2,1,0:T(8,128)S(1)}, u32[]{:S(2)}, u32[]{:S(2)}) collective-permute-start(f32[3,16,128]{2,1,0:T(8,128)S(1)} %pad_maximum_fusion.states), channel_id=1, source_target_pairs={{0,1},{1,0},{2,3},{3,2},{4,5},{5,4},{6,7},{7,6},{8,9},{9,8},{10,11... | collective-permute-start | bytes 73736 | tf_op jit(solution)/shard_map/ppermute | solution.py:48
  10.9 8.2 %collective-permute-start.1 = (f32[2,3,16,128]{3,2,1,0:T(8,128)S(1)}, f32[2,3,16,128]{3,2,1,0:T(8,128)S(1)}, u32[]{:S(2)}, u32[]{:S(2)}) collective-permute-start(f32[2,3,16,128]{3,2,1,0:T(8,128)S(1)} %broadcast_select_fusion.1), channel_id=1, source_target_pairs={{0,13},{1,12},{2,15},{3,14},{4,9},{5,8},{6,11},{7,10},{8,5},{9,4},... | collective-permute-start | bytes 147464 | tf_op jit(solution)/shard_map/ppermute | solution.py:54
  19.2 5.1 %collective-permute-start.2 = (f32[1,2,3,16,128]{4,3,2,1,0:T(8,128)S(1)}, f32[1,2,3,16,128]{4,3,2,1,0:T(8,128)S(1)}, u32[]{:S(2)}, u32[]{:S(2)}) collective-permute-start(f32[1,2,3,16,128]{4,3,2,1,0:T(8,128)S(1)} %fusion), channel_id=1, source_target_pairs={{0,5},{1,4},{2,7},{3,6},{4,1},{5,0},{6,3},{7,2},{8,13},{9,12},{10,... | collective-permute-start | bytes 147464 | tf_op jit(solution)/shard_map/ppermute | solution.py:54
  26.6 4.2 %collective-permute-start.3 = (f32[128,128]{1,0:T(8,128)S(1)}, f32[128,128]{1,0:T(8,128)S(1)}, u32[]{:S(2)}, u32[]{:S(2)}) collective-permute-start(f32[128,128]{1,0:T(8,128)S(1)} %convert_reduce_fusion), channel_id=1, source_target_pairs={{0,3},{1,2},{2,1},{3,0},{4,7},{5,6},{6,5},{7,4},{8,11},{9,10},{10,... | collective-permute-start | bytes 196616 | tf_op jit(solution)/shard_map/ppermute | solution.py:54
  27.9 11.3 %collective-permute-start.7 = (f32[2,2,3,16,128]{4,3,2,1,0:T(8,128)S(1)}, f32[2,2,3,16,128]{4,3,2,1,0:T(8,128)S(1)}, u32[]{:S(2)}, u32[]{:S(2)}) collective-permute-start(f32[2,2,3,16,128]{4,3,2,1,0:T(8,128)S(1)} %broadcast_select_fusion), channel_id=1, source_target_pairs={{0,3},{1,2},{2,1},{3,0},{4,7},{5,6},{6,5},{7,4},{8,11},{9,10},{10,... | collective-permute-start | bytes 294920 | tf_op jit(solution)/shard_map/ppermute | solution.py:54
  30.8 10.2 %collective-permute-start.6 = (f32[128,128]{1,0:T(8,128)S(1)}, f32[128,128]{1,0:T(8,128)S(1)}, u32[]{:S(2)}, u32[]{:S(2)}) collective-permute-start(f32[128,128]{1,0:T(8,128)S(1)} %add.36), channel_id=1, source_target_pairs={{0,8},{1,9},{2,10},{3,11},{4,12},{5,13},{6,14},{7,15},{8,0},{9,1},... | collective-permute-start | bytes 196616 | tf_op jit(solution)/shard_map/ppermute | solution.py:54
  38.4 6.0 %collective-permute-start.5 = (f32[128,128]{1,0:T(8,128)S(1)}, f32[128,128]{1,0:T(8,128)S(1)}, u32[]{:S(2)}, u32[]{:S(2)}) collective-permute-start(f32[128,128]{1,0:T(8,128)S(1)} %add.36), channel_id=1, source_target_pairs={{0,13},{1,12},{2,15},{3,14},{4,9},{5,8},{6,11},{7,10},{8,5},{9,4},... | collective-permute-start | bytes 196616 | tf_op jit(solution)/shard_map/ppermute | solution.py:54
  38.4 7.1 %collective-permute-start.4 = (f32[128,128]{1,0:T(8,128)S(1)}, f32[128,128]{1,0:T(8,128)S(1)}, u32[]{:S(2)}, u32[]{:S(2)}) collective-permute-start(f32[128,128]{1,0:T(8,128)S(1)} %add.36), channel_id=1, source_target_pairs={{0,5},{1,4},{2,7},{3,6},{4,1},{5,0},{6,3},{7,2},{8,13},{9,12},{10,... | collective-permute-start | bytes 196616 | tf_op jit(solution)/shard_map/ppermute | solution.py:54
  70.2 3.6 %collective-permute-start.8 = (bf16[16,128,128]{2,1,0:T(8,128)(2,1)S(1)}, bf16[16,128,128]{2,1,0:T(8,128)(2,1)S(1)}, u32[]{:S(2)}, u32[]{:S(2)}) collective-permute-start(bf16[16,128,128]{2,1,0:T(8,128)(2,1)S(1)} %all_to_all.16.half), channel_id=1, source_target_pairs={{0,1},{1,0},{2,3},{3,2},{4,5},{5,4},{6,7},{7,6},{8,9},{9,8},{10,11... | collective-permute-start | bytes 1572872 | tf_op jit(solution)/shard_map/ppermute | solution.py:48
  72.2 1.5 %collective-permute-start.9 = (f32[16,128]{1,0:T(8,128)S(1)}, f32[16,128]{1,0:T(8,128)S(1)}, u32[]{:S(2)}, u32[]{:S(2)}) collective-permute-start(f32[16,128]{1,0:T(8,128)S(1)} %dynamic-slice_bitcast_fusion), channel_id=1, source_target_pairs={{0,1},{1,0},{2,3},{3,2},{4,5},{5,4},{6,7},{7,6},{8,9},{9,8},{10,11... | collective-permute-start | bytes 24584 | tf_op jit(solution)/shard_map/ppermute | solution.py:48
